TPU v7x, 32 devices: a whole 2x2x4 slice. The times are simulated.
32 devices in a mesh: section: 2 (over core), dp: 4 (over z), tensor: 4 (over y, x).
Axes of the slice: x: 2, y: 2, z: 4, core: 2. Of those that a mesh axis runs over, the one named last changes fastest.
Arguments:
- inputs: bfloat16 [2, 4, 1024, 768], P(None, 'dp', 'tensor'), may hold values from -6 to 6
- segment_ids: int32 [2, 4, 1024], P(None, 'dp'), may hold values from 0 to 7, never falling along the last dimension, each value on 1 to 384 neighbouring positions
- cotangent: float32 [2, 4, 1024, 768], P(None, 'dp', 'tensor'), may hold values from -6 to 6
- qkv_weight: bfloat16 [2, 3, 768, 768], P('section', None, 'dp', 'tensor'), may hold values from -0.21875 to 0.21875
- out_weight: bfloat16 [2, 768, 768], P('section', 'tensor', 'dp'), may hold values from -0.875 to 0.875
- up_weight: bfloat16 [2, 768, 3072], P('section', 'dp', 'tensor'), may hold values from -0.21875 to 0.21875
- down_weight: bfloat16 [2, 3072, 768], P('section', 'tensor', 'dp'), may hold values from -0.109375 to 0.109375
- norm_gain: float32 [2, 2, 768], P('section'), may hold values from 0.5 to 1.5
- norm_bias: float32 [2, 2, 768], P('section'), may hold values from -4 to 4
- qv_bias: float32 [2, 2, 768], P('section'), may hold values from -6 to 6
- up_bias: float32 [2, 3072], P('section'), may hold values from -6 to 6
- resid_bias: float32 [2, 768], P('section'), may hold values from -6 to 6
Outputs:
- outputs: float32 [2, 2, 4, 1024, 768], P('section', None, 'dp', 'tensor')
- input_grads: float32 [2, 2, 4, 1024, 768], P('section', None, 'dp', 'tensor')
- qkv_grad: float32 [2, 3, 768, 768], P('section', None, 'dp', 'tensor')
- out_grad: float32 [2, 768, 768], P('section', 'tensor', 'dp')
- up_grad: float32 [2, 768, 3072], P('section', 'dp', 'tensor')
- down_grad: float32 [2, 3072, 768], P('section', 'tensor', 'dp')
- gain_grad: float32 [2, 2, 768], P('section')
- norm_bias_grad: float32 [2, 2, 768], P('section')
- qv_bias_grad: float32 [2, 2, 768], P('section')
- up_bias_grad: float32 [2, 3072], P('section')
- resid_bias_grad: float32 [2, 768], P('section')
Inputs may be any that keep to these rules, and one draw needn't show every extreme that they name: `segment_ids`: along each sequence the ids never fall; every id 0 to 7 holds 1 to 384 tokens, one of them exactly 384.
All inputs are finite; a program needn't handle non-finite values.
Results may differ from a plain program's by a relative error of at most 0.012.
Values may be sent and summed in bfloat16 or wider, within the bound.
A program may use at most 256 MiB of HBM per device.

v0:
```python
import math

import jax
import jax.numpy as jnp
from jax import lax
from jax.sharding import PartitionSpec as P

HEAD_DIM = 64
ROT = 16


epsilon = 1e-05
root_half = 0.7071067811865476
inv_root_tau = 0.3989422804014327
masked_score = -1e30


def passed_along(block, axis, distance):
    devices = range(lax.axis_size(axis))
    route = [(i - distance, i) for i in devices if i - distance in devices]
    return lax.ppermute(block, axis, route)


def normalize(values, gain_row, shift_row):
    centre = jnp.mean(values, axis=-1, keepdims=True)
    centred = values - centre
    inverse = lax.rsqrt(jnp.mean(centred * centred, axis=-1, keepdims=True) + epsilon)
    unit_rows = centred * inverse
    return (unit_rows, inverse, unit_rows * gain_row + shift_row)


def normalize_back(incoming, unit_rows, inverse, gain_row):
    scaled = incoming * gain_row
    return inverse * (
        scaled
        - jnp.mean(scaled, axis=-1, keepdims=True)
        - unit_rows * jnp.mean(scaled * unit_rows, axis=-1, keepdims=True)
    )


def gelu_value(values):
    return values * 0.5 * (1.0 + lax.erf(values * root_half))


def gelu_slope(values):
    return 0.5 * (1.0 + lax.erf(values * root_half)) + values * inv_root_tau * jnp.exp(
        -0.5 * values * values
    )


def rotary_tables(length, rotated):
    positions = lax.broadcasted_iota(jnp.float32, (length, rotated // 2), 0)
    orders = lax.broadcasted_iota(jnp.float32, (length, rotated // 2), 1)
    angles = positions * jnp.exp(orders * (-2.0 * math.log(10000.0) / rotated))
    return (jnp.cos(angles), jnp.sin(angles))


def rotate(head_vals, cosine_table, sine_table, direction):
    half_rot = cosine_table.shape[-1]
    lower_part = head_vals[..., :half_rot]
    upper_part = head_vals[..., half_rot : 2 * half_rot]
    turned = direction * sine_table
    return jnp.concatenate(
        [
            lower_part * cosine_table - upper_part * turned,
            upper_part * cosine_table + lower_part * turned,
            head_vals[..., 2 * half_rot :],
        ],
        axis=-1,
    )


def score_block(query_part, key_b, segments, offset):
    row_count = query_part.shape[1]
    length = key_b.shape[1]
    scores = jnp.einsum("sqhd,skhd->shqk", query_part, key_b, preferred_element_type=jnp.float32)
    query_pos = lax.broadcasted_iota(jnp.int32, (row_count, length), 0) + offset
    key_pos = lax.broadcasted_iota(jnp.int32, (row_count, length), 1)
    same_doc = segments[:, offset : offset + row_count][:, :, None] == segments[:, None, :]
    allowed = same_doc & (key_pos <= query_pos)[None]
    return jnp.where(allowed[:, None], scores, masked_score)


def attend(query_b, key_b, value_b, segments):
    length = query_b.shape[1]
    block_rows = min(512, length)
    contexts = []
    log_totals = []
    for offset in range(0, length, block_rows):
        scores = score_block(query_b[:, offset : offset + block_rows], key_b, segments, offset)
        row_top = jnp.max(scores, axis=-1, keepdims=True)
        log_total = row_top + jnp.log(jnp.sum(jnp.exp(scores - row_top), axis=-1, keepdims=True))
        probs_b = jnp.exp(scores - log_total).astype(jnp.bfloat16)
        contexts.append(
            jnp.einsum(
                "shqk,skhd->sqhd", probs_b, value_b, preferred_element_type=jnp.float32
            ).astype(jnp.bfloat16)
        )
        log_totals.append(log_total)
    return (jnp.concatenate(contexts, axis=1), jnp.concatenate(log_totals, axis=2))


def attend_back(query_b, key_b, value_b, segments, log_totals, context_gradient):
    length = query_b.shape[1]
    block_rows = min(512, length)
    key_grad = jnp.zeros(key_b.shape, jnp.float32)
    value_grad = jnp.zeros(value_b.shape, jnp.float32)
    query_parts = []
    for offset in range(0, length, block_rows):
        query_part = query_b[:, offset : offset + block_rows]
        grad_part = context_gradient[:, offset : offset + block_rows]
        scores = score_block(query_part, key_b, segments, offset)
        probs = jnp.exp(scores - log_totals[:, :, offset : offset + block_rows])
        probs_b = probs.astype(jnp.bfloat16)
        value_grad = value_grad + jnp.einsum(
            "shqk,sqhd->skhd", probs_b, grad_part, preferred_element_type=jnp.float32
        )
        prob_grad = jnp.einsum(
            "sqhd,skhd->shqk", grad_part, value_b, preferred_element_type=jnp.float32
        )
        score_grad = probs * (prob_grad - jnp.sum(probs * prob_grad, axis=-1, keepdims=True))
        score_b = score_grad.astype(jnp.bfloat16)
        query_parts.append(
            jnp.einsum("shqk,skhd->sqhd", score_b, key_b, preferred_element_type=jnp.float32)
        )
        key_grad = key_grad + jnp.einsum(
            "shqk,sqhd->skhd", score_b, query_part, preferred_element_type=jnp.float32
        )
    return (jnp.concatenate(query_parts, axis=1), key_grad, value_grad)


def layer_pieces(x_part, segments, weight_matrices, params, cosine_table, sine_table):
    query_key_value_matrix, output_matrix, up_matrix, down_matrix = weight_matrices
    gain_pair, shift_pair, qv_local, up_weight_shard, resid_row = params
    gathered = lax.all_gather(x_part, "tensor", axis=1, tiled=True)
    widened = gathered.astype(jnp.float32)
    unit_one, inverse_one, normed_one = normalize(widened, gain_pair[0], shift_pair[0])
    unit_two, inverse_two, normed_two = normalize(widened, gain_pair[1], shift_pair[1])
    attention_input = normed_one.astype(jnp.bfloat16)
    feedforward_input = normed_two.astype(jnp.bfloat16)
    projected_rows = jnp.einsum(
        "bnp,kpq->kbnq", attention_input, query_key_value_matrix, preferred_element_type=jnp.float32
    )
    seq_count = attention_input.shape[0]
    length = attention_input.shape[1]
    heads_local = query_key_value_matrix.shape[2] // HEAD_DIM
    head_shape = (seq_count, length, heads_local, HEAD_DIM)
    cos_b = cosine_table[None, :, None, :]
    sin_b = sine_table[None, :, None, :]
    query_b = (
        rotate((projected_rows[0] + qv_local[0]).reshape(head_shape), cos_b, sin_b, 1.0) * 0.125
    ).astype(jnp.bfloat16)
    key_b = rotate(projected_rows[1].reshape(head_shape), cos_b, sin_b, 1.0).astype(jnp.bfloat16)
    value_b = (projected_rows[2] + qv_local[1]).reshape(head_shape).astype(jnp.bfloat16)
    context, log_totals = attend(query_b, key_b, value_b, segments)
    up_pre = (
        jnp.einsum("ogu,ui->ogi", feedforward_input, up_matrix, preferred_element_type=jnp.float32)
        + up_weight_shard
    )
    hidden_block = gelu_value(up_pre).astype(jnp.bfloat16)
    return (
        attention_input,
        feedforward_input,
        query_b,
        key_b,
        value_b,
        context,
        log_totals,
        up_pre,
        hidden_block,
        unit_one,
        inverse_one,
        unit_two,
        inverse_two,
    )


def layer_forward(x_part, segments, weight_matrices, params, cosine_table, sine_table):
    pieces = layer_pieces(x_part, segments, weight_matrices, params, cosine_table, sine_table)
    context = pieces[5]
    hidden_block = pieces[8]
    flattened_context = context.reshape(context.shape[0], context.shape[1], -1)
    branch = jnp.einsum(
        "xji,iy->xjy", flattened_context, weight_matrices[1], preferred_element_type=jnp.float32
    ) + jnp.einsum(
        "teo,ov->tev", hidden_block, weight_matrices[3], preferred_element_type=jnp.float32
    )
    summed = lax.psum_scatter(branch, "tensor", scatter_dimension=1, tiled=True)
    return x_part.astype(jnp.float32) + summed + params[4]


def layer_backward(x_part, segments, incoming, weight_matrices, params, cosine_table, sine_table):
    query_key_value_matrix, output_matrix, up_matrix, down_matrix = weight_matrices
    gain_pair, shift_pair, qv_local, up_weight_shard, resid_row = params
    (
        attention_input,
        feedforward_input,
        query_b,
        key_b,
        value_b,
        context,
        log_totals,
        up_pre,
        hidden_block,
        unit_one_all,
        inverse_one_all,
        unit_two_all,
        inverse_two_all,
    ) = layer_pieces(x_part, segments, weight_matrices, params, cosine_table, sine_table)
    seq_count = context.shape[0]
    length = context.shape[1]
    flattened_context = context.reshape(seq_count, length, -1)
    grad_b = incoming.astype(jnp.bfloat16)
    gradient_rows = lax.all_gather(grad_b, "tensor", axis=1, tiled=True)
    down_weight_gradient = jnp.einsum(
        "zca,zck->ak", hidden_block, gradient_rows, preferred_element_type=jnp.float32
    )
    output_weight_gradient = jnp.einsum(
        "afx,afp->xp", flattened_context, gradient_rows, preferred_element_type=jnp.float32
    )
    pre_grad = jnp.einsum(
        "qhi,ji->qhj", gradient_rows, down_matrix, preferred_element_type=jnp.float32
    ) * gelu_slope(up_pre)
    up_bias_g = jnp.sum(pre_grad, axis=(0, 1))
    preactivation_block = pre_grad.astype(jnp.bfloat16)
    up_weight_gradient = jnp.einsum(
        "oec,oep->cp", feedforward_input, preactivation_block, preferred_element_type=jnp.float32
    )
    feedforward_input_gradient = jnp.einsum(
        "gmi,ti->gmt", preactivation_block, up_matrix, preferred_element_type=jnp.float32
    )
    context_gradient = jnp.einsum(
        "cwm,am->cwa", gradient_rows, output_matrix, preferred_element_type=jnp.float32
    )
    context_gradient = context_gradient.astype(jnp.bfloat16).reshape(context.shape)
    query_grad, key_grad, value_grad = attend_back(
        query_b, key_b, value_b, segments, log_totals, context_gradient
    )
    cos_b = cosine_table[None, :, None, :]
    sin_b = sine_table[None, :, None, :]
    query_grad = rotate(query_grad, cos_b, sin_b, -1.0) * 0.125
    key_grad = rotate(key_grad, cos_b, sin_b, -1.0)
    flat_shape = (seq_count, length, flattened_context.shape[2])
    stacked = jnp.stack(
        [
            query_grad.reshape(flat_shape),
            key_grad.reshape(flat_shape),
            value_grad.reshape(flat_shape),
        ]
    )
    qv_g = jnp.stack([jnp.sum(stacked[0], axis=(0, 1)), jnp.sum(stacked[2], axis=(0, 1))])
    stacked_block = stacked.astype(jnp.bfloat16)
    query_key_value_gradient = jnp.einsum(
        "ivw,qivn->qwn", attention_input, stacked_block, preferred_element_type=jnp.float32
    )
    attn_in_grad = jnp.einsum(
        "hria,hoa->rio", stacked_block, query_key_value_matrix, preferred_element_type=jnp.float32
    )
    attn_part, mlp_part = (
        lax.psum_scatter(attn_in_grad, "tensor", scatter_dimension=1, tiled=True),
        lax.psum_scatter(feedforward_input_gradient, "tensor", scatter_dimension=1, tiled=True),
    )
    widened = x_part.astype(jnp.float32)
    unit_one, inverse_one, normed_skip = normalize(widened, gain_pair[0], shift_pair[0])
    unit_two, inverse_two, normed_drop = normalize(widened, gain_pair[1], shift_pair[1])
    gain_g = jnp.stack(
        [jnp.sum(attn_part * unit_one, axis=(0, 1)), jnp.sum(mlp_part * unit_two, axis=(0, 1))]
    )
    shift_g = jnp.stack([jnp.sum(attn_part, axis=(0, 1)), jnp.sum(mlp_part, axis=(0, 1))])
    input_grad = (
        incoming
        + normalize_back(attn_part, unit_one, inverse_one, gain_pair[0])
        + normalize_back(mlp_part, unit_two, inverse_two, gain_pair[1])
    )
    resid_g = jnp.sum(incoming, axis=(0, 1))
    return (
        input_grad,
        (
            query_key_value_gradient,
            output_weight_gradient,
            up_weight_gradient,
            down_weight_gradient,
        ),
        (gain_g, shift_g, qv_g, up_bias_g, resid_g),
    )


def body(
    inputs,
    segment_ids,
    cotangent,
    qkv_weight,
    out_weight,
    up_weight,
    down_weight,
    norm_gain,
    norm_bias,
    qv_bias,
    up_bias,
    resid_bias,
):
    leading = lax.axis_index("section") == 0
    column = lax.axis_index("tensor")
    micro_count = inputs.shape[0]
    head_cols = qkv_weight.shape[3]
    ff_local = up_weight.shape[2]
    qv_local = lax.dynamic_slice_in_dim(qv_bias[0], column * head_cols, head_cols, 1)
    up_weight_shard = lax.dynamic_slice_in_dim(up_bias[0], column * ff_local, ff_local, 0)
    params = (norm_gain[0], norm_bias[0], qv_local, up_weight_shard, resid_bias[0])
    shards = (qkv_weight[0], out_weight[0], up_weight[0], down_weight[0])
    cosine_table, sine_table = rotary_tables(segment_ids.shape[2], ROT)

    def fetch_weights():
        return (
            lax.all_gather(shards[0], "dp", axis=1, tiled=True),
            lax.all_gather(shards[1], "dp", axis=1, tiled=True),
            lax.all_gather(shards[2], "dp", axis=0, tiled=True),
            lax.all_gather(shards[3], "dp", axis=1, tiled=True),
        )

    arriving = jnp.zeros(inputs.shape[1:], jnp.bfloat16)
    seen_inputs = []
    made_outputs = []
    for moment in range(micro_count + 1):
        current = min(moment, micro_count - 1)
        earlier = max(moment - 1, 0)
        layer_in = jnp.where(leading, inputs[current], arriving)
        layer_seg = jnp.where(leading, segment_ids[current], segment_ids[earlier])
        weight_matrices = fetch_weights()
        layer_wide = layer_forward(
            layer_in, layer_seg, weight_matrices, params, cosine_table, sine_table
        )
        layer_out = layer_wide.astype(jnp.bfloat16)
        arriving = passed_along(layer_out, "section", 1)
        seen_inputs.append(layer_in)
        made_outputs.append(layer_wide)
    held_inputs = [
        jnp.where(leading, seen_inputs[slot_no], seen_inputs[slot_no + 1])
        for slot_no in range(micro_count)
    ]
    grads_held = tuple((jnp.zeros(piece.shape, jnp.float32) for piece in shards))
    small_held = (
        jnp.zeros(norm_gain.shape[1:], jnp.float32),
        jnp.zeros(norm_bias.shape[1:], jnp.float32),
        jnp.zeros((2, head_cols), jnp.float32),
        jnp.zeros((ff_local,), jnp.float32),
        jnp.zeros(resid_bias.shape[1:], jnp.float32),
    )
    returning = jnp.zeros(cotangent.shape[1:], jnp.float32)
    back_list = []
    for moment in range(micro_count + 1):
        current = min(moment, micro_count - 1)
        earlier = max(moment - 1, 0)
        active = jnp.where(leading, moment >= 1, moment < micro_count).astype(jnp.float32)
        incoming = jnp.where(leading, returning, cotangent[current]) * active
        layer_in = jnp.where(leading, held_inputs[earlier], held_inputs[current])
        layer_seg = jnp.where(leading, segment_ids[earlier], segment_ids[current])
        weight_matrices = fetch_weights()
        input_grad, matrix_grads, small_grads = layer_backward(
            layer_in, layer_seg, incoming, weight_matrices, params, cosine_table, sine_table
        )
        returning = passed_along(input_grad, "section", -1)
        back_list.append(input_grad)
        reduced = (
            lax.psum_scatter(matrix_grads[0], "dp", scatter_dimension=1, tiled=True),
            lax.psum_scatter(matrix_grads[1], "dp", scatter_dimension=1, tiled=True),
            lax.psum_scatter(matrix_grads[2], "dp", scatter_dimension=0, tiled=True),
            lax.psum_scatter(matrix_grads[3], "dp", scatter_dimension=1, tiled=True),
        )
        grads_held = tuple((held + piece for held, piece in zip(grads_held, reduced)))
        small_held = tuple((held + piece for held, piece in zip(small_held, small_grads)))
    qv_full = lax.dynamic_update_slice_in_dim(
        jnp.zeros((2, qv_bias.shape[2]), jnp.float32), small_held[2], column * head_cols, 1
    )
    up_full = lax.dynamic_update_slice_in_dim(
        jnp.zeros((up_bias.shape[1],), jnp.float32), small_held[3], column * ff_local, 0
    )
    totals = lax.psum(
        (small_held[0], small_held[1], qv_full, up_full, small_held[4]), ("dp", "tensor")
    )
    outputs = jnp.stack(
        [
            jnp.where(leading, made_outputs[slot_no], made_outputs[slot_no + 1])
            for slot_no in range(micro_count)
        ]
    )[None]
    input_grads = jnp.stack(
        [
            jnp.where(leading, back_list[slot_no + 1], back_list[slot_no])
            for slot_no in range(micro_count)
        ]
    )[None]
    return (
        outputs,
        input_grads,
        grads_held[0][None],
        grads_held[1][None],
        grads_held[2][None],
        grads_held[3][None],
        totals[0][None],
        totals[1][None],
        totals[2][None],
        totals[3][None],
        totals[4][None],
    )


def solution(mesh):
    return jax.shard_map(
        body,
        mesh=mesh,
        in_specs=(
            P(None, "dp", "tensor", None),
            P(None, "dp", None),
            P(None, "dp", "tensor", None),
            P("section", None, "dp", "tensor"),
            P("section", "tensor", "dp"),
            P("section", "dp", "tensor"),
            P("section", "tensor", "dp"),
            P("section", None, None),
            P("section", None, None),
            P("section", None, None),
            P("section", None),
            P("section", None),
        ),
        out_specs=(
            P("section", None, "dp", "tensor", None),
            P("section", None, "dp", "tensor", None),
            P("section", None, "dp", "tensor"),
            P("section", "tensor", "dp"),
            P("section", "dp", "tensor"),
            P("section", "tensor", "dp"),
            P("section", None, None),
            P("section", None, None),
            P("section", None, None),
            P("section", None),
            P("section", None),
        ),
        check_vma=False,
    )
```

profile of v0, /device:TPU:0, one launch (start us, length us, event | category | flops | bytes accessed | tf_op | source)
XLA Modules:
  0.0 1101.3 jit_solution(5559627993317711063)
XLA Ops:
  17.8 21.3 %all-gather.2 = bf16[1,192,768]{1,0,2:T(2,128)(2,1)S(1)} all-gather(bf16[1,192,192]{1,0,2:T(2,128)(2,1)S(1)} %copy.35), channel_id=4, replica_groups=mesh['section'=2,'dp'=4,'tensor'=4] {'dp'}, dimensions={2}, use_global_device_ids=true | all-gather | bytes 368640 | tf_op jit(solution)/shard_map/all_gather | solution.py:316
  39.6 40.7 %all-gather.1 = bf16[1,3,768,192]{3,1,0,2:T(4,128)(2,1)S(1)} all-gather(bf16[1,3,192,192]{3,1,0,2:T(4,128)(2,1)S(1)} %copy.33), channel_id=3, replica_groups=mesh['section'=2,'dp'=4,'tensor'=4] {'dp'}, dimensions={2}, use_global_device_ids=true | all-gather | bytes 1105920 | tf_op jit(solution)/shard_map/all_gather | solution.py:315
  100.5 17.1 %all-gather.37.cloned.1.call-done = bf16[1,768,768]{1,2,0:T(8,128)(2,1)} async-done(((bf16[1,768,192]{1,2,0:T(8,128)(2,1)}), bf16[1,768,768]{1,2,0:T(8,128)(2,1)}) %all-gather.37.cloned.1.call-update) | async-done | bytes 1179664 | tf_op jit(solution)/shard_map/all_gather | solution.py:318
  117.6 6.6 fusion.206
  124.2 4.2 add_bitcast_fusion.2
  129.1 42.5 %reduce-scatter.18.cloned.1.call-done = f32[1,256,768]{2,1,0:T(8,128)} async-done(((f32[1,1024,768]{2,1,0:T(8,128)}), f32[1,256,768]{2,1,0:T(8,128)}) %reduce-scatter.18.cloned.1.call-update) | async-done | bytes 786448 | tf_op jit(solution)/shard_map/reduce_scatter | solution.py:188
  178.4 29.6 %all-gather.17.cloned.1.call-done = bf16[1,1024,768]{2,1,0:T(8,128)(2,1)} async-done(((bf16[1,256,768]{2,1,0:T(8,128)(2,1)}), bf16[1,1024,768]{2,1,0:T(8,128)(2,1)}) %all-gather.17.cloned.1.call-update) | async-done | bytes 1572880 | tf_op jit(solution)/shard_map/all_gather | solution.py:135
  224.0 6.6 fusion.204
  230.6 4.2 add_bitcast_fusion.1
  237.5 41.4 %reduce-scatter.20.cloned.1.call-done = f32[1,256,768]{2,1,0:T(8,128)} async-done(((f32[1,1024,768]{2,1,0:T(8,128)}), f32[1,256,768]{2,1,0:T(8,128)}) %reduce-scatter.20.cloned.1.call-update) | async-done | bytes 786448 | tf_op jit(solution)/shard_map/reduce_scatter | solution.py:188
  286.4 2.8 convert_reduce_fusion.7
  289.3 23.0 %all-gather.23.cloned.1.call-done = bf16[1,1024,768]{2,1,0:T(8,128)(2,1)} async-done(((bf16[1,256,768]{2,1,0:T(8,128)(2,1)}), bf16[1,1024,768]{2,1,0:T(8,128)(2,1)}) %all-gather.23.cloned.1.call-update) | async-done | bytes 1572880 | tf_op jit(solution)/shard_map/all_gather | solution.py:214
  312.3 2.8 fusion.184
  315.4 29.8 %all-gather.29.cloned.1.call-done = bf16[1,1024,768]{2,1,0:T(8,128)(2,1)} async-done(((bf16[1,256,768]{2,1,0:T(8,128)(2,1)}), bf16[1,1024,768]{2,1,0:T(8,128)(2,1)}) %all-gather.29.cloned.1.call-update) | async-done | bytes 1572880 | tf_op jit(solution)/shard_map/all_gather | solution.py:135
  346.9 31.2 %all-gather.19.cloned.1.call-done = bf16[1,1024,768]{2,1,0:T(8,128)(2,1)} async-done(((bf16[1,256,768]{2,1,0:T(8,128)(2,1)}), bf16[1,1024,768]{2,1,0:T(8,128)(2,1)}) %all-gather.19.cloned.1.call-update) | async-done | bytes 1572880 | tf_op jit(solution)/shard_map/all_gather | solution.py:135
  379.7 31.6 %all-gather.21.cloned.1.call-done = bf16[1,1024,768]{2,1,0:T(8,128)(2,1)} async-done(((bf16[1,256,768]{2,1,0:T(8,128)(2,1)}), bf16[1,1024,768]{2,1,0:T(8,128)(2,1)}) %all-gather.21.cloned.1.call-update) | async-done | bytes 1572880 | tf_op jit(solution)/shard_map/all_gather | solution.py:135
  416.6 27.6 %all-gather.25.cloned.1.call-done = bf16[1,1024,768]{2,1,0:T(8,128)(2,1)} async-done(((bf16[1,256,768]{2,1,0:T(8,128)(2,1)}), bf16[1,1024,768]{2,1,0:T(8,128)(2,1)}) %all-gather.25.cloned.1.call-update) | async-done | bytes 1572880 | tf_op jit(solution)/shard_map/all_gather | solution.py:135
  463.6 3.9 select_reduce_fusion.4
  467.5 3.8 select_reduce_fusion.5
  473.1 3.4 fusion.482
  477.7 3.0 convolution_bitcast_fusion.4
  480.8 3.8 exponential_reduce_fusion.4
  484.7 4.0 exponential_reduce_fusion.5
  507.4 3.1 convolution_bitcast_fusion.5
  511.9 13.1 %reduce-scatter.26.cloned.1.call-done = f32[1,256,768]{2,1,0:T(8,128)} async-done(((f32[1,1024,768]{2,1,0:T(8,128)}), f32[1,256,768]{2,1,0:T(8,128)}) %reduce-scatter.26.cloned.1.call-update) | async-done | bytes 786448 | tf_op jit(solution)/shard_map/reduce_scatter | solution.py:261
  525.0 47.0 %reduce-scatter.24.cloned.1.call-done = f32[1,256,768]{2,1,0:T(8,128)} async-done(((f32[1,1024,768]{2,1,0:T(8,128)}), f32[1,256,768]{2,1,0:T(8,128)}) %reduce-scatter.24.cloned.1.call-update) | async-done | bytes 786448 | tf_op jit(solution)/shard_map/reduce_scatter | solution.py:260
  571.9 2.7 fusion.298
  589.2 3.7 fusion.212
  594.5 20.1 %all-gather.27.cloned.1.call-done = bf16[1,1024,768]{2,1,0:T(8,128)(2,1)} async-done(((bf16[1,256,768]{2,1,0:T(8,128)(2,1)}), bf16[1,1024,768]{2,1,0:T(8,128)(2,1)}) %all-gather.27.cloned.1.call-update) | async-done | bytes 1572880 | tf_op jit(solution)/shard_map/all_gather | solution.py:214
  614.6 5.5 fusion.483
  621.2 3.1 convolution_bitcast_fusion.2
  626.7 4.8 multiply_reduce_fusion.3
  647.1 3.0 convolution_bitcast_fusion.3
  674.2 5.2 exponential_reduce_fusion.1
  679.4 5.4 exponential_reduce_fusion
  684.8 30.5 %reduce-scatter.28.cloned.1.call-done = f32[1,256,768]{2,1,0:T(8,128)} async-done(((f32[1,1024,768]{2,1,0:T(8,128)}), f32[1,256,768]{2,1,0:T(8,128)}) %reduce-scatter.28.cloned.1.call-update) | async-done | bytes 786448 | tf_op jit(solution)/shard_map/reduce_scatter | solution.py:260
  715.3 2.7 fusion.287
  718.0 2.8 select_bitcast_fusion
  722.7 5.2 fusion.232
  733.4 4.6 fusion.236
  744.7 2.7 fusion.116
  747.4 15.0 %all-gather.31.cloned.1.call-done = bf16[1,1024,768]{2,1,0:T(8,128)(2,1)} async-done(((bf16[1,256,768]{2,1,0:T(8,128)(2,1)}), bf16[1,1024,768]{2,1,0:T(8,128)(2,1)}) %all-gather.31.cloned.1.call-update) | async-done | bytes 1572880 | tf_op jit(solution)/shard_map/all_gather | solution.py:214
  764.5 5.4 fusion.357
  769.9 7.2 multiply_reduce_fusion.1
  785.5 7.5 multiply_reduce_fusion
  803.7 2.9 copy.40
  806.7 2.8 reshape.2915
  809.7 3.5 fusion.209
  813.3 2.8 fusion.481
  817.3 3.1 convolution_bitcast_fusion
  821.9 3.1 convolution_bitcast_fusion.1
  826.4 6.2 fusion.202
  832.7 4.6 fusion.231
  837.3 4.7 fusion.230
  845.9 3.3 fusion.318
  851.2 3.3 add_add_fusion.1
  854.5 3.7 fusion.93
  861.0 3.3 add_add_fusion
  869.5 28.5 %reduce-scatter.34.cloned.1.call-done = f32[1,256,768]{2,1,0:T(8,128)} async-done(((f32[1,1024,768]{2,1,0:T(8,128)}), f32[1,256,768]{2,1,0:T(8,128)}) %reduce-scatter.34.cloned.1.call-update) | async-done | bytes 786448 | tf_op jit(solution)/shard_map/reduce_scatter | solution.py:261
  897.9 47.0 %reduce-scatter.32.cloned.1.call-done = f32[1,256,768]{2,1,0:T(8,128)} async-done(((f32[1,1024,768]{2,1,0:T(8,128)}), f32[1,256,768]{2,1,0:T(8,128)}) %reduce-scatter.32.cloned.1.call-update) | async-done | bytes 786448 | tf_op jit(solution)/shard_map/reduce_scatter | solution.py:260
  944.9 2.7 fusion.276
  947.7 78.1 %all-reduce = (f32[1,2,768]{2,1,0:T(2,128)}, f32[1,2,768]{2,1,0:T(2,128)}, f32[1,2,768]{2,1,0:T(2,128)}, f32[1,3072]{1,0:T(1,128)}, f32[1,768]{1,0:T(1,128)}) all-reduce(f32[1,2,768]{2,1,0:T(2,128)S(1)} %fusion.405, f32[1,2,768]{2,1,0:T(2,128)S(1)} %fusion.407, ...), channel_id=1, replica_groups=mesh['section'=2,'dp'=4,'tensor'=4] {'dp','tensor'}, use_global_device_ids=true, to_apply=%region_87.88 | all-reduce | flops 8448 | bytes 67584 | tf_op jit(solution)/shard_map/psum | solution.py:378
  1030.8 13.1 %reduce-scatter.36.cloned.1.call-done = f32[192,768]{1,0:T(8,128)} async-done(((f32[768,768]{1,0:T(8,128)}), f32[192,768]{1,0:T(8,128)}) %reduce-scatter.36.cloned.1.call-update) | async-done | bytes 589840 | tf_op jit(solution)/shard_map/reduce_scatter | solution.py:367
  1043.9 50.4 %reduce-scatter.38.cloned.1.call-done = f32[768,192]{0,1:T(8,128)} async-done(((f32[768,768]{0,1:T(8,128)}), f32[768,192]{0,1:T(8,128)}) %reduce-scatter.38.cloned.1.call-update) | async-done | bytes 589840 | tf_op jit(solution)/shard_map/reduce_scatter | solution.py:368
  (839 shorter events, 230.8 us)
Async XLA Ops:
  7.2 74.0 %copy-start = (f32[1,3072]{1,0:T(1,128)S(1)}, f32[1,3072]{1,0:T(1,128)}, u32[]{:S(2)}) copy-start(f32[1,3072]{1,0:T(1,128)} %param.22) | copy-start | bytes 36868
  7.2 77.8 %all-gather.33.cloned.1.call-start = ((), (), s32[]{:S(2)}) async-start(), calls=%async_computation.30 | async-start | bytes 1966080 | tf_op jit(solution)/shard_map/all_gather | solution.py:135
  9.0 91.5 %all-gather.35.cloned.1.call-start = ((), (), s32[]{:S(2)}) async-start(), calls=%async_computation.31 | async-start | bytes 1474560 | tf_op jit(solution)/shard_map/all_gather | solution.py:317
  9.8 107.8 %all-gather.37.cloned.1.call-start = ((), (), s32[]{:S(2)}) async-start(), calls=%async_computation.32 | async-start | bytes 1474560 | tf_op jit(solution)/shard_map/all_gather | solution.py:318
  10.5 161.1 %reduce-scatter.18.cloned.1.call-start = ((), (), s32[]{:S(2)}) async-start(), calls=%async_computation.13 | async-start | bytes 3932160 | tf_op jit(solution)/shard_map/reduce_scatter | solution.py:188
  10.6 166.3 %copy-start.137 = (s32[512]{0:T(512)}, s32[512]{0:T(512)S(1)}, u32[]{:S(2)}) copy-start(s32[512]{0:T(512)S(1)} %iota_add_fusion) | copy-start | bytes 6148
  13.6 85.1 %copy-start.173 = (f32[3,64]{1,0:T(4,128)}, f32[3,64]{1,0:T(4,128)S(1)}, u32[]{:S(2)}) copy-start(f32[3,64]{1,0:T(4,128)S(1)} %add.830) | copy-start | bytes 2308
  14.4 574.3 %copy-start.117 = (f32[768]{0:T(1024)}, f32[768]{0:T(1024)S(1)}, u32[]{:S(2)}) copy-start(f32[768]{0:T(1024)S(1)} %get-tuple-element.91) | copy-start | bytes 9220
  15.3 73.5 %copy-start.189 = (f32[768]{0:T(1024)}, f32[768]{0:T(1024)S(1)}, u32[]{:S(2)}) copy-start(f32[768]{0:T(1024)S(1)} %get-tuple-element.92) | copy-start | bytes 9220
  15.3 102.4 %copy-start.186 = (f32[768]{0:T(1024)}, f32[768]{0:T(1024)S(1)}, u32[]{:S(2)}) copy-start(f32[768]{0:T(1024)S(1)} %get-tuple-element.93) | copy-start | bytes 9220
  15.5 625.9 %copy-start.45 = (f32[1024,8]{0,1:T(8,128)}, f32[1024,8]{0,1:T(8,128)S(1)}, u32[]{:S(2)}) copy-start(f32[1024,8]{0,1:T(8,128)S(1)} %get-tuple-element.239) | copy-start | bytes 98308
  15.5 625.9 %copy-start.76 = (f32[1024,8]{0,1:T(8,128)}, f32[1024,8]{0,1:T(8,128)S(1)}, u32[]{:S(2)}) copy-start(f32[1024,8]{0,1:T(8,128)S(1)} %get-tuple-element.237) | copy-start | bytes 98308
  39.6 84.6 %copy-start.41 = (bf16[1,192,768]{2,1,0:T(8,128)(2,1)}, bf16[1,192,768]{2,1,0:T(8,128)(2,1)S(1)}, u32[]{:S(2)}) copy-start(bf16[1,192,768]{2,1,0:T(8,128)(2,1)S(1)} %copy.36) | copy-start | bytes 884740
  128.4 43.3 %copy-start.20 = (bf16[2,1,256,768]{3,2,1,0:T(8,128)(2,1)S(1)}, bf16[2,1,256,768]{3,2,1,0:T(8,128)(2,1)}, u32[]{:S(2)}) copy-start(bf16[2,1,256,768]{3,2,1,0:T(8,128)(2,1)} %param.12) | copy-start | bytes 2359300
  128.4 48.5 %copy-start.179 = (s32[1,512]{1,0:T(1,128)S(1)}, s32[1,512]{1,0:T(1,128)}, u32[]{:S(2)}) copy-start(s32[1,512]{1,0:T(1,128)} %get-tuple-element.283) | copy-start | bytes 6148
  128.4 48.5 %copy-start.180 = (s32[1,512]{1,0:T(1,128)S(1)}, s32[1,512]{1,0:T(1,128)}, u32[]{:S(2)}) copy-start(s32[1,512]{1,0:T(1,128)} %get-tuple-element.284) | copy-start | bytes 6148
  128.4 79.6 %all-gather.17.cloned.1.call-start = ((), (), s32[]{:S(2)}) async-start(), calls=%async_computation.14 | async-start | bytes 1966080 | tf_op jit(solution)/shard_map/all_gather | solution.py:135
  129.1 149.8 %copy-start.127 = (f32[768]{0:T(1024)}, f32[768]{0:T(1024)S(1)}, u32[]{:S(2)}) copy-start(f32[768]{0:T(1024)S(1)} %reduce.114) | copy-start | bytes 9220
  172.9 39.0 %copy-start.190 = (f32[768]{0:T(1024)S(1)}, f32[768]{0:T(1024)}, u32[]{:S(2)}) copy-start(f32[768]{0:T(1024)} %copy-done.189) | copy-start | bytes 9220
  172.9 3.1 collective-permute-start
  176.8 102.1 %reduce-scatter.20.cloned.1.call-start = ((), (), s32[]{:S(2)}) async-start(), calls=%async_computation.15 | async-start | bytes 3932160 | tf_op jit(solution)/shard_map/reduce_scatter | solution.py:188
  234.8 44.1 %copy-start.7 = (bf16[1,256,768]{2,1,0:T(8,128)(2,1)S(1)}, bf16[1,256,768]{2,1,0:T(8,128)(2,1)}, u32[]{:S(2)}) copy-start(bf16[1,256,768]{2,1,0:T(8,128)(2,1)} %bitcast_select_fusion.3) | copy-start | bytes 1179652
  234.8 77.5 %all-gather.23.cloned.1.call-start = ((), (), s32[]{:S(2)}) async-start(), calls=%async_computation.19 | async-start | bytes 1966080 | tf_op jit(solution)/shard_map/all_gather | solution.py:214
  237.5 107.7 %all-gather.29.cloned.1.call-start = ((), (), s32[]{:S(2)}) async-start(), calls=%async_computation.26 | async-start | bytes 1966080 | tf_op jit(solution)/shard_map/all_gather | solution.py:135
  281.4 3.1 collective-permute-start.1
  285.6 92.4 %all-gather.19.cloned.1.call-start = ((), (), s32[]{:S(2)}) async-start(), calls=%async_computation.16 | async-start | bytes 1966080 | tf_op jit(solution)/shard_map/all_gather | solution.py:135
  286.4 124.9 %all-gather.21.cloned.1.call-start = ((), (), s32[]{:S(2)}) async-start(), calls=%async_computation.18 | async-start | bytes 1966080 | tf_op jit(solution)/shard_map/all_gather | solution.py:135
  286.4 60.4 %copy-start.143 = (f32[256]{0:T(256)}, f32[256]{0:T(256)S(1)}, u32[]{:S(2)}) copy-start(f32[256]{0:T(256)S(1)} %broadcast_multiply_fusion.11) | copy-start | bytes 3076
  289.3 154.9 %all-gather.25.cloned.1.call-start = ((), (), s32[]{:S(2)}) async-start(), calls=%async_computation.22 | async-start | bytes 1966080 | tf_op jit(solution)/shard_map/all_gather | solution.py:135
  315.2 209.8 %reduce-scatter.26.cloned.1.call-start = ((), (), s32[]{:S(2)}) async-start(), calls=%async_computation.21 | async-start | bytes 3932160 | tf_op jit(solution)/shard_map/reduce_scatter | solution.py:261
  413.1 44.9 %copy-start.154 = (f32[1024]{0:T(1024)}, f32[1024]{0:T(1024)S(1)}, u32[]{:S(2)}) copy-start(f32[1024]{0:T(1024)S(1)} %broadcast_multiply_fusion.1) | copy-start | bytes 12292
  415.2 42.9 %copy-start.194 = (f32[1024]{0:T(1024)}, f32[1024]{0:T(1024)S(1)}, u32[]{:S(2)}) copy-start(f32[1024]{0:T(1024)S(1)} %add_rsqrt_fusion) | copy-start | bytes 12292
  415.2 39.8 %copy-start.163 = (f32[1024]{0:T(1024)}, f32[1024]{0:T(1024)S(1)}, u32[]{:S(2)}) copy-start(f32[1024]{0:T(1024)S(1)} %broadcast_multiply_fusion.4) | copy-start | bytes 12292
  415.9 39.1 %copy-start.204 = (f32[1024]{0:T(1024)}, f32[1024]{0:T(1024)S(1)}, u32[]{:S(2)}) copy-start(f32[1024]{0:T(1024)S(1)} %add_rsqrt_fusion.3) | copy-start | bytes 12292
  415.9 55.3 %copy-start.157 = (f32[1024]{0:T(1024)}, f32[1024]{0:T(1024)S(1)}, u32[]{:S(2)}) copy-start(f32[1024]{0:T(1024)S(1)} %broadcast_multiply_fusion.3) | copy-start | bytes 12292
  416.6 54.7 %copy-start.197 = (f32[1024]{0:T(1024)}, f32[1024]{0:T(1024)S(1)}, u32[]{:S(2)}) copy-start(f32[1024]{0:T(1024)S(1)} %add_rsqrt_fusion.2) | copy-start | bytes 12292
  446.0 142.7 %copy-start.160 = (f32[1024]{0:T(1024)}, f32[1024]{0:T(1024)S(1)}, u32[]{:S(2)}) copy-start(f32[1024]{0:T(1024)S(1)} %broadcast_multiply_fusion.2) | copy-start | bytes 12292
  480.8 91.2 %reduce-scatter.24.cloned.1.call-start = ((), (), s32[]{:S(2)}) async-start(), calls=%async_computation.20 | async-start | bytes 3932160 | tf_op jit(solution)/shard_map/reduce_scatter | solution.py:260
  510.5 67.7 %copy-start.68 = (f32[1,1024,3,64]{1,3,2,0:T(8,128)S(1)}, f32[1,1024,3,64]{1,3,2,0:T(8,128)}, u32[]{:S(2)}) copy-start(f32[1,1024,3,64]{1,3,2,0:T(8,128)} %copy-done.67) | copy-start | bytes 2359300
  510.5 104.1 %all-gather.27.cloned.1.call-start = ((), (), s32[]{:S(2)}) async-start(), calls=%async_computation.23 | async-start | bytes 1966080 | tf_op jit(solution)/shard_map/all_gather | solution.py:214
  511.8 66.4 %copy-start.103 = (f32[1,1024,3,8]{1,3,2,0:T(8,128)S(1)}, f32[1,1024,3,8]{1,3,2,0:T(8,128)}, u32[]{:S(2)}) copy-start(f32[1,1024,3,8]{1,3,2,0:T(8,128)} %get-tuple-element.155) | copy-start | bytes 294916
  576.9 4.2 collective-permute-start.2
  583.5 101.3 %reduce-scatter.30.cloned.1.call-start = ((), (), s32[]{:S(2)}) async-start(), calls=%async_computation.25 | async-start | bytes 3932160 | tf_op jit(solution)/shard_map/reduce_scatter | solution.py:261
  624.4 90.9 %reduce-scatter.28.cloned.1.call-start = ((), (), s32[]{:S(2)}) async-start(), calls=%async_computation.24 | async-start | bytes 3932160 | tf_op jit(solution)/shard_map/reduce_scatter | solution.py:260
  650.2 112.2 %all-gather.31.cloned.1.call-start = ((), (), s32[]{:S(2)}) async-start(), calls=%async_computation.27 | async-start | bytes 1966080 | tf_op jit(solution)/shard_map/all_gather | solution.py:214
  652.8 124.3 %copy-start.12 = (pred[512,1024]{1,0:T(8,128)(4,1)}, pred[512,1024]{1,0:T(8,128)(4,1)S(1)}, u32[]{:S(2)}) copy-start(pred[512,1024]{1,0:T(8,128)(4,1)S(1)} %get-tuple-element.212) | copy-start | bytes 1572868
  652.8 144.7 %copy-start.14 = (pred[512,1024]{1,0:T(8,128)(4,1)}, pred[512,1024]{1,0:T(8,128)(4,1)S(1)}, u32[]{:S(2)}) copy-start(pred[512,1024]{1,0:T(8,128)(4,1)S(1)} %get-tuple-element.213) | copy-start | bytes 1572868
  679.4 38.6 %copy-start.22 = (f32[1,256,768]{2,1,0:T(8,128)S(1)}, f32[1,256,768]{2,1,0:T(8,128)}, u32[]{:S(2)}) copy-start(f32[1,256,768]{2,1,0:T(8,128)} %copy-done.21) | copy-start | bytes 2359300
  684.8 37.9 %copy-start.122 = (f32[3,512]{1,0:T(4,128)S(1)}, f32[3,512]{1,0:T(4,128)}, u32[]{:S(2)}) copy-start(f32[3,512]{1,0:T(4,128)} %copy-done.121) | copy-start | bytes 18436
  720.8 7.2 collective-permute-start.3
  730.4 135.0 %reduce-scatter.42.cloned.1.call-start = ((), (), s32[]{:S(2)}) async-start(), calls=%async_computation.36 | async-start | bytes 983040
  785.4 81.8 %reduce-scatter.40.cloned.1.call-start = ((), (), s32[]{:S(2)}) async-start(), calls=%async_computation.35 | async-start | bytes 2457600
  809.6 88.4 %reduce-scatter.34.cloned.1.call-start = ((), (), s32[]{:S(2)}) async-start(), calls=%async_computation.29 | async-start | bytes 3932160 | tf_op jit(solution)/shard_map/reduce_scatter | solution.py:261
  820.4 124.5 %reduce-scatter.32.cloned.1.call-start = ((), (), s32[]{:S(2)}) async-start(), calls=%async_computation.28 | async-start | bytes 3932160 | tf_op jit(solution)/shard_map/reduce_scatter | solution.py:260
  825.1 200.7 %reduce-scatter.22.cloned.1.call-start = ((), (), s32[]{:S(2)}) async-start(), calls=%async_computation.17 | async-start | bytes 3932160 | tf_op jit(solution)/shard_map/reduce_scatter | solution.py:188
  844.5 199.4 %reduce-scatter.36.cloned.1.call-start = ((), (), s32[]{:S(2)}) async-start(), calls=%async_computation.33 | async-start | bytes 2949120 | tf_op jit(solution)/shard_map/reduce_scatter | solution.py:367
  854.5 239.8 %reduce-scatter.38.cloned.1.call-start = ((), (), s32[]{:S(2)}) async-start(), calls=%async_computation.34 | async-start | bytes 2949120 | tf_op jit(solution)/shard_map/reduce_scatter | solution.py:368
  864.3 80.6 %copy-start.11 = (bf16[1,256,768]{2,1,0:T(8,128)(2,1)S(1)}, bf16[1,256,768]{2,1,0:T(8,128)(2,1)}, u32[]{:S(2)}) copy-start(bf16[1,256,768]{2,1,0:T(8,128)(2,1)} %get-tuple-element.106) | copy-start | bytes 1179652
  864.3 80.6 %copy-start.144 = (f32[256]{0:T(256)S(1)}, f32[256]{0:T(256)}, u32[]{:S(2)}) copy-start(f32[256]{0:T(256)} %copy-done.143) | copy-start | bytes 3076
  864.3 161.5 %copy-start.8 = (bf16[1,256,768]{2,1,0:T(8,128)(2,1)S(1)}, bf16[1,256,768]{2,1,0:T(8,128)(2,1)}, u32[]{:S(2)}) copy-start(bf16[1,256,768]{2,1,0:T(8,128)(2,1)} %bitcast_select_fusion.3) | copy-start | bytes 1179652
  864.3 161.5 %copy-start.51 = (bf16[1,256,768]{2,1,0:T(8,128)(2,1)S(1)}, bf16[1,256,768]{2,1,0:T(8,128)(2,1)}, u32[]{:S(2)}) copy-start(bf16[1,256,768]{2,1,0:T(8,128)(2,1)} %get-tuple-element.107) | copy-start | bytes 1179652
  864.4 161.5 %copy-start.128 = (f32[768]{0:T(1024)S(1)}, f32[768]{0:T(1024)}, u32[]{:S(2)}) copy-start(f32[768]{0:T(1024)} %copy-done.127) | copy-start | bytes 9220
  864.4 83.3 %copy-start.170 = (f32[256]{0:T(256)}, f32[256]{0:T(256)S(1)}, u32[]{:S(2)}) copy-start(f32[256]{0:T(256)S(1)} %add_rsqrt_fusion.6) | copy-start | bytes 3076
  1028.9 65.4 %copy-start.1 = (f32[1,3072]{1,0:T(1,128)S(1)}, f32[1,3072]{1,0:T(1,128)}, u32[]{:S(2)}) copy-start(f32[1,3072]{1,0:T(1,128)} %param.22) | copy-start | bytes 36868
  (226 other events, 1147.7 us)
Sparse Core Ops, SparseCore 0:
  10.4 33.6 all-gather.32
  45.7 40.4 all-gather.34
  87.8 29.7 all-gather.36
  128.5 43.0 reduce-scatter.17
  177.0 30.9 all-gather.16
  234.9 43.9 reduce-scatter.19
  281.3 30.9 all-gather.22
  314.2 30.9 all-gather.28
  347.0 30.9 all-gather.18
  380.3 30.9 all-gather.20
  413.1 30.9 all-gather.24
  480.9 44.0 reduce-scatter.25
  528.0 43.9 reduce-scatter.23
  583.6 30.9 all-gather.26
  624.5 43.9 reduce-scatter.29
  671.3 43.9 reduce-scatter.27
  730.5 31.7 all-gather.30
  785.5 23.3 reduce-scatter.41
  811.2 40.6 reduce-scatter.39
  854.7 43.1 reduce-scatter.33
  900.9 43.9 reduce-scatter.31
  947.9 44.9 reduce-scatter.21
  995.8 48.1 reduce-scatter.35
  1046.7 47.6 reduce-scatter.37
where the time goes:
time: 1110 us; the launch traced here: 1100 us
  waiting for transfers between devices  545 us (49%)
  matrix products  232 us (21%)
  blocking collectives  140 us (13%)
  other arithmetic  106 us (10%)
  local copies, waits for them, and re-layouts  51.3 us (5%)
  between operations  18.4 us (2%)
    all_gather x6, waiting for transfers between devices, layer_pieces(): gathered = lax.all_gather(x_part, 'tensor', axis=1, tiled=True)  150 us
    reduce_scatter x3, waiting for transfers between devices, layer_backward(): lax.psum_scatter(attn_in_grad, 'tensor', scatter_dimension=1, tiled=True)  124 us
    reduce_scatter x3, waiting for transfers between devices, layer_forward(): summed = lax.psum_scatter(branch, 'tensor', scatter_dimension=1, tiled=True)  83.9 us
    psum x1, blocking collectives, body(): lax.psum((small_held[0], small_held[1], qv_full, up_full, small_held[4]),...  78.1 us
    all_gather x3, waiting for transfers between devices, layer_backward(): gradient_rows = lax.all_gather(grad_b, 'tensor', axis=1, tiled=True)  58 us
    reduce_scatter x1, waiting for transfers between devices, body(): lax.psum_scatter(matrix_grads[3], 'dp', scatter_dimension=1, tiled=True)  50.4 us
    reduce_scatter x3, waiting for transfers between devices, layer_backward(): lax.psum_scatter(feedforward_input_gradient, 'tensor', scatter_dimension=...  41.6 us
    all_gather x1, blocking collectives, fetch_weights(): lax.all_gather(shards[0], 'dp', axis=1, tiled=True)  40.7 us
  transfers between devices with their start and end apart: 28, of which 21 were waited for; matrix products, arithmetic and copies ran while one was open for 23% of the time, Pallas kernels for 0%

commit v1 on v0

v1 whole, which is shorter than its diff:
```python
import functools
import math

import jax
import jax.numpy as jnp
import numpy as np
from jax import lax
from jax.experimental import pallas as pl
from jax.experimental.pallas import tpu as pltpu
from jax.sharding import PartitionSpec as P

HEAD_DIM = 64
ROT = 16
SEG_MOST = 384
EPS = 1e-05
MASKED = -1e30
ROOT_HALF = 0.7071067811865476
INV_ROOT_TAU = 0.3989422804014327

BF = jnp.bfloat16
F32 = jnp.float32
MESH = pl.DeviceIdType.MESH

NN = (((1,), (0,)), ((), ()))
NT = (((1,), (1,)), ((), ()))
TN = (((0,), (0,)), ((), ()))

BQ = 128
BK = BQ + SEG_MOST
HL = 256
QO, KO, VO, OO = 0, 192, 384, 576


def mm(a, b, dims):
    return lax.dot_general(a, b, dims, preferred_element_type=F32)


def lane_iota(rows, cols=HL):
    return lax.broadcasted_iota(jnp.int32, (rows, cols), 1)


def remote(src, dst, send, recv, dev):
    return pltpu.make_async_remote_copy(
        src_ref=src, dst_ref=dst, send_sem=send, recv_sem=recv, device_id=dev, device_id_type=MESH
    )


def kernel(
    n,
    heads,
    x_in,
    cot_in,
    segc_in,
    segr_in,
    w_in,
    par_in,
    taba,
    tabb,
    out_y,
    out_g,
    out_w,
    out_s,
    w,
    x,
    an,
    mn,
    mu,
    rstd,
    qb,
    kb,
    vb,
    cb,
    lse,
    slope,
    hid,
    gb,
    du,
    dqkv,
    dc,
    dq,
    dk,
    dv,
    bias,
    pscr,
    dpscr,
    sendb,
    recvb,
    ownp,
    gw,
    gsr,
    zrecv,
    wacc,
    cotv,
    yst,
    gst,
    segc,
    par,
    sm,
    smr,
    smt,
    smz,
    tall,
    lsem,
    psem,
    xs,
    xr,
    gs,
    gr,
    ws,
    wr,
    fs,
    fr,
    rss,
    rsr,
    osend,
    orecv,
    ghs,
    ghr,
    zs,
    zr,
    sms,
    smrs,
):
    s = lax.axis_index("section")
    z = lax.axis_index("dp")
    t = lax.axis_index("tensor")
    sib = (1 - s, z, t)
    width = x.shape[2]
    length = x.shape[1]
    chunk = length // 4
    rows_z = w_in.shape[1]
    nblk = length // BQ
    own = pl.ds(t * chunk, chunk)
    zrows = pl.ds(z * rows_z, rows_z)

    def plane(k):
        return (s, z, t ^ k)

    def other_z(j):
        return lax.rem(z + j, n)

    lx = pltpu.make_async_copy(x_in.at[s], x.at[0, own], lsem.at[0])
    lc = pltpu.make_async_copy(cot_in.at[s], cotv, lsem.at[1])
    lw = [
        pltpu.make_async_copy(w_in.at[p], w.at[s, p, zrows], lsem.at[2 + p]) for p in range(3)
    ]
    lseg = pltpu.make_async_copy(segc_in.at[s], segc, lsem.at[5])
    lpar = pltpu.make_async_copy(par_in, par.at[s], lsem.at[6])
    lx.start()
    for p in range(3):
        lw[p].start()
    lpar.start()
    lc.start()
    lseg.start()

    barrier = pltpu.get_barrier_semaphore()
    pl.semaphore_signal(barrier, inc=1, device_id=sib, device_id_type=MESH)
    for k in range(1, 4):
        pl.semaphore_signal(barrier, inc=1, device_id=plane(k), device_id_type=MESH)
    for j in range(1, n):
        pl.semaphore_signal(barrier, inc=1, device_id=(s, other_z(j), t), device_id_type=MESH)
    pl.semaphore_wait(barrier, 4 + n - 1)

    def w_copy(p, j):
        return remote(
            w.at[s, p, zrows],
            w.at[s, p, zrows],
            ws.at[p, j - 1],
            wr.at[p, j - 1],
            (s, other_z(j), t),
        )

    def w_arrival(p, j):
        rows = pl.ds(other_z(n - j) * rows_z, rows_z)
        return remote(
            w.at[s, p, rows], w.at[s, p, rows], ws.at[p, j - 1], wr.at[p, j - 1], (s, z, t ^ 1)
        )

    def forward(layer, p):
        return remote(w.at[layer, p], w.at[layer, p], fs.at[p], fr.at[p], sib)

    def x_copy(layer, k):
        return remote(
            x.at[layer, own], x.at[layer, own], xs.at[layer, k - 1], xr.at[layer, k - 1], plane(k)
        )

    def x_arrival(layer, k):
        rows = pl.ds((t ^ k) * chunk, chunk)
        return remote(
            x.at[layer, rows],
            x.at[layer, rows],
            xs.at[layer, k - 1],
            xr.at[layer, k - 1],
            plane(k),
        )

    def g_copy(layer, k):
        return remote(
            gb.at[layer, own], gb.at[layer, own], gs.at[layer, k - 1], gr.at[layer, k - 1], plane(k)
        )

    def g_arrival(layer, k):
        rows = pl.ds((t ^ k) * chunk, chunk)
        return remote(
            gb.at[layer, rows],
            gb.at[layer, rows],
            gs.at[layer, k - 1],
            gr.at[layer, k - 1],
            plane(k),
        )

    def part_copy(phase, k):
        return remote(
            sendb.at[k - 1],
            recvb.at[phase % 2, k - 1],
            rss.at[phase, k - 1],
            rsr.at[phase, k - 1],
            plane(k),
        )

    lx.wait()
    for k in range(1, 4):
        x_copy(0, k).start()
    lpar.wait()
    par_copy = remote(par.at[s], par.at[s], psem.at[0], psem.at[1], sib)
    par_copy.start()
    for p in range(3):
        lw[p].wait()

    @pl.when(s == 0)
    def _():
        for p in range(3):
            for j in range(1, n):
                w_copy(p, j).start()

    lc.wait()
    gb[1, own, :] = cotv[...].astype(BF)
    for k in range(1, 4):
        g_copy(1, k).start()

    lseg.wait()

    @pl.loop(0, nblk)
    def _(b):
        q0 = pl.multiple_of(b * BQ, BQ)
        k0 = pl.multiple_of(jnp.maximum(b * BQ - SEG_MOST, 0), BQ)
        seg_k = segc[pl.ds(k0, BK), :]
        seg_q = jnp.where(
            s == 0, segr_in[0:1, pl.ds(q0, BQ)], segr_in[1:2, pl.ds(q0, BQ)]
        )
        kpos = lax.broadcasted_iota(jnp.int32, (BK, BQ), 0) + k0
        qpos = lax.broadcasted_iota(jnp.int32, (BK, BQ), 1) + q0
        allowed = (seg_k == seg_q) & (kpos <= qpos)
        bias[b] = jnp.where(allowed, 0.0, MASKED).astype(BF)

    par_wait = remote(par.at[1 - s], par.at[1 - s], psem.at[0], psem.at[1], sib)
    par_copy.wait_send()
    par_wait.wait_recv()

    @pl.loop(0, 2)
    def _(i):
        sm[i] = jnp.zeros((8, width), F32)

    def need_w(layer, p):
        @pl.when(s == layer)
        def _():
            for j in range(1, n):
                w_arrival(p, j).wait_recv()
            forward(layer, p).start()

        @pl.when(s != layer)
        def _():
            forward(layer, p).wait_recv()
            if layer == 0:
                for j in range(1, n):
                    w_copy(p, j).start()

    def prow(layer, r, cols=None):
        if cols is None:
            return par[layer, r : r + 1, :]
        return par[layer, r : r + 1, cols]

    def rope_tables(b, sign):
        ca = taba[0, b]
        sa = taba[1, b]
        c0 = tabb[0]
        s0 = tabb[1]
        cos = ca * c0 - sa * s0
        sin = sa * c0 + ca * s0
        lane = lane_iota(BQ) & (HEAD_DIM - 1)
        return cos, jnp.where(lane < ROT // 2, -sign, sign) * sin

    def rope(u, b, sign):
        halves = []
        lane = lane_iota(BQ) & (HEAD_DIM - 1)
        for i in range(u.shape[0] // BQ):
            part = u[i * BQ : (i + 1) * BQ]
            cos, sin = rope_tables(b + i, sign)
            partner = jnp.where(
                lane < ROT // 2,
                pltpu.roll(part, HL - ROT // 2, 1),
                pltpu.roll(part, ROT // 2, 1),
            )
            halves.append(part * cos + partner * sin)
        return jnp.concatenate(halves, axis=0)

    def stack_heads(block):
        lane = lane_iota(BQ) >> 6
        return jnp.concatenate(
            [jnp.where(lane == h, block, jnp.zeros_like(block)) for h in range(heads)], axis=0
        )

    sub = 64

    def norm_chunk(layer, c):
        @pl.loop(0, chunk // sub)
        def _(i):
            rows = pl.ds(pl.multiple_of(c * chunk + i * sub, sub), sub)
            v = x[layer, rows, :].astype(F32)
            m = jnp.mean(v, axis=-1, keepdims=True)
            v = v - m
            r = lax.rsqrt(jnp.mean(v * v, axis=-1, keepdims=True) + EPS)
            mu[layer, rows, :] = m
            rstd[layer, rows, :] = r
            v = v * r
            an[rows, :] = (v * prow(layer, 0) + prow(layer, 2)).astype(BF)
            mn[rows, :] = (v * prow(layer, 1) + prow(layer, 3)).astype(BF)

    def renorm_all(layer):
        @pl.loop(0, length // sub)
        def _(i):
            rows = pl.ds(pl.multiple_of(i * sub, sub), sub)
            v = (x[layer, rows, :].astype(F32) - mu[layer, rows, :]) * rstd[layer, rows, :]
            an[rows, :] = (v * prow(layer, 0) + prow(layer, 2)).astype(BF)
            mn[rows, :] = (v * prow(layer, 1) + prow(layer, 3)).astype(BF)

    def forward_layer(layer):
        phase = layer
        norm_chunk(layer, t)
        for k in range(1, 4):
            x_arrival(layer, k).wait_recv()
            norm_chunk(layer, t ^ k)
        need_w(layer, 0)

        @pl.loop(0, 4)
        def _(c):
            rows = pl.ds(pl.multiple_of(c * chunk, chunk), chunk)
            a = an[rows, :]
            b0 = c * (chunk // BQ)
            lane = lane_iota(chunk)
            u = mm(a, w[layer, 0, :, QO : QO + HL], NN) + prow(layer, 4, slice(0, HL))
            qb[layer, rows, :] = (rope(u, b0, 1.0) * 0.125).astype(BF)
            u = mm(a, w[layer, 0, :, KO - 64 : KO - 64 + HL], NN)
            kb[layer, rows, :] = rope(pltpu.roll(u, HL - 64, 1), b0, 1.0).astype(BF)
            u = mm(a, w[layer, 0, :, VO : VO + HL], NN) + prow(layer, 5, slice(0, HL))
            vb[layer, rows, :] = jnp.where(lane < heads * HEAD_DIM, u, 0.0).astype(BF)

        @pl.loop(0, nblk)
        def _(b):
            q0 = pl.multiple_of(b * BQ, BQ)
            k0 = pl.multiple_of(jnp.maximum(b * BQ - SEG_MOST, 0), BQ)
            qm = stack_heads(qb[layer, pl.ds(q0, BQ), :])
            top = None
            for i in range(BK // BQ):
                keys = kb[layer, pl.ds(k0 + i * BQ, BQ), :]
                blk = bias[b, i * BQ : (i + 1) * BQ, :].astype(F32)
                sc = mm(keys, qm, NT) + jnp.concatenate([blk] * heads, axis=1)
                pscr[i * BQ : (i + 1) * BQ, :] = sc
                peak = jnp.max(sc, axis=0, keepdims=True)
                top = peak if top is None else jnp.maximum(top, peak)
            total = None
            for i in range(BK // BQ):
                e = jnp.exp(pscr[i * BQ : (i + 1) * BQ, :] - top)
                pscr[i * BQ : (i + 1) * BQ, :] = e
                part = jnp.sum(e, axis=0, keepdims=True)
                total = part if total is None else total + part
            lse[layer, b] = top + jnp.log(total)
            inv = 1.0 / total
            lane = lane_iota(BQ) >> 6
            ctx = jnp.zeros((BQ, HL), F32)
            vals = vb[layer, pl.ds(k0, BK), :]
            for h in range(heads):
                cols = slice(h * BQ, (h + 1) * BQ)
                ph = (pscr[:, cols] * inv[:, cols]).astype(BF)
                ctx = jnp.where(lane == h, mm(ph, vals, TN), ctx)
            cb[layer, pl.ds(q0, BQ), :] = pltpu.roll(ctx, HL - heads * HEAD_DIM, 1).astype(BF)

        need_w(layer, 1)

        @pl.loop(0, 4)
        def _(c):
            rows = pl.ds(pl.multiple_of(c * chunk, chunk), chunk)
            a = mn[rows, :]
            for j in range(width // 256):
                cols = slice(j * 256, (j + 1) * 256)
                u = mm(a, w[layer, 1, :, cols], NN) + prow(layer, 6, cols)
                phi = 0.5 * (1.0 + lax.erf(u * ROOT_HALF))
                hid[layer, rows, cols] = (u * phi).astype(BF)
                slope[layer, rows, cols] = (
                    phi + u * INV_ROOT_TAU * jnp.exp(-0.5 * u * u)
                ).astype(BF)

        need_w(layer, 2)
        if layer == 1:
            for k in range(1, 4):
                part_copy(0, k).wait_send()
        for k in (1, 2, 3, 0):
            rows = pl.ds(pl.multiple_of((t ^ k) * chunk, chunk), chunk)
            c = cb[layer, rows, :]
            h = hid[layer, rows, :]
            for j in range(width // 256):
                cols = slice(j * 256, (j + 1) * 256)
                y = mm(c, w[layer, 0, cols, 512:768], NT) + mm(h, w[layer, 2, cols, :], NT)
                if k:
                    sendb[k - 1, :, cols] = y.astype(BF)
                else:
                    ownp[phase % 2, :, cols] = y
            if k:
                part_copy(phase, k).start()

    def place(layer, stage, out, idx):
        @pl.when(s == layer)
        def _():
            pltpu.make_async_copy(stage, out.at[s], osend.at[idx]).start()

        @pl.when(s != layer)
        def _():
            remote(stage, out.at[s], osend.at[idx], orecv.at[idx // 2], sib).start()

    def placed(layer, stage, out, idx):
        @pl.when(s == layer)
        def _():
            pltpu.make_async_copy(stage, out.at[s], osend.at[idx]).wait()

        @pl.when(s != layer)
        def _():
            remote(stage, out.at[s], osend.at[idx], orecv.at[idx // 2], sib).wait_send()

    def finish_y(layer):
        phase = layer
        for k in range(1, 4):
            part_copy(phase, k).wait_recv()
        if layer == 1:
            placed(0, yst, out_y, 0)

        @pl.loop(0, chunk // sub)
        def _(i):
            r = pl.ds(pl.multiple_of(i * sub, sub), sub)
            rows = pl.ds(pl.multiple_of(t * chunk + i * sub, sub), sub)
            y = x[layer, rows, :].astype(F32) + ownp[phase % 2, r, :] + prow(layer, 7)
            for k in range(3):
                y = y + recvb[phase % 2, k, r, :].astype(F32)
            yst[r, :] = y
            if layer == 0:
                x[1, rows, :] = y.astype(BF)

        if layer == 0:
            for k in range(1, 4):
                x_copy(1, k).start()
        place(layer, yst, out_y, layer)

    def reduce_start(layer, p, buf):
        @pl.when(s != layer)
        def _():
            remote(buf.at[p], gsr.at[p], ghs.at[p], ghr.at[p], sib).start()

    def z_copy(p, j, buf):
        rows = pl.ds(other_z(j) * rows_z, rows_z)
        return remote(
            buf.at[p, rows],
            zrecv.at[p, j - 1],
            zs.at[p, j - 1],
            zr.at[p, j - 1],
            (s, other_z(j), t),
        )

    step = 48

    def reduce_cores(layer, p, buf):
        @pl.when(s == layer)
        def _():
            remote(buf.at[p], gsr.at[p], ghs.at[p], ghr.at[p], sib).wait_recv()

            @pl.loop(0, rows_z // step)
            def _(i):
                r = pl.ds(pl.multiple_of(i * step, 16), step)
                q = pl.ds(pl.multiple_of(z * rows_z + i * step, 16), step)
                wacc[p, r, :] = buf[p, q, :].astype(F32) + gsr[p, q, :].astype(F32)

            for j in range(1, n):
                base = other_z(j) * rows_z

                @pl.loop(0, rows_z // step)
                def _(i):
                    q = pl.ds(pl.multiple_of(base + i * step, 16), step)
                    buf[p, q, :] = (buf[p, q, :].astype(F32) + gsr[p, q, :].astype(F32)).astype(BF)

                z_copy(p, j, buf).start()

        @pl.when(s != layer)
        def _():
            remote(buf.at[p], gsr.at[p], ghs.at[p], ghr.at[p], sib).wait_send()

    def grad_part(layer, p, buf):
        for j in range(width // 256):
            cols = slice(j * 256, (j + 1) * 256)
            if p == 2:
                buf[p, cols, :] = mm(gb[layer, :, cols], hid[layer], TN).astype(BF)
            elif p == 1:
                buf[p, cols, :] = mm(mn[:, cols], du[...], TN).astype(BF)
            else:
                buf[p, cols, 0:512] = mm(an[:, cols], dqkv[:, 0:512], TN).astype(BF)
                buf[p, cols, 512:768] = (
                    mm(an[:, cols], dqkv[:, 512:768], TN) + mm(gb[layer, :, cols], cb[layer], TN)
                ).astype(BF)
        reduce_start(layer, p, buf)

    def backward_layer(layer, buf, between):
        phase = 3 - layer
        for k in range(1, 4):
            g_arrival(layer, k).wait_recv()
        grad_part(layer, 2, buf)

        @pl.loop(0, 4)
        def _(c):
            rows = pl.ds(pl.multiple_of(c * chunk, chunk), chunk)
            g = gb[layer, rows, :]
            for j in range(width // 256):
                cols = slice(j * 256, (j + 1) * 256)
                d = mm(g, w[layer, 2, :, cols], NN) * slope[layer, rows, cols].astype(F32)
                sm[layer, 6:7, cols] = sm[layer, 6:7, cols] + jnp.sum(d, axis=0, keepdims=True)
                du[rows, cols] = d.astype(BF)
            d = pltpu.roll(mm(g, w[layer, 0, :, 512:768], NN), HL - 64, 1)
            lane = lane_iota(chunk)
            dc[rows, :] = jnp.where(lane < heads * HEAD_DIM, d, 0.0).astype(BF)
            dk[rows, :] = jnp.zeros((chunk, HL), F32)
            dv[rows, :] = jnp.zeros((chunk, HL), F32)

        grad_part(layer, 1, buf)
        between(2)

        @pl.loop(0, nblk)
        def _(b):
            q0 = pl.multiple_of(b * BQ, BQ)
            k0 = pl.multiple_of(jnp.maximum(b * BQ - SEG_MOST, 0), BQ)
            qm = stack_heads(qb[layer, pl.ds(q0, BQ), :])
            dm = stack_heads(dc[pl.ds(q0, BQ), :])
            ls = lse[layer, b]
            total = None
            for i in range(BK // BQ):
                krows = pl.ds(k0 + i * BQ, BQ)
                irows = slice(i * BQ, (i + 1) * BQ)
                blk = bias[b, irows, :].astype(F32)
                sc = mm(kb[layer, krows, :], qm, NT) + jnp.concatenate([blk] * heads, axis=1)
                pr = jnp.exp(sc - ls)
                dp = mm(vb[layer, krows, :], dm, NT)
                dv[krows, :] = dv[krows, :] + mm(pr.astype(BF), dm, NN)
                pscr[irows, :] = pr
                dpscr[irows, :] = dp
                part = jnp.sum(pr * dp, axis=0, keepdims=True)
                total = part if total is None else total + part
            lane = lane_iota(BQ) >> 6
            acc = [jnp.zeros((BQ, HL), F32) for _ in range(heads)]
            for i in range(BK // BQ):
                krows = pl.ds(k0 + i * BQ, BQ)
                irows = slice(i * BQ, (i + 1) * BQ)
                ds = (pscr[irows, :] * (dpscr[irows, :] - total)).astype(BF)
                dk[krows, :] = dk[krows, :] + mm(ds, qm, NN)
                keys = kb[layer, krows, :]
                for h in range(heads):
                    acc[h] = acc[h] + mm(ds[:, h * BQ : (h + 1) * BQ], keys, TN)
            out = jnp.zeros((BQ, HL), F32)
            for h in range(heads):
                out = jnp.where(lane == h, acc[h], out)
            dq[pl.ds(q0, BQ), :] = out

        between(1)

        @pl.loop(0, 4)
        def _(c):
            rows = pl.ds(pl.multiple_of(c * chunk, chunk), chunk)
            b0 = c * (chunk // BQ)
            lane = lane_iota(chunk)
            gq = rope(dq[rows, :], b0, -1.0) * 0.125
            gk = rope(dk[rows, :], b0, -1.0)
            gv = dv[rows, :]
            sm[layer, 4:5, 0:HL] = sm[layer, 4:5, 0:HL] + jnp.sum(gq, axis=0, keepdims=True)
            sm[layer, 5:6, 0:HL] = sm[layer, 5:6, 0:HL] + jnp.sum(gv, axis=0, keepdims=True)
            rk = pltpu.roll(gk, 192, 1)
            rv = pltpu.roll(gv, 128, 1)
            dqkv[rows, 0:256] = jnp.where(lane < 192, gq, rk).astype(BF)
            dqkv[rows, 256:512] = jnp.where(lane < 128, rk, rv).astype(BF)
            dqkv[rows, 512:768] = jnp.where(lane < 64, rv, 0.0).astype(BF)

        for k in range(1, 4):
            part_copy(1 if layer == 1 else 2, k).wait_send()
        for k in (1, 2, 3, 0):
            rows = pl.ds(pl.multiple_of((t ^ k) * chunk, chunk), chunk)
            da_in = dqkv[rows, :]
            du_in = du[rows, :]
            m = mu[layer, rows, :]
            r = rstd[layer, rows, :]
            for j in range(width // 256):
                cols = slice(j * 256, (j + 1) * 256)
                da = mm(da_in, w[layer, 0, cols, :], NT)
                dm = mm(du_in, w[layer, 1, cols, :], NT)
                unit = (x[layer, rows, cols].astype(F32) - m) * r
                sums = [da * unit, dm * unit, da, dm]
                for i in range(4):
                    sm[layer, i : i + 1, cols] = sm[layer, i : i + 1, cols] + jnp.sum(
                        sums[i], axis=0, keepdims=True
                    )
                e = da * prow(layer, 0, cols) + dm * prow(layer, 1, cols)
                if k:
                    sendb[k - 1, :, cols] = e.astype(BF)
                else:
                    ownp[phase % 2, :, cols] = e
            if k:
                part_copy(phase, k).start()
        grad_part(layer, 0, buf)

    def finish_e(layer):
        phase = 3 - layer
        for k in range(1, 4):
            part_copy(phase, k).wait_recv()
        stage = gst.at[1 - layer]
        given = cotv if layer == 1 else gst.at[0]
        resid = jnp.zeros((1, width), F32)

        @pl.loop(0, chunk // sub)
        def _(i):
            r = pl.ds(pl.multiple_of(i * sub, sub), sub)
            rows = pl.ds(pl.multiple_of(t * chunk + i * sub, sub), sub)
            e = ownp[phase % 2, r, :]
            for k in range(3):
                e = e + recvb[phase % 2, k, r, :].astype(F32)
            rs = rstd[layer, rows, :]
            unit = (x[layer, rows, :].astype(F32) - mu[layer, rows, :]) * rs
            g = given[r, :]
            sm[layer, 7:8, :] = sm[layer, 7:8, :] + jnp.sum(g, axis=0, keepdims=True)
            d = rs * (
                e
                - jnp.mean(e, axis=-1, keepdims=True)
                - unit * jnp.mean(e * unit, axis=-1, keepdims=True)
            )
            g = g + d
            stage[r, :] = g
            if layer == 1:
                gb[0, rows, :] = g.astype(BF)

        if layer == 1:
            for k in range(1, 4):
                g_copy(0, k).start()
        place(layer, stage, out_g, 2 + layer)

    forward_layer(0)
    finish_y(0)
    forward_layer(1)
    backward_layer(1, gw, lambda p: None)
    finish_y(1)
    finish_e(1)
    renorm_all(0)
    for p in (2, 1, 0):
        reduce_cores(1, p, gw)
    late = w.at[1]
    for p in range(3):
        for j in range(1, n):
            w_copy(p, j).wait_send()

        @pl.when(s == 0)
        def _():
            forward(0, p).wait_send()

        @pl.when(s == 1)
        def _():
            forward(1, p).wait_send()

    backward_layer(0, late, lambda p: reduce_cores(0, p, late))
    finish_e(0)

    to_sib = remote(sm.at[1 - s], smr, sms.at[0], smrs.at[0], sib)
    to_sib.start()
    to_sib.wait()
    smt[...] = sm[s] + smr[...]
    for j in range(1, n):
        remote(
            smt, smz.at[j - 1], sms.at[j], smrs.at[j], (s, other_z(j), t)
        ).start()
    reduce_cores(0, 0, late)
    for j in range(1, n):
        remote(smt, smz.at[j - 1], sms.at[j], smrs.at[j], (s, other_z(j), t)).wait()
    total = smt[...]
    for j in range(1, n):
        total = total + smz[j - 1]
    tall[t] = total

    def small_copy(k):
        return remote(tall.at[t], tall.at[t], sms.at[n + k - 1], smrs.at[n + k - 1], plane(k))

    for k in range(1, 4):
        small_copy(k).start()

    for p in (2, 1, 0):
        for j in range(1, n):
            z_copy(p, j, late).wait_recv()

            @pl.loop(0, rows_z // step)
            def _(i):
                r = pl.ds(pl.multiple_of(i * step, 16), step)
                wacc[p, r, :] = wacc[p, r, :] + zrecv[p, j - 1, r, :].astype(F32)

        pltpu.make_async_copy(wacc.at[p], out_w.at[p], lsem.at[p]).start()
    for k in range(1, 4):
        small_copy(k).wait_send()
        remote(
            tall.at[t ^ k], tall.at[t ^ k], sms.at[n + k - 1], smrs.at[n + k - 1], plane(k)
        ).wait_recv()
    out_s[...] = tall[...]

    for p in range(3):
        pltpu.make_async_copy(wacc.at[p], out_w.at[p], lsem.at[p]).wait()
        for j in range(1, n):
            z_copy(p, j, late).wait_send()

    for k in range(1, 4):
        for layer in range(2):
            x_copy(layer, k).wait_send()
            g_copy(layer, k).wait_send()
        part_copy(3, k).wait_send()
    placed(1, yst, out_y, 1)
    placed(1, gst.at[0], out_g, 3)
    placed(0, gst.at[1], out_g, 2)
    remote(yst, out_y.at[1 - s], osend.at[0], orecv.at[0], sib).wait_recv()
    remote(gst.at[0], out_g.at[1 - s], osend.at[0], orecv.at[1], sib).wait_recv()


def rotary_rows(length, heads):
    rate = np.zeros((HL,), np.float64)
    for h in range(heads):
        for j in range(ROT // 2):
            value = math.exp(j * (-2.0 * math.log(10000.0) / ROT))
            rate[h * HEAD_DIM + j] = value
            rate[h * HEAD_DIM + j + ROT // 2] = value
    live = (np.arange(HL) < heads * HEAD_DIM).astype(np.float64)
    starts = np.arange(length // BQ)[:, None] * BQ * rate[None]
    offsets = np.arange(BQ)[:, None] * rate[None]
    first = np.stack([np.cos(starts), np.sin(starts)])[:, :, None].astype(np.float32)
    second = np.stack([np.cos(offsets) * live, np.sin(offsets) * live]).astype(np.float32)
    return first, second


def body(
    n,
    inputs,
    segment_ids,
    cotangent,
    qkv_weight,
    out_weight,
    up_weight,
    down_weight,
    norm_gain,
    norm_bias,
    qv_bias,
    up_bias,
    resid_bias,
):
    column = lax.axis_index("tensor")
    micro, _, chunk, width = inputs.shape
    length = segment_ids.shape[2]
    head_cols = qkv_weight.shape[3]
    rows_z = qkv_weight.shape[2]
    ff_local = up_weight.shape[2]
    heads = head_cols // HEAD_DIM
    assert micro == 2 and length == 4 * chunk and ff_local == width
    assert head_cols == 192 and width == 768

    packed = jnp.concatenate(
        [qkv_weight[0, 0], qkv_weight[0, 1], qkv_weight[0, 2], out_weight[0].T], axis=1
    )
    w_in = jnp.stack([packed, up_weight[0], down_weight[0].T])
    qv_local = lax.dynamic_slice_in_dim(qv_bias[0], column * head_cols, head_cols, 1)
    qv_local = jnp.pad(qv_local, ((0, 0), (0, width - head_cols)))
    up_local = lax.dynamic_slice_in_dim(up_bias, column * ff_local, ff_local, 1)
    par_in = jnp.concatenate([norm_gain[0], norm_bias[0], qv_local, up_local, resid_bias], axis=0)
    first, second = rotary_rows(length, heads)
    seg = segment_ids.reshape(micro, length)

    vm = pl.BlockSpec(memory_space=pltpu.VMEM)
    anywhere = pl.BlockSpec(memory_space=pl.ANY)
    blk = heads * BQ
    nblk = length // BQ
    dma = pltpu.SemaphoreType.DMA

    def vmem(*shape, dtype=BF):
        return pltpu.VMEM(shape, dtype)

    scratch = dict(
        w=vmem(2, 3, width, width),
        x=vmem(2, length, width),
        an=vmem(length, width),
        mn=vmem(length, width),
        mu=vmem(2, length, 1, dtype=F32),
        rstd=vmem(2, length, 1, dtype=F32),
        qb=vmem(2, length, HL),
        kb=vmem(2, length, HL),
        vb=vmem(2, length, HL),
        cb=vmem(2, length, HL),
        lse=vmem(2, nblk, 1, blk, dtype=F32),
        slope=vmem(2, length, width),
        hid=vmem(2, length, width),
        gb=vmem(2, length, width),
        du=vmem(length, width),
        dqkv=vmem(length, width),
        dc=vmem(length, HL),
        dq=vmem(length, HL, dtype=F32),
        dk=vmem(length, HL, dtype=F32),
        dv=vmem(length, HL, dtype=F32),
        bias=vmem(nblk, BK, BQ),
        pscr=vmem(BK, blk, dtype=F32),
        dpscr=vmem(BK, blk, dtype=F32),
        sendb=vmem(3, chunk, width),
        recvb=vmem(2, 3, chunk, width),
        ownp=vmem(2, chunk, width, dtype=F32),
        gw=vmem(3, width, width),
        gsr=vmem(3, width, width),
        zrecv=vmem(3, n - 1, rows_z, width),
        wacc=vmem(3, rows_z, width, dtype=F32),
        cotv=vmem(chunk, width, dtype=F32),
        yst=vmem(chunk, width, dtype=F32),
        gst=vmem(2, chunk, width, dtype=F32),
        segc=vmem(length, 1, dtype=jnp.int32),
        par=vmem(2, 8, width, dtype=F32),
        sm=vmem(2, 8, width, dtype=F32),
        smr=vmem(8, width, dtype=F32),
        smt=vmem(8, width, dtype=F32),
        smz=vmem(n - 1, 8, width, dtype=F32),
        tall=vmem(4, 8, width, dtype=F32),
        lsem=dma((8,)),
        psem=dma((2,)),
        xs=dma((2, 3)),
        xr=dma((2, 3)),
        gs=dma((2, 3)),
        gr=dma((2, 3)),
        ws=dma((3, n - 1)),
        wr=dma((3, n - 1)),
        fs=dma((3,)),
        fr=dma((3,)),
        rss=dma((4, 3)),
        rsr=dma((4, 3)),
        osend=dma((4,)),
        orecv=dma((2,)),
        ghs=dma((3,)),
        ghr=dma((3,)),
        zs=dma((3, n - 1)),
        zr=dma((3, n - 1)),
        sms=dma((n + 3,)),
        smrs=dma((n + 3,)),
    )
    out_y, out_g, out_w, out_s = pl.pallas_call(
        functools.partial(kernel, n, heads),
        out_shape=(
            jax.ShapeDtypeStruct((2, chunk, width), F32),
            jax.ShapeDtypeStruct((2, chunk, width), F32),
            jax.ShapeDtypeStruct((3, rows_z, width), F32),
            jax.ShapeDtypeStruct((4, 8, width), F32),
        ),
        in_specs=[anywhere, anywhere, anywhere, vm, anywhere, anywhere, vm, vm],
        out_specs=(anywhere, anywhere, anywhere, vm),
        scratch_shapes=list(scratch.values()),
        compiler_params=pltpu.CompilerParams(
            collective_id=0, has_side_effects=True, vmem_limit_bytes=67043328
        ),
        name="two_layers",
    )(
        inputs.reshape(micro, chunk, width),
        cotangent.reshape(micro, chunk, width),
        seg[:, :, None],
        seg,
        w_in,
        par_in,
        jnp.asarray(first),
        jnp.asarray(second),
    )
    qkv_grad = jnp.stack([out_w[0, :, i * head_cols : (i + 1) * head_cols] for i in range(3)])
    sums = jnp.sum(out_s, axis=0)
    return (
        out_y.reshape(1, micro, 1, chunk, width),
        out_g.reshape(1, micro, 1, chunk, width),
        qkv_grad[None],
        out_w[0, :, 3 * head_cols :].T[None],
        out_w[1][None],
        out_w[2].T[None],
        sums[None, 0:2],
        sums[None, 2:4],
        out_s[:, 4:6, :head_cols].transpose(1, 0, 2).reshape(1, 2, -1),
        out_s[:, 6, :].reshape(1, -1),
        sums[None, 7],
    )


def solution(mesh):
    return jax.shard_map(
        functools.partial(body, mesh.shape["dp"]),
        mesh=mesh,
        in_specs=(
            P(None, "dp", "tensor", None),
            P(None, "dp", None),
            P(None, "dp", "tensor", None),
            P("section", None, "dp", "tensor"),
            P("section", "tensor", "dp"),
            P("section", "dp", "tensor"),
            P("section", "tensor", "dp"),
            P("section", None, None),
            P("section", None, None),
            P("section", None, None),
            P("section", None),
            P("section", None),
        ),
        out_specs=(
            P("section", None, "dp", "tensor", None),
            P("section", None, "dp", "tensor", None),
            P("section", None, "dp", "tensor"),
            P("section", "tensor", "dp"),
            P("section", "dp", "tensor"),
            P("section", "tensor", "dp"),
            P("section", None, None),
            P("section", None, None),
            P("section", None, None),
            P("section", None),
            P("section", None),
        ),
        check_vma=False,
    )
```

time: 1110 us -> 268 us (0.24)
  the two profiles are of different devices: /device:TPU:0 before, /device:TPU:24 now
where the time goes in v1:
time: 268 us; the launch traced here: 267 us
  Pallas kernels  242 us (90%)
  local copies, waits for them, and re-layouts  19.8 us (7%)
  other arithmetic  4.65 us (2%)
    pallas_call x1, Pallas kernels, body(): pl.pallas_call(functools.partial(kernel, n, heads), out_shape=(jax.ShapeD...  242 us
    unnamed x15, local copies, waits for them, and re-layouts  7.14 us

profile of v1, /device:TPU:24, one launch (start us, length us, event | category | flops | bytes accessed | tf_op | source)
XLA Modules:
  0.0 267.2 jit_solution(11839859565671710712)
XLA Ops:
  0.6 0.0 copy-start.3
  0.7 0.0 copy-start.4
  0.7 0.8 dynamic-slice_bitcast_fusion
  1.5 0.7 constant_dynamic-slice_fusion
  2.2 1.3 copy.37
  3.5 0.7 reduce
  4.2 1.4 concatenate.7.par_in
  5.6 1.0 copy.29
  6.6 1.0 slice_bitcast_fusion.4
  7.6 0.1 maximum_bitcast_fusion.1
  7.7 0.0 copy-done.3
  7.7 0.0 copy-done.4
  7.7 1.0 pad_maximum_fusion.w_in
  8.7 1.3 broadcast_in_dim_reshape.4.segc_in
  10.1 242.0 %two_layers.1 = (f32[2,256,768]{2,1,0:T(8,128)}, f32[2,256,768]{2,1,0:T(8,128)}, f32[3,192,768]{2,1,0:T(8,128)}, f32[4,8,768]{2,1,0:T(8,128)}) custom-call(bf16[2,256,768]{2,1,0:T(8,128)(2,1)} %bitcast.55, f32[2,256,768]{2,1,0:T(8,128)} %bitcast.54, s32[2,1024,1]{2,1,0:T(8,128)} %broadcast_in_dim_reshape.4.segc_in, s32[2,1024]{1,0:T(2,128)} %bitcast.58, ...), custom_call_target="tpu_custom_call" | custom-call | tf_op jit(solution)/shard_map/two_layers/pallas_call | solution.py:859
  252.0 0.0 copy-start
  252.0 0.9 slice_bitcast_fusion.5
  252.9 0.7 reshape.46
  253.6 1.5 slice.54
  255.1 0.9 reduce_sum.9
  256.0 0.6 slice.58
  256.6 0.6 slice_bitcast_fusion.6
  257.2 2.2 slice_bitcast_fusion.1
  259.4 0.0 copy-done
  259.4 0.0 copy-start.2
  259.4 1.1 slice_bitcast_fusion
  260.5 1.7 copy.34
  262.2 1.9 maximum_bitcast_fusion
  264.1 0.0 copy-done.2
  264.1 0.0 copy-start.1
  264.1 1.1 copy.40
  265.2 0.8 copy-done.1
  266.0 1.1 copy.41
  (2 shorter events, 0.0 us)
Async XLA Ops:
  0.6 7.1 %copy-start.3 = (bf16[1,768,192]{1,2,0:T(8,128)(2,1)S(1)}, bf16[1,768,192]{1,2,0:T(8,128)(2,1)}, u32[]{:S(2)}) copy-start(bf16[1,768,192]{1,2,0:T(8,128)(2,1)} %param.20) | copy-start | bytes 884740
  0.7 7.1 %copy-start.4 = (bf16[1,192,768]{2,1,0:T(8,128)(2,1)S(1)}, bf16[1,192,768]{2,1,0:T(8,128)(2,1)}, u32[]{:S(2)}) copy-start(bf16[1,192,768]{2,1,0:T(8,128)(2,1)} %param.19) | copy-start | bytes 884740
  252.0 7.4 %copy-start = (f32[3,192,768]{2,1,0:T(8,128)S(1)}, f32[3,192,768]{2,1,0:T(8,128)}, u32[]{:S(2)}) copy-start(f32[3,192,768]{2,1,0:T(8,128)} %get-tuple-element.17) | copy-start | bytes 5308420
  259.4 4.7 %copy-start.2 = (f32[2,256,768]{2,1,0:T(8,128)S(1)}, f32[2,256,768]{2,1,0:T(8,128)}, u32[]{:S(2)}) copy-start(f32[2,256,768]{2,1,0:T(8,128)} %get-tuple-element.15) | copy-start | bytes 4718596
  264.1 2.0 copy-start.1

commit v2 on v1

--- a/solution.py
+++ b/solution.py
@@ -50,10 +50,16 @@
     heads,
     x_in,
     cot_in,
-    segc_in,
-    segr_in,
-    w_in,
-    par_in,
+    seg_in,
+    qkv_in,
+    wo_in,
+    up_in,
+    down_in,
+    gain_in,
+    shift_in,
+    qv_in,
+    upb_in,
+    resid_in,
     taba,
     tabb,
     out_y,
@@ -85,6 +91,7 @@
     dpscr,
     sendb,
     recvb,
+    relayed,
     ownp,
     gw,
     gsr,
@@ -94,6 +101,7 @@
     yst,
     gst,
     segc,
+    segr,
     par,
     sm,
     smr,
@@ -104,6 +112,10 @@
     psem,
     xs,
     xr,
+    agx,
+    agxr,
+    agg,
+    aggr,
     gs,
     gr,
     ws,
@@ -128,7 +140,8 @@
     width = x.shape[2]
     length = x.shape[1]
     chunk = length // 4
-    rows_z = w_in.shape[1]
+    rows_z = up_in.shape[1]
+    half = chunk // 2
     nblk = length // BQ
     own = pl.ds(t * chunk, chunk)
     zrows = pl.ds(z * rows_z, rows_z)
@@ -141,17 +154,35 @@
 
     lx = pltpu.make_async_copy(x_in.at[s], x.at[0, own], lsem.at[0])
     lc = pltpu.make_async_copy(cot_in.at[s], cotv, lsem.at[1])
-    lw = [
-        pltpu.make_async_copy(w_in.at[p], w.at[s, p, zrows], lsem.at[2 + p]) for p in range(3)
-    ]
-    lseg = pltpu.make_async_copy(segc_in.at[s], segc, lsem.at[5])
-    lpar = pltpu.make_async_copy(par_in, par.at[s], lsem.at[6])
+    lu = pltpu.make_async_copy(up_in.at[0], w.at[s, 1, zrows], lsem.at[3])
+    ld = pltpu.make_async_copy(down_in, w.at[s, 2, zrows], lsem.at[4])
     lx.start()
-    for p in range(3):
-        lw[p].start()
-    lpar.start()
+    lu.start()
+    ld.start()
     lc.start()
-    lseg.start()
+
+    head_cols = heads * HEAD_DIM
+
+    def picks(first):
+        rows = lax.broadcasted_iota(jnp.int32, (head_cols, width), 0)
+        cols = lax.broadcasted_iota(jnp.int32, (head_cols, width), 1)
+        return (rows + first == cols).astype(F32).astype(BF)
+
+    packed = mm(qkv_in[0, 0], picks(QO), NN) + mm(qkv_in[0, 1], picks(KO), NN)
+    packed = packed + mm(qkv_in[0, 2], picks(VO), NN) + mm(wo_in[0], picks(OO), TN)
+    w[s, 0, zrows, :] = packed.astype(BF)
+
+    par[s, 0:2, :] = gain_in[0]
+    par[s, 2:4, :] = shift_in[0]
+    par[s, 4:6, :] = qv_in[0]
+    par[s, 6:7, :] = upb_in[0:1, pl.ds(pl.multiple_of(t * width, 128), width)]
+    par[s, 7:8, :] = resid_in[...]
+    rows8 = par[s]
+    turned = rows8
+    for i in range(1, 4):
+        turned = jnp.where(t == i, pltpu.roll(rows8, width - i * head_cols, 1), turned)
+    row = lax.broadcasted_iota(jnp.int32, (8, width), 0)
+    par[s] = jnp.where((row == 4) | (row == 5), turned, rows8)
 
     barrier = pltpu.get_barrier_semaphore()
     pl.semaphore_signal(barrier, inc=1, device_id=sib, device_id_type=MESH)
@@ -161,93 +192,171 @@
         pl.semaphore_signal(barrier, inc=1, device_id=(s, other_z(j), t), device_id_type=MESH)
     pl.semaphore_wait(barrier, 4 + n - 1)
 
+    right = (s, lax.rem(z + 1, n), t)
+    left = (s, lax.rem(z + n - 1, n), t)
+
+    def w_rows(origin):
+        return pl.ds(origin * rows_z, rows_z)
+
+    def line_copy(p, origin, dev):
+        up = dev is right
+        i = 0 if up else 1
+        return remote(
+            w.at[0, p, w_rows(origin)],
+            w.at[0, p, w_rows(origin)],
+            ws.at[i, p, origin],
+            wr.at[i, p, origin],
+            dev,
+        )
+
+    def across(p, origin):
+        rows = w_rows(origin)
+        return remote(w.at[0, p, rows], w.at[0, p, rows], fs.at[p, origin], fr.at[p, origin], sib)
+
     def w_copy(p, j):
         return remote(
-            w.at[s, p, zrows],
-            w.at[s, p, zrows],
-            ws.at[p, j - 1],
-            wr.at[p, j - 1],
+            w.at[1, p, zrows],
+            w.at[1, p, zrows],
+            ws.at[0, p, j - 1],
+            wr.at[0, p, j - 1],
             (s, other_z(j), t),
         )
 
     def w_arrival(p, j):
-        rows = pl.ds(other_z(n - j) * rows_z, rows_z)
+        rows = w_rows(other_z(n - j))
         return remote(
-            w.at[s, p, rows], w.at[s, p, rows], ws.at[p, j - 1], wr.at[p, j - 1], (s, z, t ^ 1)
+            w.at[1, p, rows], w.at[1, p, rows], ws.at[0, p, j - 1], wr.at[0, p, j - 1], sib
         )
 
-    def forward(layer, p):
-        return remote(w.at[layer, p], w.at[layer, p], fs.at[p], fr.at[p], sib)
-
-    def x_copy(layer, k):
-        return remote(
-            x.at[layer, own], x.at[layer, own], xs.at[layer, k - 1], xr.at[layer, k - 1], plane(k)
-        )
-
-    def x_arrival(layer, k):
+    def forward(p):
+        return remote(w.at[1, p], w.at[1, p], fs.at[p, 0], fr.at[p, 0], sib)
+
+    def x_copy(k):
+        return remote(x.at[0, own], x.at[0, own], xs.at[k - 1], xr.at[k - 1], plane(k))
+
+    def x_arrival(k):
         rows = pl.ds((t ^ k) * chunk, chunk)
-        return remote(
-            x.at[layer, rows],
-            x.at[layer, rows],
-            xs.at[layer, k - 1],
-            xr.at[layer, k - 1],
-            plane(k),
-        )
-
-    def g_copy(layer, k):
-        return remote(
-            gb.at[layer, own], gb.at[layer, own], gs.at[layer, k - 1], gr.at[layer, k - 1], plane(k)
-        )
-
-    def g_arrival(layer, k):
+        return remote(x.at[0, rows], x.at[0, rows], xs.at[k - 1], xr.at[k - 1], plane(k))
+
+    def g_copy(k):
+        return remote(gb.at[1, own], gb.at[1, own], gs.at[k - 1], gr.at[k - 1], plane(k))
+
+    def g_arrival(k):
         rows = pl.ds((t ^ k) * chunk, chunk)
-        return remote(
-            gb.at[layer, rows],
-            gb.at[layer, rows],
-            gs.at[layer, k - 1],
-            gr.at[layer, k - 1],
-            plane(k),
-        )
-
-    def part_copy(phase, k):
-        return remote(
-            sendb.at[k - 1],
-            recvb.at[phase % 2, k - 1],
-            rss.at[phase, k - 1],
-            rsr.at[phase, k - 1],
-            plane(k),
-        )
+        return remote(gb.at[1, rows], gb.at[1, rows], gs.at[k - 1], gr.at[k - 1], plane(k))
+
+    hops = ((0, 0, 1), (0, 1, 2), (0, 1, 1), (0, 0, 2), (1, 0, 2), (2, 1, 1))
+
+    def gather_copy(buf, send, recv, i):
+        k, h, to = hops[i]
+        rows = pl.ds((t ^ k) * chunk + h * half, half)
+        return remote(buf.at[rows], buf.at[rows], send.at[i], recv.at[i], plane(to))
+
+    def gather_arrival(buf, send, recv, i):
+        k, h, to = hops[i]
+        rows = pl.ds((t ^ k ^ to) * chunk + h * half, half)
+        return remote(buf.at[rows], buf.at[rows], send.at[i], recv.at[i], plane(to))
+
+    def gather_start(buf, send, recv):
+        for i in range(4):
+            gather_copy(buf, send, recv, i).start()
+
+    def gather_pass(buf, send, recv):
+        gather_arrival(buf, send, recv, 0).wait_recv()
+        gather_copy(buf, send, recv, 4).start()
+        gather_arrival(buf, send, recv, 1).wait_recv()
+        gather_copy(buf, send, recv, 5).start()
+
+    def gather_wait(buf, send, recv, k):
+        for i in {1: (2,), 2: (3,), 3: (4, 5)}[k]:
+            gather_arrival(buf, send, recv, i).wait_recv()
+
+    def arrive(buf, send, recv, k):
+        for i in range(1, 4):
+
+            @pl.when(k == i)
+            def _():
+                gather_wait(buf, send, recv, i)
+
+    def part_copy(phase, i):
+        low, high = pl.ds(0, half), pl.ds(half, half)
+        bank = phase % 2
+        src, dst, to = (
+            (sendb.at[2, low], relayed.at[bank, 0], 1),
+            (sendb.at[2, high], relayed.at[bank, 1], 2),
+            (sendb.at[0, low], recvb.at[bank, 0, low], 1),
+            (sendb.at[1, high], recvb.at[bank, 1, high], 2),
+            (sendb.at[1, low], recvb.at[bank, 1, low], 2),
+            (sendb.at[0, high], recvb.at[bank, 0, high], 1),
+        )[i]
+        return remote(src, dst, rss.at[phase, i], rsr.at[phase, i], plane(to))
+
+    def parts_start(phase, k):
+        for i in {3: (0, 1), 1: (2,), 2: (3,)}[k]:
+            part_copy(phase, i).start()
+
+    def parts_pass(phase):
+        for i in range(2):
+            part_copy(phase, i).wait_recv()
+            rows = slice(i * half, (i + 1) * half)
+            mine = sendb[1 - i, rows, :].astype(F32)
+            sendb[1 - i, rows, :] = (mine + relayed[phase % 2, i].astype(F32)).astype(BF)
+            part_copy(phase, 4 + i).start()
+
+    def parts_sent(phase):
+        for i in range(6):
+            part_copy(phase, i).wait_send()
+
+    def parts_wait(phase):
+        for i in range(2, 6):
+            part_copy(phase, i).wait_recv()
+
+    ag_x = (x.at[1], agx, agxr)
+    ag_g = (gb.at[0], agg, aggr)
+
+    def send_own(p):
+        @pl.when(z + 1 < n)
+        def _():
+            line_copy(p, z, right).start()
+
+        @pl.when(z > 0)
+        def _():
+            line_copy(p, z, left).start()
+
+    @pl.when(s == 0)
+    def _():
+        send_own(0)
 
     lx.wait()
     for k in range(1, 4):
-        x_copy(0, k).start()
-    lpar.wait()
+        x_copy(k).start()
     par_copy = remote(par.at[s], par.at[s], psem.at[0], psem.at[1], sib)
     par_copy.start()
-    for p in range(3):
-        lw[p].wait()
+    lu.wait()
+    ld.wait()
 
     @pl.when(s == 0)
     def _():
         for p in range(3):
-            for j in range(1, n):
-                w_copy(p, j).start()
+            across(p, z).start()
 
     lc.wait()
     gb[1, own, :] = cotv[...].astype(BF)
     for k in range(1, 4):
-        g_copy(1, k).start()
-
-    lseg.wait()
+        g_copy(k).start()
+
+    for i in range(length // BQ):
+        cols = slice(i * BQ, (i + 1) * BQ)
+        ids = jnp.where(s == 0, seg_in[0, :, cols], seg_in[1, :, cols]).astype(F32)
+        segr[:, cols] = ids
+        segc[cols, :] = jnp.broadcast_to(ids, (BQ, BQ)).T
 
     @pl.loop(0, nblk)
     def _(b):
         q0 = pl.multiple_of(b * BQ, BQ)
         k0 = pl.multiple_of(jnp.maximum(b * BQ - SEG_MOST, 0), BQ)
         seg_k = segc[pl.ds(k0, BK), :]
-        seg_q = jnp.where(
-            s == 0, segr_in[0:1, pl.ds(q0, BQ)], segr_in[1:2, pl.ds(q0, BQ)]
-        )
+        seg_q = segr[:, pl.ds(q0, BQ)]
         kpos = lax.broadcasted_iota(jnp.int32, (BK, BQ), 0) + k0
         qpos = lax.broadcasted_iota(jnp.int32, (BK, BQ), 1) + q0
         allowed = (seg_k == seg_q) & (kpos <= qpos)
@@ -261,19 +370,83 @@
     def _(i):
         sm[i] = jnp.zeros((8, width), F32)
 
-    def need_w(layer, p):
-        @pl.when(s == layer)
+    def first_w(p):
+        @pl.when(s == 0)
+        def _():
+            for d in range(1, n):
+
+                @pl.when(z >= d)
+                def _():
+                    origin = jnp.maximum(z - d, 0)
+                    line_copy(p, origin, right).wait_recv()
+
+                    @pl.when(z + 1 < n)
+                    def _():
+                        line_copy(p, origin, right).start()
+
+                    across(p, origin).start()
+
+                @pl.when(z + d < n)
+                def _():
+                    origin = jnp.minimum(z + d, n - 1)
+                    line_copy(p, origin, left).wait_recv()
+
+                    @pl.when(z > 0)
+                    def _():
+                        line_copy(p, origin, left).start()
+
+                    across(p, origin).start()
+
+                if d == 1 and p < 2:
+                    send_own(p + 1)
+
+        @pl.when(s == 1)
+        def _():
+            for origin in range(n):
+                across(p, origin).wait_recv()
+
+    def first_w_sent():
+        @pl.when(s == 0)
+        def _():
+            for p in range(3):
+                for origin in range(n):
+
+                    @pl.when((z >= origin) & (z + 1 < n))
+                    def _():
+                        line_copy(p, origin, right).wait_send()
+
+                    @pl.when((z <= origin) & (z > 0))
+                    def _():
+                        line_copy(p, origin, left).wait_send()
+
+                    across(p, origin).wait_send()
+
+    def second_w_send():
+        @pl.when(s == 1)
+        def _():
+            for p in range(3):
+                for j in range(1, n):
+                    w_copy(p, j).start()
+
+    def second_w_pass(p):
+        @pl.when(s == 1)
         def _():
             for j in range(1, n):
                 w_arrival(p, j).wait_recv()
-            forward(layer, p).start()
-
-        @pl.when(s != layer)
-        def _():
-            forward(layer, p).wait_recv()
-            if layer == 0:
+            forward(p).start()
+
+    def second_w_wait(p):
+        @pl.when(s == 0)
+        def _():
+            forward(p).wait_recv()
+
+    def second_w_sent():
+        @pl.when(s == 1)
+        def _():
+            for p in range(3):
                 for j in range(1, n):
-                    w_copy(p, j).start()
+                    w_copy(p, j).wait_send()
+                forward(p).wait_send()
 
     def prow(layer, r, cols=None):
         if cols is None:
@@ -334,27 +507,19 @@
             an[rows, :] = (v * prow(layer, 0) + prow(layer, 2)).astype(BF)
             mn[rows, :] = (v * prow(layer, 1) + prow(layer, 3)).astype(BF)
 
-    def forward_layer(layer):
-        phase = layer
-        norm_chunk(layer, t)
-        for k in range(1, 4):
-            x_arrival(layer, k).wait_recv()
-            norm_chunk(layer, t ^ k)
-        need_w(layer, 0)
-
-        @pl.loop(0, 4)
-        def _(c):
-            rows = pl.ds(pl.multiple_of(c * chunk, chunk), chunk)
-            a = an[rows, :]
-            b0 = c * (chunk // BQ)
-            lane = lane_iota(chunk)
-            u = mm(a, w[layer, 0, :, QO : QO + HL], NN) + prow(layer, 4, slice(0, HL))
-            qb[layer, rows, :] = (rope(u, b0, 1.0) * 0.125).astype(BF)
-            u = mm(a, w[layer, 0, :, KO - 64 : KO - 64 + HL], NN)
-            kb[layer, rows, :] = rope(pltpu.roll(u, HL - 64, 1), b0, 1.0).astype(BF)
-            u = mm(a, w[layer, 0, :, VO : VO + HL], NN) + prow(layer, 5, slice(0, HL))
-            vb[layer, rows, :] = jnp.where(lane < heads * HEAD_DIM, u, 0.0).astype(BF)
-
+    def project_in(layer, c):
+        rows = pl.ds(pl.multiple_of(c * chunk, chunk), chunk)
+        a = an[rows, :]
+        b0 = c * (chunk // BQ)
+        lane = lane_iota(chunk)
+        u = mm(a, w[layer, 0, :, QO : QO + HL], NN) + prow(layer, 4, slice(0, HL))
+        qb[layer, rows, :] = (rope(u, b0, 1.0) * 0.125).astype(BF)
+        u = mm(a, w[layer, 0, :, KO - 64 : KO - 64 + HL], NN)
+        kb[layer, rows, :] = rope(pltpu.roll(u, HL - 64, 1), b0, 1.0).astype(BF)
+        u = mm(a, w[layer, 0, :, VO : VO + HL], NN) + prow(layer, 5, slice(0, HL))
+        vb[layer, rows, :] = jnp.where(lane < heads * HEAD_DIM, u, 0.0).astype(BF)
+
+    def attend(layer):
         @pl.loop(0, nblk)
         def _(b):
             q0 = pl.multiple_of(b * BQ, BQ)
@@ -385,26 +550,21 @@
                 ctx = jnp.where(lane == h, mm(ph, vals, TN), ctx)
             cb[layer, pl.ds(q0, BQ), :] = pltpu.roll(ctx, HL - heads * HEAD_DIM, 1).astype(BF)
 
-        need_w(layer, 1)
-
-        @pl.loop(0, 4)
-        def _(c):
-            rows = pl.ds(pl.multiple_of(c * chunk, chunk), chunk)
-            a = mn[rows, :]
-            for j in range(width // 256):
-                cols = slice(j * 256, (j + 1) * 256)
-                u = mm(a, w[layer, 1, :, cols], NN) + prow(layer, 6, cols)
-                phi = 0.5 * (1.0 + lax.erf(u * ROOT_HALF))
-                hid[layer, rows, cols] = (u * phi).astype(BF)
-                slope[layer, rows, cols] = (
-                    phi + u * INV_ROOT_TAU * jnp.exp(-0.5 * u * u)
-                ).astype(BF)
-
-        need_w(layer, 2)
+    def hidden(layer, c):
+        rows = pl.ds(pl.multiple_of(c * chunk, chunk), chunk)
+        a = mn[rows, :]
+        for j in range(width // 256):
+            cols = slice(j * 256, (j + 1) * 256)
+            u = mm(a, w[layer, 1, :, cols], NN) + prow(layer, 6, cols)
+            phi = 0.5 * (1.0 + lax.erf(u * ROOT_HALF))
+            hid[layer, rows, cols] = (u * phi).astype(BF)
+            slope[layer, rows, cols] = (phi + u * INV_ROOT_TAU * jnp.exp(-0.5 * u * u)).astype(BF)
+
+    def project_out(layer):
+        phase = layer
         if layer == 1:
-            for k in range(1, 4):
-                part_copy(0, k).wait_send()
-        for k in (1, 2, 3, 0):
+            parts_sent(0)
+        for k in (3, 1, 2, 0):
             rows = pl.ds(pl.multiple_of((t ^ k) * chunk, chunk), chunk)
             c = cb[layer, rows, :]
             h = hid[layer, rows, :]
@@ -416,7 +576,7 @@
                 else:
                     ownp[phase % 2, :, cols] = y
             if k:
-                part_copy(phase, k).start()
+                parts_start(phase, k)
 
     def place(layer, stage, out, idx):
         @pl.when(s == layer)
@@ -438,8 +598,7 @@
 
     def finish_y(layer):
         phase = layer
-        for k in range(1, 4):
-            part_copy(phase, k).wait_recv()
+        parts_wait(phase)
         if layer == 1:
             placed(0, yst, out_y, 0)
 
@@ -448,15 +607,14 @@
             r = pl.ds(pl.multiple_of(i * sub, sub), sub)
             rows = pl.ds(pl.multiple_of(t * chunk + i * sub, sub), sub)
             y = x[layer, rows, :].astype(F32) + ownp[phase % 2, r, :] + prow(layer, 7)
-            for k in range(3):
+            for k in range(2):
                 y = y + recvb[phase % 2, k, r, :].astype(F32)
             yst[r, :] = y
             if layer == 0:
                 x[1, rows, :] = y.astype(BF)
 
         if layer == 0:
-            for k in range(1, 4):
-                x_copy(1, k).start()
+            gather_start(*ag_x)
         place(layer, yst, out_y, layer)
 
     def reduce_start(layer, p, buf):
@@ -515,31 +673,27 @@
                 ).astype(BF)
         reduce_start(layer, p, buf)
 
-    def backward_layer(layer, buf, between):
-        phase = 3 - layer
-        for k in range(1, 4):
-            g_arrival(layer, k).wait_recv()
-        grad_part(layer, 2, buf)
-
-        @pl.loop(0, 4)
-        def _(c):
-            rows = pl.ds(pl.multiple_of(c * chunk, chunk), chunk)
-            g = gb[layer, rows, :]
-            for j in range(width // 256):
-                cols = slice(j * 256, (j + 1) * 256)
-                d = mm(g, w[layer, 2, :, cols], NN) * slope[layer, rows, cols].astype(F32)
-                sm[layer, 6:7, cols] = sm[layer, 6:7, cols] + jnp.sum(d, axis=0, keepdims=True)
-                du[rows, cols] = d.astype(BF)
-            d = pltpu.roll(mm(g, w[layer, 0, :, 512:768], NN), HL - 64, 1)
-            lane = lane_iota(chunk)
-            dc[rows, :] = jnp.where(lane < heads * HEAD_DIM, d, 0.0).astype(BF)
-            dk[rows, :] = jnp.zeros((chunk, HL), F32)
-            dv[rows, :] = jnp.zeros((chunk, HL), F32)
-
-        grad_part(layer, 1, buf)
-        between(2)
-
-        @pl.loop(0, nblk)
+    def hidden_back(layer, c):
+        rows = pl.ds(pl.multiple_of(c * chunk, chunk), chunk)
+        g = gb[layer, rows, :]
+        for j in range(width // 256):
+            cols = slice(j * 256, (j + 1) * 256)
+            d = mm(g, w[layer, 2, :, cols], NN) * slope[layer, rows, cols].astype(F32)
+            sm[layer, 6:7, cols] = sm[layer, 6:7, cols] + jnp.sum(d, axis=0, keepdims=True)
+            du[rows, cols] = d.astype(BF)
+        d = pltpu.roll(mm(g, w[layer, 0, :, 512:768], NN), HL - 64, 1)
+        lane = lane_iota(chunk)
+        dc[rows, :] = jnp.where(lane < heads * HEAD_DIM, d, 0.0).astype(BF)
+
+    def zero_sums():
+        @pl.loop(0, length // sub)
+        def _(i):
+            rows = pl.ds(pl.multiple_of(i * sub, sub), sub)
+            dk[rows, :] = jnp.zeros((sub, HL), F32)
+            dv[rows, :] = jnp.zeros((sub, HL), F32)
+
+    def attend_back(layer, first, last):
+        @pl.loop(first, last)
         def _(b):
             q0 = pl.multiple_of(b * BQ, BQ)
             k0 = pl.multiple_of(jnp.maximum(b * BQ - SEG_MOST, 0), BQ)
@@ -574,8 +728,7 @@
                 out = jnp.where(lane == h, acc[h], out)
             dq[pl.ds(q0, BQ), :] = out
 
-        between(1)
-
+    def pack_qkv(layer):
         @pl.loop(0, 4)
         def _(c):
             rows = pl.ds(pl.multiple_of(c * chunk, chunk), chunk)
@@ -592,9 +745,10 @@
             dqkv[rows, 256:512] = jnp.where(lane < 128, rk, rv).astype(BF)
             dqkv[rows, 512:768] = jnp.where(lane < 64, rv, 0.0).astype(BF)
 
-        for k in range(1, 4):
-            part_copy(1 if layer == 1 else 2, k).wait_send()
-        for k in (1, 2, 3, 0):
+    def project_back(layer):
+        phase = 3 - layer
+        parts_sent(1 if layer == 1 else 2)
+        for k in (3, 1, 2, 0):
             rows = pl.ds(pl.multiple_of((t ^ k) * chunk, chunk), chunk)
             da_in = dqkv[rows, :]
             du_in = du[rows, :]
@@ -616,23 +770,20 @@
                 else:
                     ownp[phase % 2, :, cols] = e
             if k:
-                part_copy(phase, k).start()
-        grad_part(layer, 0, buf)
+                parts_start(phase, k)
 
     def finish_e(layer):
         phase = 3 - layer
-        for k in range(1, 4):
-            part_copy(phase, k).wait_recv()
+        parts_wait(phase)
         stage = gst.at[1 - layer]
         given = cotv if layer == 1 else gst.at[0]
-        resid = jnp.zeros((1, width), F32)
 
         @pl.loop(0, chunk // sub)
         def _(i):
             r = pl.ds(pl.multiple_of(i * sub, sub), sub)
             rows = pl.ds(pl.multiple_of(t * chunk + i * sub, sub), sub)
             e = ownp[phase % 2, r, :]
-            for k in range(3):
+            for k in range(2):
                 e = e + recvb[phase % 2, k, r, :].astype(F32)
             rs = rstd[layer, rows, :]
             unit = (x[layer, rows, :].astype(F32) - mu[layer, rows, :]) * rs
@@ -649,33 +800,116 @@
                 gb[0, rows, :] = g.astype(BF)
 
         if layer == 1:
-            for k in range(1, 4):
-                g_copy(0, k).start()
+            gather_start(*ag_g)
         place(layer, stage, out_g, 2 + layer)
 
-    forward_layer(0)
+    norm_chunk(0, t)
+    first_w(0)
+    for k in range(1, 4):
+        x_arrival(k).wait_recv()
+        norm_chunk(0, t ^ k)
+
+    @pl.loop(0, 4)
+    def _(c):
+        project_in(0, c)
+
+    attend(0)
+    first_w(1)
+
+    @pl.loop(0, 4)
+    def _(c):
+        hidden(0, c)
+
+    first_w(2)
+    second_w_send()
+    project_out(0)
+    parts_pass(0)
+    second_w_pass(0)
     finish_y(0)
-    forward_layer(1)
-    backward_layer(1, gw, lambda p: None)
+
+    second_w_wait(0)
+    @pl.loop(0, 4)
+    def _(k):
+        arrive(*ag_x, k)
+        norm_chunk(1, t ^ k)
+        project_in(1, t ^ k)
+
+        @pl.when(k == 0)
+        def _():
+            gather_pass(*ag_x)
+            second_w_pass(1)
+            second_w_wait(1)
+
+        hidden(1, t ^ k)
+
+    second_w_pass(2)
+    attend(1)
+    second_w_wait(2)
+    project_out(1)
+
+    for k in range(1, 4):
+        g_arrival(k).wait_recv()
+    zero_sums()
+
+    @pl.loop(0, 4)
+    def _(c):
+        hidden_back(1, c)
+
+    parts_pass(1)
+    attend_back(1, 0, nblk)
+    pack_qkv(1)
+    project_back(1)
+    grad_part(1, 2, gw)
+    parts_pass(2)
+    grad_part(1, 1, gw)
+    grad_part(1, 0, gw)
     finish_y(1)
     finish_e(1)
-    renorm_all(0)
-    for p in (2, 1, 0):
-        reduce_cores(1, p, gw)
+
     late = w.at[1]
-    for p in range(3):
-        for j in range(1, n):
-            w_copy(p, j).wait_send()
-
-        @pl.when(s == 0)
-        def _():
-            forward(0, p).wait_send()
-
-        @pl.when(s == 1)
-        def _():
-            forward(1, p).wait_send()
-
-    backward_layer(0, late, lambda p: reduce_cores(0, p, late))
+    per = chunk // BQ
+    first_w_sent()
+    second_w_sent()
+    zero_sums()
+
+    @pl.loop(0, 8)
+    def _(step_no):
+        k = jnp.where(step_no < 2, 0, jnp.where(step_no < 5, step_no - 1, step_no - 4))
+
+        @pl.when((step_no == 0) | ((step_no >= 2) & (step_no < 5)))
+        def _():
+            arrive(*ag_g, k)
+            hidden_back(0, t ^ k)
+
+        @pl.when(step_no == 5)
+        def _():
+            grad_part(0, 2, late)
+            grad_part(0, 1, late)
+
+        @pl.when(step_no == 6)
+        def _():
+            reduce_cores(0, 2, late)
+
+        @pl.when(step_no == 7)
+        def _():
+            reduce_cores(0, 1, late)
+
+        @pl.when((step_no == 1) | (step_no >= 5))
+        def _():
+            attend_back(0, (t ^ k) * per, ((t ^ k) + 1) * per)
+
+        @pl.when(step_no == 1)
+        def _():
+            gather_pass(*ag_g)
+            for p in (2, 1, 0):
+                reduce_cores(1, p, gw)
+            renorm_all(0)
+
+    pack_qkv(0)
+    project_back(0)
+    grad_part(0, 0, late)
+    parts_pass(3)
+    reduce_cores(0, 0, late)
     finish_e(0)
 
     to_sib = remote(sm.at[1 - s], smr, sms.at[0], smrs.at[0], sib)
@@ -686,7 +920,6 @@
         remote(
             smt, smz.at[j - 1], sms.at[j], smrs.at[j], (s, other_z(j), t)
         ).start()
-    reduce_cores(0, 0, late)
     for j in range(1, n):
         remote(smt, smz.at[j - 1], sms.at[j], smrs.at[j], (s, other_z(j), t)).wait()
     total = smt[...]
@@ -723,10 +956,12 @@
             z_copy(p, j, late).wait_send()
 
     for k in range(1, 4):
-        for layer in range(2):
-            x_copy(layer, k).wait_send()
-            g_copy(layer, k).wait_send()
-        part_copy(3, k).wait_send()
+        x_copy(k).wait_send()
+        g_copy(k).wait_send()
+    for i in range(6):
+        gather_copy(*ag_x, i).wait_send()
+        gather_copy(*ag_g, i).wait_send()
+    parts_sent(3)
     placed(1, yst, out_y, 1)
     placed(1, gst.at[0], out_g, 3)
     placed(0, gst.at[1], out_g, 2)
@@ -764,7 +999,6 @@
     up_bias,
     resid_bias,
 ):
-    column = lax.axis_index("tensor")
     micro, _, chunk, width = inputs.shape
     length = segment_ids.shape[2]
     head_cols = qkv_weight.shape[3]
@@ -774,16 +1008,7 @@
     assert micro == 2 and length == 4 * chunk and ff_local == width
     assert head_cols == 192 and width == 768
 
-    packed = jnp.concatenate(
-        [qkv_weight[0, 0], qkv_weight[0, 1], qkv_weight[0, 2], out_weight[0].T], axis=1
-    )
-    w_in = jnp.stack([packed, up_weight[0], down_weight[0].T])
-    qv_local = lax.dynamic_slice_in_dim(qv_bias[0], column * head_cols, head_cols, 1)
-    qv_local = jnp.pad(qv_local, ((0, 0), (0, width - head_cols)))
-    up_local = lax.dynamic_slice_in_dim(up_bias, column * ff_local, ff_local, 1)
-    par_in = jnp.concatenate([norm_gain[0], norm_bias[0], qv_local, up_local, resid_bias], axis=0)
     first, second = rotary_rows(length, heads)
-    seg = segment_ids.reshape(micro, length)
 
     vm = pl.BlockSpec(memory_space=pltpu.VMEM)
     anywhere = pl.BlockSpec(memory_space=pl.ANY)
@@ -819,7 +1044,8 @@
         pscr=vmem(BK, blk, dtype=F32),
         dpscr=vmem(BK, blk, dtype=F32),
         sendb=vmem(3, chunk, width),
-        recvb=vmem(2, 3, chunk, width),
+        recvb=vmem(2, 2, chunk, width),
+        relayed=vmem(2, 2, chunk // 2, width),
         ownp=vmem(2, chunk, width, dtype=F32),
         gw=vmem(3, width, width),
         gsr=vmem(3, width, width),
@@ -828,7 +1054,8 @@
         cotv=vmem(chunk, width, dtype=F32),
         yst=vmem(chunk, width, dtype=F32),
         gst=vmem(2, chunk, width, dtype=F32),
-        segc=vmem(length, 1, dtype=jnp.int32),
+        segc=vmem(length, BQ, dtype=F32),
+        segr=vmem(1, length, dtype=F32),
         par=vmem(2, 8, width, dtype=F32),
         sm=vmem(2, 8, width, dtype=F32),
         smr=vmem(8, width, dtype=F32),
@@ -837,16 +1064,20 @@
         tall=vmem(4, 8, width, dtype=F32),
         lsem=dma((8,)),
         psem=dma((2,)),
-        xs=dma((2, 3)),
-        xr=dma((2, 3)),
-        gs=dma((2, 3)),
-        gr=dma((2, 3)),
-        ws=dma((3, n - 1)),
-        wr=dma((3, n - 1)),
-        fs=dma((3,)),
-        fr=dma((3,)),
-        rss=dma((4, 3)),
-        rsr=dma((4, 3)),
+        xs=dma((3,)),
+        xr=dma((3,)),
+        agx=dma((6,)),
+        agxr=dma((6,)),
+        agg=dma((6,)),
+        aggr=dma((6,)),
+        gs=dma((3,)),
+        gr=dma((3,)),
+        ws=dma((2, 3, n)),
+        wr=dma((2, 3, n)),
+        fs=dma((3, n)),
+        fr=dma((3, n)),
+        rss=dma((4, 6)),
+        rsr=dma((4, 6)),
         osend=dma((4,)),
         orecv=dma((2,)),
         ghs=dma((3,)),
@@ -864,7 +1095,7 @@
             jax.ShapeDtypeStruct((3, rows_z, width), F32),
             jax.ShapeDtypeStruct((4, 8, width), F32),
         ),
-        in_specs=[anywhere, anywhere, anywhere, vm, anywhere, anywhere, vm, vm],
+        in_specs=[anywhere, anywhere, vm, vm, vm, anywhere, anywhere] + [vm] * 7,
         out_specs=(anywhere, anywhere, anywhere, vm),
         scratch_shapes=list(scratch.values()),
         compiler_params=pltpu.CompilerParams(
@@ -874,10 +1105,16 @@
     )(
         inputs.reshape(micro, chunk, width),
         cotangent.reshape(micro, chunk, width),
-        seg[:, :, None],
-        seg,
-        w_in,
-        par_in,
+        segment_ids,
+        qkv_weight,
+        out_weight,
+        up_weight,
+        down_weight[0].T,
+        norm_gain,
+        norm_bias,
+        qv_bias,
+        up_bias,
+        resid_bias,
         jnp.asarray(first),
         jnp.asarray(second),
     )

time: 268 us -> 245 us (0.914)
  the two profiles are of different devices: /device:TPU:24 before, /device:TPU:0 now
where the time goes in v2:
time: 245 us; the launch traced here: 244 us
  Pallas kernels  229 us (93%)
  local copies, waits for them, and re-layouts  12.4 us (5%)
  other arithmetic  2.78 us (1%)
    pallas_call x1, Pallas kernels, body(): pl.pallas_call(functools.partial(kernel, n, heads), out_shape=(jax.ShapeD...  229 us

profile of v2, /device:TPU:0, one launch (start us, length us, event | category | flops | bytes accessed | tf_op | source)
XLA Modules:
  0.0 244.4 jit_solution(7980273544070406681)
XLA Ops:
  0.6 228.6 %two_layers.1 = (f32[2,256,768]{2,1,0:T(8,128)}, f32[2,256,768]{2,1,0:T(8,128)}, f32[3,192,768]{2,1,0:T(8,128)}, f32[4,8,768]{2,1,0:T(8,128)}) custom-call(bf16[2,256,768]{2,1,0:T(8,128)(2,1)} %bitcast.35, f32[2,256,768]{2,1,0:T(8,128)} %bitcast.32, s32[2,1,1024]{2,1,0:T(1,128)} %seg_in.1, bf16[1,3,192,192]{3,2,1,0:T(8,128)(2,1)} %qkv_in.1, ...), custom_call_target="tpu_custom_call" | custom-call | tf_op jit(solution)/shard_map/two_layers/pallas_call | solution.py:1090
  229.3 0.0 copy-start
  229.3 0.9 slice_bitcast_fusion.2
  230.2 0.7 reshape.41
  230.8 1.5 slice.42
  232.3 0.9 reduce_sum.9
  233.3 0.6 slice.46
  233.8 0.6 slice_bitcast_fusion.3
  234.4 2.2 slice_bitcast_fusion.1
  236.6 0.0 copy-done
  236.6 0.0 copy-start.2
  236.6 1.1 slice_bitcast_fusion
  237.7 1.7 copy.31
  239.4 1.9 maximum_bitcast_fusion
  241.3 0.0 copy-done.2
  241.3 0.0 copy-start.1
  241.3 1.1 copy.34
  242.5 0.8 copy-done.1
  243.3 1.1 copy.35
  (1 shorter events, 0.0 us)
Async XLA Ops:
  229.3 7.4 %copy-start = (f32[3,192,768]{2,1,0:T(8,128)S(1)}, f32[3,192,768]{2,1,0:T(8,128)}, u32[]{:S(2)}) copy-start(f32[3,192,768]{2,1,0:T(8,128)} %get-tuple-element.17) | copy-start | bytes 5308420
  236.6 4.7 %copy-start.2 = (f32[2,256,768]{2,1,0:T(8,128)S(1)}, f32[2,256,768]{2,1,0:T(8,128)}, u32[]{:S(2)}) copy-start(f32[2,256,768]{2,1,0:T(8,128)} %get-tuple-element.15) | copy-start | bytes 4718596
  241.3 2.0 copy-start.1

commit v3 on v2

--- a/solution.py
+++ b/solution.py
@@ -96,6 +96,7 @@
     gw,
     gsr,
     zrecv,
+    zacc,
     wacc,
     cotv,
     yst,
@@ -130,6 +131,7 @@
     ghr,
     zs,
     zr,
+    za,
     sms,
     smrs,
 ):
@@ -161,29 +163,6 @@
     ld.start()
     lc.start()
 
-    head_cols = heads * HEAD_DIM
-
-    def picks(first):
-        rows = lax.broadcasted_iota(jnp.int32, (head_cols, width), 0)
-        cols = lax.broadcasted_iota(jnp.int32, (head_cols, width), 1)
-        return (rows + first == cols).astype(F32).astype(BF)
-
-    packed = mm(qkv_in[0, 0], picks(QO), NN) + mm(qkv_in[0, 1], picks(KO), NN)
-    packed = packed + mm(qkv_in[0, 2], picks(VO), NN) + mm(wo_in[0], picks(OO), TN)
-    w[s, 0, zrows, :] = packed.astype(BF)
-
-    par[s, 0:2, :] = gain_in[0]
-    par[s, 2:4, :] = shift_in[0]
-    par[s, 4:6, :] = qv_in[0]
-    par[s, 6:7, :] = upb_in[0:1, pl.ds(pl.multiple_of(t * width, 128), width)]
-    par[s, 7:8, :] = resid_in[...]
-    rows8 = par[s]
-    turned = rows8
-    for i in range(1, 4):
-        turned = jnp.where(t == i, pltpu.roll(rows8, width - i * head_cols, 1), turned)
-    row = lax.broadcasted_iota(jnp.int32, (8, width), 0)
-    par[s] = jnp.where((row == 4) | (row == 5), turned, rows8)
-
     barrier = pltpu.get_barrier_semaphore()
     pl.semaphore_signal(barrier, inc=1, device_id=sib, device_id_type=MESH)
     for k in range(1, 4):
@@ -192,51 +171,93 @@
         pl.semaphore_signal(barrier, inc=1, device_id=(s, other_z(j), t), device_id_type=MESH)
     pl.semaphore_wait(barrier, 4 + n - 1)
 
-    right = (s, lax.rem(z + 1, n), t)
-    left = (s, lax.rem(z + n - 1, n), t)
+    head_cols = heads * HEAD_DIM
+
+    def picks(first):
+        rows = lax.broadcasted_iota(jnp.int32, (head_cols, width), 0)
+        cols = lax.broadcasted_iota(jnp.int32, (head_cols, width), 1)
+        return (rows + first == cols).astype(F32).astype(BF)
+
+    def pack_share():
+        packed = mm(qkv_in[0, 0], picks(QO), NN) + mm(qkv_in[0, 1], picks(KO), NN)
+        packed = packed + mm(qkv_in[0, 2], picks(VO), NN) + mm(wo_in[0], picks(OO), TN)
+        w[s, 0, zrows, :] = packed.astype(BF)
+
+    def pack_params():
+        par[s, 0:2, :] = gain_in[0]
+        par[s, 2:4, :] = shift_in[0]
+        par[s, 4:6, :] = qv_in[0]
+        par[s, 6:7, :] = upb_in[0:1, pl.ds(pl.multiple_of(t * width, 128), width)]
+        par[s, 7:8, :] = resid_in[...]
+        rows8 = par[s]
+        turned = rows8
+        for i in range(1, 4):
+            turned = jnp.where(t == i, pltpu.roll(rows8, width - i * head_cols, 1), turned)
+        row = lax.broadcasted_iota(jnp.int32, (8, width), 0)
+        par[s] = jnp.where((row == 4) | (row == 5), turned, rows8)
 
     def w_rows(origin):
         return pl.ds(origin * rows_z, rows_z)
 
-    def line_copy(p, origin, dev):
-        up = dev is right
-        i = 0 if up else 1
+    def w_step(p, origin, far, src=None):
+        rows = w_rows(origin)
+        i = {1: 0, 2: 1, -1: 2, -2: 3}[far]
         return remote(
-            w.at[0, p, w_rows(origin)],
-            w.at[0, p, w_rows(origin)],
+            w.at[s, p, rows] if src is None else src,
+            w.at[s, p, rows],
             ws.at[i, p, origin],
-            wr.at[i, p, origin],
-            dev,
+            wr.at[p, origin],
+            (s, lax.rem(z + far + n, n), t),
         )
+
+    def inside(far):
+        return (z + far < n) if far > 0 else (z + far >= 0)
+
+    def w_send(p, src=None):
+        for far in (1, -1, 2, -2):
+
+            @pl.when(inside(far))
+            def _():
+                w_step(p, z, far, src).start()
+
+    def w_arrive(p, distances, passed, then):
+        for e in distances:
+            for sign in (1, -1):
+
+                @pl.when(inside(-sign * e))
+                def _():
+                    origin = lax.rem(z - sign * e + n, n)
+                    w_step(p, origin, sign).wait_recv()
+                    if passed:
+                        for far in (sign, 2 * sign):
+
+                            @pl.when(inside(far))
+                            def _():
+                                w_step(p, origin, far).start()
+
+                    if then is not None:
+                        then(p, origin)
+
+    def w_sent(p):
+        for far in (1, -1, 2, -2):
+
+            @pl.when(inside(far))
+            def _():
+                w_step(p, z, far).wait_send()
+
+            sign = 1 if far > 0 else -1
+            for e in range(2, n, 2):
+
+                @pl.when(inside(-sign * e) & inside(far))
+                def _():
+                    w_step(p, lax.rem(z - sign * e + n, n), far).wait_send()
 
     def across(p, origin):
         rows = w_rows(origin)
         return remote(w.at[0, p, rows], w.at[0, p, rows], fs.at[p, origin], fr.at[p, origin], sib)
 
-    def w_copy(p, j):
-        return remote(
-            w.at[1, p, zrows],
-            w.at[1, p, zrows],
-            ws.at[0, p, j - 1],
-            wr.at[0, p, j - 1],
-            (s, other_z(j), t),
-        )
-
-    def w_arrival(p, j):
-        rows = w_rows(other_z(n - j))
-        return remote(
-            w.at[1, p, rows], w.at[1, p, rows], ws.at[0, p, j - 1], wr.at[0, p, j - 1], sib
-        )
-
     def forward(p):
         return remote(w.at[1, p], w.at[1, p], fs.at[p, 0], fr.at[p, 0], sib)
-
-    def x_copy(k):
-        return remote(x.at[0, own], x.at[0, own], xs.at[k - 1], xr.at[k - 1], plane(k))
-
-    def x_arrival(k):
-        rows = pl.ds((t ^ k) * chunk, chunk)
-        return remote(x.at[0, rows], x.at[0, rows], xs.at[k - 1], xr.at[k - 1], plane(k))
 
     def g_copy(k):
         return remote(gb.at[1, own], gb.at[1, own], gs.at[k - 1], gr.at[k - 1], plane(k))
@@ -311,25 +332,24 @@
         for i in range(2, 6):
             part_copy(phase, i).wait_recv()
 
+    ag_i = (x.at[0], xs, xr)
     ag_x = (x.at[1], agx, agxr)
     ag_g = (gb.at[0], agg, aggr)
 
-    def send_own(p):
-        @pl.when(z + 1 < n)
-        def _():
-            line_copy(p, z, right).start()
-
-        @pl.when(z > 0)
-        def _():
-            line_copy(p, z, left).start()
-
     @pl.when(s == 0)
     def _():
-        send_own(0)
+        w_send(1, up_in.at[0])
 
     lx.wait()
-    for k in range(1, 4):
-        x_copy(k).start()
+    gather_start(*ag_i)
+    pack_share()
+
+    @pl.when(s == 0)
+    def _():
+        w_send(0)
+        w_send(2, down_in)
+
+    pack_params()
     par_copy = remote(par.at[s], par.at[s], psem.at[0], psem.at[1], sib)
     par_copy.start()
     lu.wait()
@@ -337,13 +357,8 @@
 
     @pl.when(s == 0)
     def _():
-        for p in range(3):
+        for p in (1, 0, 2):
             across(p, z).start()
-
-    lc.wait()
-    gb[1, own, :] = cotv[...].astype(BF)
-    for k in range(1, 4):
-        g_copy(k).start()
 
     for i in range(length // BQ):
         cols = slice(i * BQ, (i + 1) * BQ)
@@ -370,35 +385,15 @@
     def _(i):
         sm[i] = jnp.zeros((8, width), F32)
 
+    def first_w_pass(p):
+        @pl.when(s == 0)
+        def _():
+            w_arrive(p, range(2, n, 2), True, lambda p, origin: across(p, origin).start())
+
     def first_w(p):
         @pl.when(s == 0)
         def _():
-            for d in range(1, n):
-
-                @pl.when(z >= d)
-                def _():
-                    origin = jnp.maximum(z - d, 0)
-                    line_copy(p, origin, right).wait_recv()
-
-                    @pl.when(z + 1 < n)
-                    def _():
-                        line_copy(p, origin, right).start()
-
-                    across(p, origin).start()
-
-                @pl.when(z + d < n)
-                def _():
-                    origin = jnp.minimum(z + d, n - 1)
-                    line_copy(p, origin, left).wait_recv()
-
-                    @pl.when(z > 0)
-                    def _():
-                        line_copy(p, origin, left).start()
-
-                    across(p, origin).start()
-
-                if d == 1 and p < 2:
-                    send_own(p + 1)
+            w_arrive(p, range(1, n, 2), False, lambda p, origin: across(p, origin).start())
 
         @pl.when(s == 1)
         def _():
@@ -409,33 +404,29 @@
         @pl.when(s == 0)
         def _():
             for p in range(3):
+                w_sent(p)
                 for origin in range(n):
-
-                    @pl.when((z >= origin) & (z + 1 < n))
-                    def _():
-                        line_copy(p, origin, right).wait_send()
-
-                    @pl.when((z <= origin) & (z > 0))
-                    def _():
-                        line_copy(p, origin, left).wait_send()
-
                     across(p, origin).wait_send()
 
     def second_w_send():
         @pl.when(s == 1)
         def _():
-            for p in range(3):
-                for j in range(1, n):
-                    w_copy(p, j).start()
+            w_send(1, up_in.at[0])
+            w_send(0)
+            w_send(2, down_in)
 
     def second_w_pass(p):
         @pl.when(s == 1)
         def _():
-            for j in range(1, n):
-                w_arrival(p, j).wait_recv()
+            w_arrive(p, range(2, n, 2), True, None)
+
+    def second_w_give(p):
+        @pl.when(s == 1)
+        def _():
+            w_arrive(p, range(1, n, 2), False, None)
             forward(p).start()
 
-    def second_w_wait(p):
+    def second_w(p):
         @pl.when(s == 0)
         def _():
             forward(p).wait_recv()
@@ -444,8 +435,7 @@
         @pl.when(s == 1)
         def _():
             for p in range(3):
-                for j in range(1, n):
-                    w_copy(p, j).wait_send()
+                w_sent(p)
                 forward(p).wait_send()
 
     def prow(layer, r, cols=None):
@@ -622,15 +612,82 @@
         def _():
             remote(buf.at[p], gsr.at[p], ghs.at[p], ghr.at[p], sib).start()
 
-    def z_copy(p, j, buf):
-        rows = pl.ds(other_z(j) * rows_z, rows_z)
+    def z_item(p, e, sign, buf):
+        dest = lax.rem(z + sign * e + n, n)
+        way = 0 if sign > 0 else 1
+        if e <= 2:
+            slot = 2 * way + e - 1
+            dst, recv, far = zrecv.at[p, slot], zr.at[p, slot], e
+        else:
+            place_no = e - 3 if sign > 0 else n - z + e - 4
+            dst, recv, far = zacc.at[p, place_no], za.at[way, p, e - 3], 1
         return remote(
-            buf.at[p, rows],
-            zrecv.at[p, j - 1],
-            zs.at[p, j - 1],
-            zr.at[p, j - 1],
-            (s, other_z(j), t),
+            buf.at[p, w_rows(dest)],
+            dst,
+            zs.at[way, p, e - 1],
+            recv,
+            (s, lax.rem(z + sign * far + n, n), t),
         )
+
+    def first_of(sign):
+        return (z == 0) if sign > 0 else (z == n - 1)
+
+    def z_send(p, buf):
+        for e in range(n - 1, 0, -1):
+            for sign in (1, -1):
+                go = inside(sign * e)
+                if e > 1:
+                    go = go & first_of(sign)
+
+                @pl.when(go)
+                def _():
+                    z_item(p, e, sign, buf).start()
+
+    def z_pass(layer, p, buf):
+        @pl.when(s == layer)
+        def _():
+            for e in range(n - 2, 1, -1):
+                for sign in (1, -1):
+
+                    @pl.when(inside(sign * e) & inside(-sign))
+                    def _():
+                        way = 0 if sign > 0 else 1
+                        place_no = e - 2 if sign > 0 else n - z + e - 4
+                        got = zacc.at[p, place_no]
+                        remote(got, got, zs.at[way, p, e - 1], za.at[way, p, e - 2], sib).wait_recv()
+                        base = lax.rem(z + sign * e + n, n) * rows_z
+
+                        @pl.loop(0, rows_z // step)
+                        def _(i):
+                            r = pl.ds(pl.multiple_of(i * step, 16), step)
+                            q = pl.ds(pl.multiple_of(base + i * step, 16), step)
+                            more = zacc[p, place_no, r, :].astype(F32)
+                            buf[p, q, :] = (buf[p, q, :].astype(F32) + more).astype(BF)
+
+                        z_item(p, e, sign, buf).start()
+
+    def z_end(p, buf):
+        for slot in range(4):
+            sign = 1 if slot < 2 else -1
+            e = slot % 2 + 1
+
+            @pl.when(inside(-sign * e))
+            def _():
+                got = zrecv.at[p, slot]
+                remote(got, got, zs.at[0, p, 0], zr.at[p, slot], sib).wait_recv()
+
+                @pl.loop(0, rows_z // step)
+                def _(i):
+                    r = pl.ds(pl.multiple_of(i * step, 16), step)
+                    wacc[p, r, :] = wacc[p, r, :] + zrecv[p, slot, r, :].astype(F32)
+
+    def z_sent(p, buf):
+        for e in range(1, n):
+            for sign in (1, -1):
+
+                @pl.when(inside(sign * e))
+                def _():
+                    z_item(p, e, sign, buf).wait_send()
 
     step = 48
 
@@ -653,7 +710,7 @@
                     q = pl.ds(pl.multiple_of(base + i * step, 16), step)
                     buf[p, q, :] = (buf[p, q, :].astype(F32) + gsr[p, q, :].astype(F32)).astype(BF)
 
-                z_copy(p, j, buf).start()
+            z_send(p, buf)
 
         @pl.when(s != layer)
         def _():
@@ -804,47 +861,65 @@
         place(layer, stage, out_g, 2 + layer)
 
     norm_chunk(0, t)
+    gather_pass(*ag_i)
+    lc.wait()
+    gb[1, own, :] = cotv[...].astype(BF)
+    for k in range(1, 4):
+        g_copy(k).start()
+    first_w_pass(1)
+
+    @pl.loop(1, 4)
+    def _(k):
+        arrive(*ag_i, k)
+        norm_chunk(0, t ^ k)
+
+    first_w(1)
+
+    @pl.loop(0, 4)
+    def _(c):
+        hidden(0, c)
+
+    first_w_pass(0)
     first_w(0)
-    for k in range(1, 4):
-        x_arrival(k).wait_recv()
-        norm_chunk(0, t ^ k)
 
     @pl.loop(0, 4)
     def _(c):
         project_in(0, c)
 
     attend(0)
-    first_w(1)
-
-    @pl.loop(0, 4)
-    def _(c):
-        hidden(0, c)
-
+    first_w_pass(2)
     first_w(2)
     second_w_send()
     project_out(0)
     parts_pass(0)
-    second_w_pass(0)
+    second_w_pass(1)
     finish_y(0)
 
-    second_w_wait(0)
     @pl.loop(0, 4)
     def _(k):
         arrive(*ag_x, k)
         norm_chunk(1, t ^ k)
-        project_in(1, t ^ k)
 
         @pl.when(k == 0)
         def _():
+            second_w_give(1)
             gather_pass(*ag_x)
-            second_w_pass(1)
-            second_w_wait(1)
+            second_w_pass(0)
+            second_w(1)
 
         hidden(1, t ^ k)
 
+    second_w_give(0)
     second_w_pass(2)
+    second_w(0)
+
+    @pl.loop(0, 4)
+    def _(c):
+        project_in(1, c)
+
     attend(1)
-    second_w_wait(2)
+    second_w_give(2)
+    second_w(2)
     project_out(1)
 
     for k in range(1, 4):
@@ -855,15 +930,20 @@
     def _(c):
         hidden_back(1, c)
 
+    grad_part(1, 2, gw)
     parts_pass(1)
+    grad_part(1, 1, gw)
     attend_back(1, 0, nblk)
+    reduce_cores(1, 2, gw)
+    reduce_cores(1, 1, gw)
     pack_qkv(1)
     project_back(1)
-    grad_part(1, 2, gw)
+    z_pass(1, 2, gw)
+    grad_part(1, 0, gw)
     parts_pass(2)
-    grad_part(1, 1, gw)
-    grad_part(1, 0, gw)
+    z_pass(1, 1, gw)
     finish_y(1)
+    reduce_cores(1, 0, gw)
     finish_e(1)
 
     late = w.at[1]
@@ -901,12 +981,13 @@
         @pl.when(step_no == 1)
         def _():
             gather_pass(*ag_g)
-            for p in (2, 1, 0):
-                reduce_cores(1, p, gw)
+            z_pass(1, 0, gw)
             renorm_all(0)
 
+    z_pass(0, 2, late)
     pack_qkv(0)
     project_back(0)
+    z_pass(0, 1, late)
     grad_part(0, 0, late)
     parts_pass(3)
     reduce_cores(0, 0, late)
@@ -933,15 +1014,9 @@
     for k in range(1, 4):
         small_copy(k).start()
 
+    z_pass(0, 0, late)
     for p in (2, 1, 0):
-        for j in range(1, n):
-            z_copy(p, j, late).wait_recv()
-
-            @pl.loop(0, rows_z // step)
-            def _(i):
-                r = pl.ds(pl.multiple_of(i * step, 16), step)
-                wacc[p, r, :] = wacc[p, r, :] + zrecv[p, j - 1, r, :].astype(F32)
-
+        z_end(p, late)
         pltpu.make_async_copy(wacc.at[p], out_w.at[p], lsem.at[p]).start()
     for k in range(1, 4):
         small_copy(k).wait_send()
@@ -952,13 +1027,12 @@
 
     for p in range(3):
         pltpu.make_async_copy(wacc.at[p], out_w.at[p], lsem.at[p]).wait()
-        for j in range(1, n):
-            z_copy(p, j, late).wait_send()
+        z_sent(p, late)
 
     for k in range(1, 4):
-        x_copy(k).wait_send()
         g_copy(k).wait_send()
     for i in range(6):
+        gather_copy(*ag_i, i).wait_send()
         gather_copy(*ag_x, i).wait_send()
         gather_copy(*ag_g, i).wait_send()
     parts_sent(3)
@@ -967,6 +1041,34 @@
     placed(0, gst.at[1], out_g, 2)
     remote(yst, out_y.at[1 - s], osend.at[0], orecv.at[0], sib).wait_recv()
     remote(gst.at[0], out_g.at[1 - s], osend.at[0], orecv.at[1], sib).wait_recv()
+
+
+def write_outputs(
+    head_cols, y, g, wg, small, y_out, g_out, up, down, qkv, out, gain, shift, qv, upb, resid, sem
+):
+    pairs = ((y, y_out), (g, g_out), (wg.at[1], up), (wg.at[2], down))
+    copies = [pltpu.make_async_copy(src, dst, sem.at[i]) for i, (src, dst) in enumerate(pairs)]
+    for copy in copies:
+        copy.start()
+    first = wg[0]
+    width = first.shape[1]
+    for i in range(3):
+        turned = pltpu.roll(first, width - i * head_cols, 1) if i else first
+        qkv[i] = turned[:, :head_cols]
+    last = pltpu.roll(first, width - 3 * head_cols, 1)[:, :256]
+    out[...] = last.T[:head_cols, :]
+    total = small[0] + small[1] + small[2] + small[3]
+    gain[...] = total[0:2]
+    shift[...] = total[2:4]
+    resid[...] = total[7:8]
+    spread = small[0]
+    upb[:, 0:width] = small[0, 6:7, :]
+    for i in range(1, 4):
+        spread = spread + pltpu.roll(small[i], i * head_cols, 1)
+        upb[:, i * width : (i + 1) * width] = small[i, 6:7, :]
+    qv[...] = spread[4:6]
+    for copy in copies:
+        copy.wait()
 
 
 def rotary_rows(length, heads):
@@ -1049,7 +1151,8 @@
         ownp=vmem(2, chunk, width, dtype=F32),
         gw=vmem(3, width, width),
         gsr=vmem(3, width, width),
-        zrecv=vmem(3, n - 1, rows_z, width),
+        zrecv=vmem(3, 4, rows_z, width),
+        zacc=vmem(3, max(n - 3, 1), rows_z, width),
         wacc=vmem(3, rows_z, width, dtype=F32),
         cotv=vmem(chunk, width, dtype=F32),
         yst=vmem(chunk, width, dtype=F32),
@@ -1064,16 +1167,16 @@
         tall=vmem(4, 8, width, dtype=F32),
         lsem=dma((8,)),
         psem=dma((2,)),
-        xs=dma((3,)),
-        xr=dma((3,)),
+        xs=dma((6,)),
+        xr=dma((6,)),
         agx=dma((6,)),
         agxr=dma((6,)),
         agg=dma((6,)),
         aggr=dma((6,)),
         gs=dma((3,)),
         gr=dma((3,)),
-        ws=dma((2, 3, n)),
-        wr=dma((2, 3, n)),
+        ws=dma((4, 3, n)),
+        wr=dma((3, n)),
         fs=dma((3, n)),
         fr=dma((3, n)),
         rss=dma((4, 6)),
@@ -1082,8 +1185,9 @@
         orecv=dma((2,)),
         ghs=dma((3,)),
         ghr=dma((3,)),
-        zs=dma((3, n - 1)),
-        zr=dma((3, n - 1)),
+        zs=dma((2, 3, n)),
+        zr=dma((3, 4)),
+        za=dma((2, 3, n)),
         sms=dma((n + 3,)),
         smrs=dma((n + 3,)),
     )
@@ -1118,20 +1222,39 @@
         jnp.asarray(first),
         jnp.asarray(second),
     )
-    qkv_grad = jnp.stack([out_w[0, :, i * head_cols : (i + 1) * head_cols] for i in range(3)])
-    sums = jnp.sum(out_s, axis=0)
+    shapes = (
+        (2, chunk, width),
+        (2, chunk, width),
+        (rows_z, width),
+        (rows_z, width),
+        (3, rows_z, head_cols),
+        (head_cols, rows_z),
+        (2, width),
+        (2, width),
+        (2, width),
+        (1, 4 * width),
+        (1, width),
+    )
+    y, g, up_g, down_g, qkv_g, out_gr, gain_g, shift_g, qv_g, upb_g, resid_g = pl.pallas_call(
+        functools.partial(write_outputs, head_cols),
+        out_shape=tuple(jax.ShapeDtypeStruct(shape, F32) for shape in shapes),
+        in_specs=[vm] * 4,
+        out_specs=(anywhere,) * 4 + (vm,) * 7,
+        scratch_shapes=[dma((4,))],
+        name="outputs",
+    )(out_y, out_g, out_w, out_s)
     return (
-        out_y.reshape(1, micro, 1, chunk, width),
-        out_g.reshape(1, micro, 1, chunk, width),
-        qkv_grad[None],
-        out_w[0, :, 3 * head_cols :].T[None],
-        out_w[1][None],
-        out_w[2].T[None],
-        sums[None, 0:2],
-        sums[None, 2:4],
-        out_s[:, 4:6, :head_cols].transpose(1, 0, 2).reshape(1, 2, -1),
-        out_s[:, 6, :].reshape(1, -1),
-        sums[None, 7],
+        y.reshape(1, micro, 1, chunk, width),
+        g.reshape(1, micro, 1, chunk, width),
+        qkv_g[None],
+        out_gr[None],
+        up_g[None],
+        down_g.T[None],
+        gain_g[None],
+        shift_g[None],
+        qv_g[None],
+        upb_g,
+        resid_g,
     )
 
 

time: 245 us -> 197 us (0.80)
  Pallas kernels: 229 us -> 196 us
  local copies, waits for them, and re-layouts: 12.4 us -> 0 us
  other arithmetic: 2.78 us -> 0 us
    pallas_call x1, Pallas kernels: 229 us -> 190 us  [body(): pl.pallas_call(functools.partial(kernel, n, heads), out_shape=(jax.ShapeD...]
    pallas_call x0 -> x1, Pallas kernels: none -> 5.4 us  [body(): pl.pallas_call(functools.partial(write_outputs, head_cols), out_shape=tup...]
    unnamed x9 -> x0, local copies, waits for them, and re-layouts: 4.84 us -> none
    broadcast_in_dim x3 -> x0, local copies, waits for them, and re-layouts: 3.86 us -> none  [the longest x1 2.18 us: body(): out_w[0, :, 3 * head_cols:].T[None]]
where the time goes in v3:
time: 197 us
  Pallas kernels  196 us (99%)
    pallas_call x1, Pallas kernels, body(): pl.pallas_call(functools.partial(kernel, n, heads), out_shape=(jax.ShapeD...  190 us
    pallas_call x1, Pallas kernels, body(): pl.pallas_call(functools.partial(write_outputs, head_cols), out_shape=tup...  5.4 us

profile of v3, /device:TPU:0, one launch (start us, length us, event | category | flops | bytes accessed | tf_op | source)
XLA Modules:
  0.0 196.6 jit_solution(1894609355987408617)
XLA Ops:
  0.6 190.3 %two_layers.1 = (f32[2,256,768]{2,1,0:T(8,128)}, f32[2,256,768]{2,1,0:T(8,128)}, f32[3,192,768]{2,1,0:T(8,128)}, f32[4,8,768]{2,1,0:T(8,128)}) custom-call(bf16[2,256,768]{2,1,0:T(8,128)(2,1)} %bitcast.21, f32[2,256,768]{2,1,0:T(8,128)} %bitcast.20, s32[2,1,1024]{2,1,0:T(1,128)} %seg_in.1, bf16[1,3,192,192]{3,2,1,0:T(8,128)(2,1)} %qkv_in.1, ...), custom_call_target="tpu_custom_call" | custom-call | tf_op jit(solution)/shard_map/two_layers/pallas_call | solution.py:1194
  191.0 5.4 %outputs.1 = (f32[2,256,768]{2,1,0:T(8,128)}, f32[2,256,768]{2,1,0:T(8,128)}, f32[192,768]{1,0:T(8,128)}, f32[192,768]{1,0:T(8,128)}, f32[3,192,192]{2,1,0:T(8,1...) custom-call(f32[2,256,768]{2,1,0:T(8,128)} %get-tuple-element.26.y, ...), custom_call_target="tpu_custom_call" | custom-call | tf_op jit(solution)/shard_map/outputs/pallas_call | solution.py:1238

commit v4 on v3

--- a/solution.py
+++ b/solution.py
@@ -75,6 +75,8 @@
     qb,
     kb,
     vb,
+    kt,
+    vt,
     cb,
     lse,
     slope,
@@ -89,6 +91,7 @@
     bias,
     pscr,
     dpscr,
+    dscr,
     sendb,
     recvb,
     relayed,
@@ -98,10 +101,8 @@
     zrecv,
     zacc,
     wacc,
-    cotv,
     yst,
     gst,
-    segc,
     segr,
     par,
     sm,
@@ -155,7 +156,7 @@
         return lax.rem(z + j, n)
 
     lx = pltpu.make_async_copy(x_in.at[s], x.at[0, own], lsem.at[0])
-    lc = pltpu.make_async_copy(cot_in.at[s], cotv, lsem.at[1])
+    lc = pltpu.make_async_copy(cot_in.at[s], gst.at[0], lsem.at[1])
     lu = pltpu.make_async_copy(up_in.at[0], w.at[s, 1, zrows], lsem.at[3])
     ld = pltpu.make_async_copy(down_in, w.at[s, 2, zrows], lsem.at[4])
     lx.start()
@@ -364,13 +365,13 @@
         cols = slice(i * BQ, (i + 1) * BQ)
         ids = jnp.where(s == 0, seg_in[0, :, cols], seg_in[1, :, cols]).astype(F32)
         segr[:, cols] = ids
-        segc[cols, :] = jnp.broadcast_to(ids, (BQ, BQ)).T
+        dq[cols, 0:BQ] = jnp.broadcast_to(ids, (BQ, BQ)).T
 
     @pl.loop(0, nblk)
     def _(b):
         q0 = pl.multiple_of(b * BQ, BQ)
         k0 = pl.multiple_of(jnp.maximum(b * BQ - SEG_MOST, 0), BQ)
-        seg_k = segc[pl.ds(k0, BK), :]
+        seg_k = dq[pl.ds(k0, BK), 0:BQ]
         seg_q = segr[:, pl.ds(q0, BQ)]
         kpos = lax.broadcasted_iota(jnp.int32, (BK, BQ), 0) + k0
         qpos = lax.broadcasted_iota(jnp.int32, (BK, BQ), 1) + q0
@@ -505,13 +506,20 @@
         u = mm(a, w[layer, 0, :, QO : QO + HL], NN) + prow(layer, 4, slice(0, HL))
         qb[layer, rows, :] = (rope(u, b0, 1.0) * 0.125).astype(BF)
         u = mm(a, w[layer, 0, :, KO - 64 : KO - 64 + HL], NN)
-        kb[layer, rows, :] = rope(pltpu.roll(u, HL - 64, 1), b0, 1.0).astype(BF)
+        u = rope(pltpu.roll(u, HL - 64, 1), b0, 1.0)
+        kb[layer, rows, :] = u.astype(BF)
+        kt[layer, :, rows] = u.T[: heads * HEAD_DIM].astype(BF)
         u = mm(a, w[layer, 0, :, VO : VO + HL], NN) + prow(layer, 5, slice(0, HL))
-        vb[layer, rows, :] = jnp.where(lane < heads * HEAD_DIM, u, 0.0).astype(BF)
-
-    def attend(layer):
+        u = jnp.where(lane < heads * HEAD_DIM, u, 0.0)
+        vb[layer, rows, :] = u.astype(BF)
+        vt[layer, :, rows] = u.T[: heads * HEAD_DIM].astype(BF)
+
+    def attend(layer, within=None):
         @pl.loop(0, nblk)
         def _(b):
+            if within is not None:
+                pl.when(b == nblk // 2)(within)
+
             q0 = pl.multiple_of(b * BQ, BQ)
             k0 = pl.multiple_of(jnp.maximum(b * BQ - SEG_MOST, 0), BQ)
             qm = stack_heads(qb[layer, pl.ds(q0, BQ), :])
@@ -531,14 +539,13 @@
                 total = part if total is None else total + part
             lse[layer, b] = top + jnp.log(total)
             inv = 1.0 / total
-            lane = lane_iota(BQ) >> 6
-            ctx = jnp.zeros((BQ, HL), F32)
-            vals = vb[layer, pl.ds(k0, BK), :]
+            ctx = [jnp.zeros((HL - heads * HEAD_DIM, BQ), F32)]
             for h in range(heads):
                 cols = slice(h * BQ, (h + 1) * BQ)
                 ph = (pscr[:, cols] * inv[:, cols]).astype(BF)
-                ctx = jnp.where(lane == h, mm(ph, vals, TN), ctx)
-            cb[layer, pl.ds(q0, BQ), :] = pltpu.roll(ctx, HL - heads * HEAD_DIM, 1).astype(BF)
+                vals = vt[layer, h * HEAD_DIM : (h + 1) * HEAD_DIM, pl.ds(k0, BK)]
+                ctx.append(mm(vals, ph, NN))
+            cb[layer, pl.ds(q0, BQ), :] = jnp.concatenate(ctx, axis=0).T.astype(BF)
 
     def hidden(layer, c):
         rows = pl.ds(pl.multiple_of(c * chunk, chunk), chunk)
@@ -749,9 +756,12 @@
             dk[rows, :] = jnp.zeros((sub, HL), F32)
             dv[rows, :] = jnp.zeros((sub, HL), F32)
 
-    def attend_back(layer, first, last):
+    def attend_back(layer, first, last, within=None):
         @pl.loop(first, last)
         def _(b):
+            if within is not None:
+                pl.when(b == first + 2)(within)
+
             q0 = pl.multiple_of(b * BQ, BQ)
             k0 = pl.multiple_of(jnp.maximum(b * BQ - SEG_MOST, 0), BQ)
             qm = stack_heads(qb[layer, pl.ds(q0, BQ), :])
@@ -770,20 +780,18 @@
                 dpscr[irows, :] = dp
                 part = jnp.sum(pr * dp, axis=0, keepdims=True)
                 total = part if total is None else total + part
-            lane = lane_iota(BQ) >> 6
-            acc = [jnp.zeros((BQ, HL), F32) for _ in range(heads)]
             for i in range(BK // BQ):
                 krows = pl.ds(k0 + i * BQ, BQ)
                 irows = slice(i * BQ, (i + 1) * BQ)
                 ds = (pscr[irows, :] * (dpscr[irows, :] - total)).astype(BF)
+                dscr[irows, :] = ds
                 dk[krows, :] = dk[krows, :] + mm(ds, qm, NN)
-                keys = kb[layer, krows, :]
-                for h in range(heads):
-                    acc[h] = acc[h] + mm(ds[:, h * BQ : (h + 1) * BQ], keys, TN)
-            out = jnp.zeros((BQ, HL), F32)
+            out = []
             for h in range(heads):
-                out = jnp.where(lane == h, acc[h], out)
-            dq[pl.ds(q0, BQ), :] = out
+                keys = kt[layer, h * HEAD_DIM : (h + 1) * HEAD_DIM, pl.ds(k0, BK)]
+                out.append(mm(keys, dscr[:, h * BQ : (h + 1) * BQ], NN))
+            out.append(jnp.zeros((HL - heads * HEAD_DIM, BQ), F32))
+            dq[pl.ds(q0, BQ), :] = jnp.concatenate(out, axis=0).T
 
     def pack_qkv(layer):
         @pl.loop(0, 4)
@@ -833,7 +841,7 @@
         phase = 3 - layer
         parts_wait(phase)
         stage = gst.at[1 - layer]
-        given = cotv if layer == 1 else gst.at[0]
+        given = gst.at[0]
 
         @pl.loop(0, chunk // sub)
         def _(i):
@@ -845,7 +853,8 @@
             rs = rstd[layer, rows, :]
             unit = (x[layer, rows, :].astype(F32) - mu[layer, rows, :]) * rs
             g = given[r, :]
-            sm[layer, 7:8, :] = sm[layer, 7:8, :] + jnp.sum(g, axis=0, keepdims=True)
+            if layer == 1:
+                sm[1, 7:8, :] = sm[1, 7:8, :] + jnp.sum(g, axis=0, keepdims=True)
             d = rs * (
                 e
                 - jnp.mean(e, axis=-1, keepdims=True)
@@ -854,6 +863,7 @@
             g = g + d
             stage[r, :] = g
             if layer == 1:
+                sm[0, 7:8, :] = sm[0, 7:8, :] + jnp.sum(g, axis=0, keepdims=True)
                 gb[0, rows, :] = g.astype(BF)
 
         if layer == 1:
@@ -863,7 +873,7 @@
     norm_chunk(0, t)
     gather_pass(*ag_i)
     lc.wait()
-    gb[1, own, :] = cotv[...].astype(BF)
+    gb[1, own, :] = gst[0].astype(BF)
     for k in range(1, 4):
         g_copy(k).start()
     first_w_pass(1)
@@ -886,10 +896,9 @@
     def _(c):
         project_in(0, c)
 
-    attend(0)
-    first_w_pass(2)
+    attend(0, lambda: first_w_pass(2))
+    second_w_send()
     first_w(2)
-    second_w_send()
     project_out(0)
     parts_pass(0)
     second_w_pass(1)
@@ -897,6 +906,11 @@
 
     @pl.loop(0, 4)
     def _(k):
+        @pl.when(k == 2)
+        def _():
+            second_w_pass(2)
+            second_w_give(0)
+
         arrive(*ag_x, k)
         norm_chunk(1, t ^ k)
 
@@ -909,16 +923,14 @@
 
         hidden(1, t ^ k)
 
-    second_w_give(0)
-    second_w_pass(2)
     second_w(0)
 
     @pl.loop(0, 4)
     def _(c):
         project_in(1, c)
 
+    second_w_give(2)
     attend(1)
-    second_w_give(2)
     second_w(2)
     project_out(1)
 
@@ -930,20 +942,16 @@
     def _(c):
         hidden_back(1, c)
 
-    grad_part(1, 2, gw)
-    parts_pass(1)
-    grad_part(1, 1, gw)
-    attend_back(1, 0, nblk)
-    reduce_cores(1, 2, gw)
-    reduce_cores(1, 1, gw)
+    attend_back(1, 0, nblk, lambda: parts_pass(1))
     pack_qkv(1)
     project_back(1)
-    z_pass(1, 2, gw)
+    grad_part(1, 2, gw)
+    grad_part(1, 1, gw)
+    parts_pass(2)
+    reduce_cores(1, 2, gw)
+    finish_y(1)
     grad_part(1, 0, gw)
-    parts_pass(2)
-    z_pass(1, 1, gw)
-    finish_y(1)
-    reduce_cores(1, 0, gw)
+    reduce_cores(1, 1, gw)
     finish_e(1)
 
     late = w.at[1]
@@ -951,6 +959,8 @@
     first_w_sent()
     second_w_sent()
     zero_sums()
+    z_pass(1, 2, gw)
+    reduce_cores(1, 0, gw)
 
     @pl.loop(0, 8)
     def _(step_no):
@@ -964,11 +974,16 @@
         @pl.when(step_no == 5)
         def _():
             grad_part(0, 2, late)
+
+        @pl.when(step_no == 4)
+        def _():
+            z_pass(1, 1, gw)
+
+        @pl.when(step_no == 6)
+        def _():
+            reduce_cores(0, 2, late)
             grad_part(0, 1, late)
-
-        @pl.when(step_no == 6)
-        def _():
-            reduce_cores(0, 2, late)
+            z_pass(1, 0, gw)
 
         @pl.when(step_no == 7)
         def _():
@@ -981,49 +996,53 @@
         @pl.when(step_no == 1)
         def _():
             gather_pass(*ag_g)
-            z_pass(1, 0, gw)
             renorm_all(0)
 
     z_pass(0, 2, late)
     pack_qkv(0)
     project_back(0)
-    z_pass(0, 1, late)
-    grad_part(0, 0, late)
-    parts_pass(3)
-    reduce_cores(0, 0, late)
-    finish_e(0)
 
     to_sib = remote(sm.at[1 - s], smr, sms.at[0], smrs.at[0], sib)
     to_sib.start()
+    grad_part(0, 0, late)
     to_sib.wait()
     smt[...] = sm[s] + smr[...]
+
+    def small_z(j):
+        return remote(smt, smz.at[j - 1], sms.at[j], smrs.at[j], (s, other_z(j), t))
+
+    def small_copy(k):
+        return remote(tall.at[t], tall.at[t], sms.at[n + k - 1], smrs.at[n + k - 1], plane(k))
+
     for j in range(1, n):
-        remote(
-            smt, smz.at[j - 1], sms.at[j], smrs.at[j], (s, other_z(j), t)
-        ).start()
+        small_z(j).start()
+    parts_pass(3)
+    z_pass(0, 1, late)
+    reduce_cores(0, 0, late)
+
+    def matrix_end(p):
+        z_end(p, late)
+        pltpu.make_async_copy(wacc.at[p], out_w.at[p], lsem.at[p]).start()
+
+    matrix_end(2)
     for j in range(1, n):
-        remote(smt, smz.at[j - 1], sms.at[j], smrs.at[j], (s, other_z(j), t)).wait()
+        small_z(j).wait()
     total = smt[...]
     for j in range(1, n):
         total = total + smz[j - 1]
     tall[t] = total
-
-    def small_copy(k):
-        return remote(tall.at[t], tall.at[t], sms.at[n + k - 1], smrs.at[n + k - 1], plane(k))
-
     for k in range(1, 4):
         small_copy(k).start()
-
     z_pass(0, 0, late)
-    for p in (2, 1, 0):
-        z_end(p, late)
-        pltpu.make_async_copy(wacc.at[p], out_w.at[p], lsem.at[p]).start()
+    finish_e(0)
+    matrix_end(1)
     for k in range(1, 4):
         small_copy(k).wait_send()
         remote(
             tall.at[t ^ k], tall.at[t ^ k], sms.at[n + k - 1], smrs.at[n + k - 1], plane(k)
         ).wait_recv()
     out_s[...] = tall[...]
+    matrix_end(0)
 
     for p in range(3):
         pltpu.make_async_copy(wacc.at[p], out_w.at[p], lsem.at[p]).wait()
@@ -1131,6 +1150,8 @@
         qb=vmem(2, length, HL),
         kb=vmem(2, length, HL),
         vb=vmem(2, length, HL),
+        kt=vmem(2, heads * HEAD_DIM, length),
+        vt=vmem(2, heads * HEAD_DIM, length),
         cb=vmem(2, length, HL),
         lse=vmem(2, nblk, 1, blk, dtype=F32),
         slope=vmem(2, length, width),
@@ -1145,6 +1166,7 @@
         bias=vmem(nblk, BK, BQ),
         pscr=vmem(BK, blk, dtype=F32),
         dpscr=vmem(BK, blk, dtype=F32),
+        dscr=vmem(BK, blk),
         sendb=vmem(3, chunk, width),
         recvb=vmem(2, 2, chunk, width),
         relayed=vmem(2, 2, chunk // 2, width),
@@ -1154,10 +1176,8 @@
         zrecv=vmem(3, 4, rows_z, width),
         zacc=vmem(3, max(n - 3, 1), rows_z, width),
         wacc=vmem(3, rows_z, width, dtype=F32),
-        cotv=vmem(chunk, width, dtype=F32),
         yst=vmem(chunk, width, dtype=F32),
         gst=vmem(2, chunk, width, dtype=F32),
-        segc=vmem(length, BQ, dtype=F32),
         segr=vmem(1, length, dtype=F32),
         par=vmem(2, 8, width, dtype=F32),
         sm=vmem(2, 8, width, dtype=F32),

time: 197 us -> 181 us (0.919)
  Pallas kernels: 196 us -> 180 us
    pallas_call x1, Pallas kernels: 190 us -> 175 us  [body(): pl.pallas_call(functools.partial(kernel, n, heads), out_shape=(jax.ShapeD...]
where the time goes in v4:
time: 181 us
  Pallas kernels  180 us (99%)
    pallas_call x1, Pallas kernels, body(): pl.pallas_call(functools.partial(kernel, n, heads), out_shape=(jax.ShapeD...  175 us
    pallas_call x1, Pallas kernels, body(): pl.pallas_call(functools.partial(write_outputs, head_cols), out_shape=tup...  5.4 us

profile of v4, /device:TPU:0, one launch (start us, length us, event | category | flops | bytes accessed | tf_op | source)
XLA Modules:
  0.0 181.1 jit_solution(1516377444850736645)
XLA Ops:
  0.6 174.8 %two_layers.1 = (f32[2,256,768]{2,1,0:T(8,128)}, f32[2,256,768]{2,1,0:T(8,128)}, f32[3,192,768]{2,1,0:T(8,128)}, f32[4,8,768]{2,1,0:T(8,128)}) custom-call(bf16[2,256,768]{2,1,0:T(8,128)(2,1)} %bitcast.21, f32[2,256,768]{2,1,0:T(8,128)} %bitcast.20, s32[2,1,1024]{2,1,0:T(1,128)} %seg_in.1, bf16[1,3,192,192]{3,2,1,0:T(8,128)(2,1)} %qkv_in.1, ...), custom_call_target="tpu_custom_call" | custom-call | tf_op jit(solution)/shard_map/two_layers/pallas_call | solution.py:1214
  175.5 5.4 %outputs.1 = (f32[2,256,768]{2,1,0:T(8,128)}, f32[2,256,768]{2,1,0:T(8,128)}, f32[192,768]{1,0:T(8,128)}, f32[192,768]{1,0:T(8,128)}, f32[3,192,192]{2,1,0:T(8,1...) custom-call(f32[2,256,768]{2,1,0:T(8,128)} %get-tuple-element.26.y, ...), custom_call_target="tpu_custom_call" | custom-call | tf_op jit(solution)/shard_map/outputs/pallas_call | solution.py:1258

commit v5 on v4

--- a/solution.py
+++ b/solution.py
@@ -50,11 +50,25 @@
     heads,
     x_in,
     cot_in,
+    seg_far,
+    qkv_far,
+    wo_far,
+    up_in,
+    down_in,
+    gain_far,
+    shift_far,
+    qv_far,
+    upb_far,
+    resid_far,
+    taba_far,
+    tabb_far,
+    out_y,
+    out_g,
+    out_w,
+    out_s,
     seg_in,
     qkv_in,
     wo_in,
-    up_in,
-    down_in,
     gain_in,
     shift_in,
     qv_in,
@@ -62,10 +76,6 @@
     resid_in,
     taba,
     tabb,
-    out_y,
-    out_g,
-    out_w,
-    out_s,
     w,
     x,
     an,
@@ -92,6 +102,7 @@
     pscr,
     dpscr,
     dscr,
+    pbf,
     sendb,
     recvb,
     relayed,
@@ -111,6 +122,7 @@
     smz,
     tall,
     lsem,
+    isem,
     psem,
     xs,
     xr,
@@ -159,7 +171,26 @@
     lc = pltpu.make_async_copy(cot_in.at[s], gst.at[0], lsem.at[1])
     lu = pltpu.make_async_copy(up_in.at[0], w.at[s, 1, zrows], lsem.at[3])
     ld = pltpu.make_async_copy(down_in, w.at[s, 2, zrows], lsem.at[4])
+    small_loads = [
+        pltpu.make_async_copy(src, dst, isem.at[i])
+        for i, (src, dst) in enumerate(
+            (
+                (qkv_far, qkv_in),
+                (wo_far, wo_in),
+                (gain_far, gain_in),
+                (shift_far, shift_in),
+                (qv_far, qv_in),
+                (upb_far, upb_in),
+                (resid_far, resid_in),
+                (seg_far, seg_in),
+                (taba_far, taba),
+                (tabb_far, tabb),
+            )
+        )
+    ]
     lx.start()
+    for load in small_loads:
+        load.start()
     lu.start()
     ld.start()
     lc.start()
@@ -215,17 +246,22 @@
         return (z + far < n) if far > 0 else (z + far >= 0)
 
     def w_send(p, src=None):
-        for far in (1, -1, 2, -2):
+        for far in (2, -2, 1, -1):
 
             @pl.when(inside(far))
             def _():
                 w_step(p, z, far, src).start()
 
-    def w_arrive(p, distances, passed, then):
-        for e in distances:
+    def w_arrive(p, passed, then):
+        for e in range(2, n, 2) if passed else range(1, n):
             for sign in (1, -1):
-
-                @pl.when(inside(-sign * e))
+                here = inside(-sign * e)
+                if passed:
+                    here = here & inside(sign)
+                elif e % 2 == 0:
+                    here = here & jnp.logical_not(inside(sign))
+
+                @pl.when(here)
                 def _():
                     origin = lax.rem(z - sign * e + n, n)
                     w_step(p, origin, sign).wait_recv()
@@ -253,12 +289,9 @@
                 def _():
                     w_step(p, lax.rem(z - sign * e + n, n), far).wait_send()
 
-    def across(p, origin):
-        rows = w_rows(origin)
-        return remote(w.at[0, p, rows], w.at[0, p, rows], fs.at[p, origin], fr.at[p, origin], sib)
-
-    def forward(p):
-        return remote(w.at[1, p], w.at[1, p], fs.at[p, 0], fr.at[p, 0], sib)
+    def across(p, origin, layer=0):
+        part = w.at[layer, p, w_rows(origin)]
+        return remote(part, part, fs.at[p, origin], fr.at[p, origin], sib)
 
     def g_copy(k):
         return remote(gb.at[1, own], gb.at[1, own], gs.at[k - 1], gr.at[k - 1], plane(k))
@@ -343,6 +376,8 @@
 
     lx.wait()
     gather_start(*ag_i)
+    for load in small_loads:
+        load.wait()
     pack_share()
 
     @pl.when(s == 0)
@@ -389,12 +424,12 @@
     def first_w_pass(p):
         @pl.when(s == 0)
         def _():
-            w_arrive(p, range(2, n, 2), True, lambda p, origin: across(p, origin).start())
+            w_arrive(p, True, lambda p, origin: across(p, origin).start())
 
     def first_w(p):
         @pl.when(s == 0)
         def _():
-            w_arrive(p, range(1, n, 2), False, lambda p, origin: across(p, origin).start())
+            w_arrive(p, False, lambda p, origin: across(p, origin).start())
 
         @pl.when(s == 1)
         def _():
@@ -415,29 +450,32 @@
             w_send(1, up_in.at[0])
             w_send(0)
             w_send(2, down_in)
+            for p in (1, 0, 2):
+                across(p, z, 1).start()
 
     def second_w_pass(p):
         @pl.when(s == 1)
         def _():
-            w_arrive(p, range(2, n, 2), True, None)
+            w_arrive(p, True, lambda p, origin: across(p, origin, 1).start())
 
     def second_w_give(p):
         @pl.when(s == 1)
         def _():
-            w_arrive(p, range(1, n, 2), False, None)
-            forward(p).start()
+            w_arrive(p, False, lambda p, origin: across(p, origin, 1).start())
 
     def second_w(p):
         @pl.when(s == 0)
         def _():
-            forward(p).wait_recv()
+            for origin in range(n):
+                across(p, origin, 1).wait_recv()
 
     def second_w_sent():
         @pl.when(s == 1)
         def _():
             for p in range(3):
                 w_sent(p)
-                forward(p).wait_send()
+                for origin in range(n):
+                    across(p, origin, 1).wait_send()
 
     def prow(layer, r, cols=None):
         if cols is None:
@@ -523,12 +561,13 @@
             q0 = pl.multiple_of(b * BQ, BQ)
             k0 = pl.multiple_of(jnp.maximum(b * BQ - SEG_MOST, 0), BQ)
             qm = stack_heads(qb[layer, pl.ds(q0, BQ), :])
+            pscr[...] = mm(kb[layer, pl.ds(k0, BK), :], qm, NT)
             top = None
             for i in range(BK // BQ):
-                keys = kb[layer, pl.ds(k0 + i * BQ, BQ), :]
-                blk = bias[b, i * BQ : (i + 1) * BQ, :].astype(F32)
-                sc = mm(keys, qm, NT) + jnp.concatenate([blk] * heads, axis=1)
-                pscr[i * BQ : (i + 1) * BQ, :] = sc
+                irows = slice(i * BQ, (i + 1) * BQ)
+                blk = bias[b, irows, :].astype(F32)
+                sc = pscr[irows, :] + jnp.concatenate([blk] * heads, axis=1)
+                pscr[irows, :] = sc
                 peak = jnp.max(sc, axis=0, keepdims=True)
                 top = peak if top is None else jnp.maximum(top, peak)
             total = None
@@ -614,10 +653,13 @@
             gather_start(*ag_x)
         place(layer, yst, out_y, layer)
 
-    def reduce_start(layer, p, buf):
+    def reduce_start(layer, p, j, buf):
+        rows = pl.ds(j * 256, 256)
+
+
         @pl.when(s != layer)
         def _():
-            remote(buf.at[p], gsr.at[p], ghs.at[p], ghr.at[p], sib).start()
+            remote(buf.at[p, rows], gsr.at[p, rows], ghs.at[p, j], ghr.at[p, j], sib).start()
 
     def z_item(p, e, sign, buf):
         dest = lax.rem(z + sign * e + n, n)
@@ -701,7 +743,9 @@
     def reduce_cores(layer, p, buf):
         @pl.when(s == layer)
         def _():
-            remote(buf.at[p], gsr.at[p], ghs.at[p], ghr.at[p], sib).wait_recv()
+            for j in range(width // 256):
+                rows = pl.ds(j * 256, 256)
+                remote(buf.at[p, rows], gsr.at[p, rows], ghs.at[p, j], ghr.at[p, j], sib).wait_recv()
 
             @pl.loop(0, rows_z // step)
             def _(i):
@@ -721,7 +765,22 @@
 
         @pl.when(s != layer)
         def _():
-            remote(buf.at[p], gsr.at[p], ghs.at[p], ghr.at[p], sib).wait_send()
+            for j in range(width // 256):
+                rows = pl.ds(j * 256, 256)
+                remote(buf.at[p, rows], gsr.at[p, rows], ghs.at[p, j], ghr.at[p, j], sib).wait_send()
+
+    def add_down_grad(k, buf):
+        rows = pl.ds(pl.multiple_of((t ^ k) * chunk, chunk), chunk)
+        h = hid[0, rows, :]
+        for j in range(width // 256):
+            cols = slice(j * 256, (j + 1) * 256)
+            more = mm(gb[0, rows, cols], h, TN)
+            before = jnp.where(k == 0, 0.0, buf[2, cols, :].astype(F32))
+            buf[2, cols, :] = (before + more).astype(BF)
+
+            @pl.when(k == 3)
+            def _():
+                reduce_start(0, 2, j, buf)
 
     def grad_part(layer, p, buf):
         for j in range(width // 256):
@@ -735,7 +794,7 @@
                 buf[p, cols, 512:768] = (
                     mm(an[:, cols], dqkv[:, 512:768], TN) + mm(gb[layer, :, cols], cb[layer], TN)
                 ).astype(BF)
-        reduce_start(layer, p, buf)
+            reduce_start(layer, p, j, buf)
 
     def hidden_back(layer, c):
         rows = pl.ds(pl.multiple_of(c * chunk, chunk), chunk)
@@ -767,25 +826,23 @@
             qm = stack_heads(qb[layer, pl.ds(q0, BQ), :])
             dm = stack_heads(dc[pl.ds(q0, BQ), :])
             ls = lse[layer, b]
+            win = pl.ds(k0, BK)
+            pscr[...] = mm(kb[layer, win, :], qm, NT)
+            dpscr[...] = mm(vb[layer, win, :], dm, NT)
             total = None
             for i in range(BK // BQ):
-                krows = pl.ds(k0 + i * BQ, BQ)
                 irows = slice(i * BQ, (i + 1) * BQ)
                 blk = bias[b, irows, :].astype(F32)
-                sc = mm(kb[layer, krows, :], qm, NT) + jnp.concatenate([blk] * heads, axis=1)
-                pr = jnp.exp(sc - ls)
-                dp = mm(vb[layer, krows, :], dm, NT)
-                dv[krows, :] = dv[krows, :] + mm(pr.astype(BF), dm, NN)
+                pr = jnp.exp(pscr[irows, :] + jnp.concatenate([blk] * heads, axis=1) - ls)
                 pscr[irows, :] = pr
-                dpscr[irows, :] = dp
-                part = jnp.sum(pr * dp, axis=0, keepdims=True)
+                pbf[irows, :] = pr.astype(BF)
+                part = jnp.sum(pr * dpscr[irows, :], axis=0, keepdims=True)
                 total = part if total is None else total + part
+            dv[win, :] = dv[win, :] + mm(pbf[...], dm, NN)
             for i in range(BK // BQ):
-                krows = pl.ds(k0 + i * BQ, BQ)
                 irows = slice(i * BQ, (i + 1) * BQ)
-                ds = (pscr[irows, :] * (dpscr[irows, :] - total)).astype(BF)
-                dscr[irows, :] = ds
-                dk[krows, :] = dk[krows, :] + mm(ds, qm, NN)
+                dscr[irows, :] = (pscr[irows, :] * (dpscr[irows, :] - total)).astype(BF)
+            dk[win, :] = dk[win, :] + mm(dscr[...], qm, NN)
             out = []
             for h in range(heads):
                 keys = kt[layer, h * HEAD_DIM : (h + 1) * HEAD_DIM, pl.ds(k0, BK)]
@@ -793,28 +850,27 @@
             out.append(jnp.zeros((HL - heads * HEAD_DIM, BQ), F32))
             dq[pl.ds(q0, BQ), :] = jnp.concatenate(out, axis=0).T
 
-    def pack_qkv(layer):
-        @pl.loop(0, 4)
-        def _(c):
-            rows = pl.ds(pl.multiple_of(c * chunk, chunk), chunk)
-            b0 = c * (chunk // BQ)
-            lane = lane_iota(chunk)
-            gq = rope(dq[rows, :], b0, -1.0) * 0.125
-            gk = rope(dk[rows, :], b0, -1.0)
-            gv = dv[rows, :]
-            sm[layer, 4:5, 0:HL] = sm[layer, 4:5, 0:HL] + jnp.sum(gq, axis=0, keepdims=True)
-            sm[layer, 5:6, 0:HL] = sm[layer, 5:6, 0:HL] + jnp.sum(gv, axis=0, keepdims=True)
-            rk = pltpu.roll(gk, 192, 1)
-            rv = pltpu.roll(gv, 128, 1)
-            dqkv[rows, 0:256] = jnp.where(lane < 192, gq, rk).astype(BF)
-            dqkv[rows, 256:512] = jnp.where(lane < 128, rk, rv).astype(BF)
-            dqkv[rows, 512:768] = jnp.where(lane < 64, rv, 0.0).astype(BF)
+    def pack_qkv(layer, c):
+        rows = pl.ds(pl.multiple_of(c * chunk, chunk), chunk)
+        b0 = c * (chunk // BQ)
+        lane = lane_iota(chunk)
+        gq = rope(dq[rows, :], b0, -1.0) * 0.125
+        gk = rope(dk[rows, :], b0, -1.0)
+        gv = dv[rows, :]
+        sm[layer, 4:5, 0:HL] = sm[layer, 4:5, 0:HL] + jnp.sum(gq, axis=0, keepdims=True)
+        sm[layer, 5:6, 0:HL] = sm[layer, 5:6, 0:HL] + jnp.sum(gv, axis=0, keepdims=True)
+        rk = pltpu.roll(gk, 192, 1)
+        rv = pltpu.roll(gv, 128, 1)
+        dqkv[rows, 0:256] = jnp.where(lane < 192, gq, rk).astype(BF)
+        dqkv[rows, 256:512] = jnp.where(lane < 128, rk, rv).astype(BF)
+        dqkv[rows, 512:768] = jnp.where(lane < 64, rv, 0.0).astype(BF)
 
     def project_back(layer):
         phase = 3 - layer
         parts_sent(1 if layer == 1 else 2)
         for k in (3, 1, 2, 0):
             rows = pl.ds(pl.multiple_of((t ^ k) * chunk, chunk), chunk)
+            pack_qkv(layer, t ^ k)
             da_in = dqkv[rows, :]
             du_in = du[rows, :]
             m = mu[layer, rows, :]
@@ -871,6 +927,7 @@
         place(layer, stage, out_g, 2 + layer)
 
     norm_chunk(0, t)
+    zero_sums()
     gather_pass(*ag_i)
     lc.wait()
     gb[1, own, :] = gst[0].astype(BF)
@@ -896,7 +953,8 @@
     def _(c):
         project_in(0, c)
 
-    attend(0, lambda: first_w_pass(2))
+    first_w_pass(2)
+    attend(0)
     second_w_send()
     first_w(2)
     project_out(0)
@@ -911,6 +969,14 @@
             second_w_pass(2)
             second_w_give(0)
 
+        @pl.when(k == 3)
+        def _():
+            second_w(0)
+
+            @pl.loop(0, 3)
+            def _(m):
+                project_in(1, t ^ m)
+
         arrive(*ag_x, k)
         norm_chunk(1, t ^ k)
 
@@ -923,12 +989,7 @@
 
         hidden(1, t ^ k)
 
-    second_w(0)
-
-    @pl.loop(0, 4)
-    def _(c):
-        project_in(1, c)
-
+    project_in(1, t ^ 3)
     second_w_give(2)
     attend(1)
     second_w(2)
@@ -936,22 +997,20 @@
 
     for k in range(1, 4):
         g_arrival(k).wait_recv()
-    zero_sums()
-
     @pl.loop(0, 4)
     def _(c):
         hidden_back(1, c)
 
     attend_back(1, 0, nblk, lambda: parts_pass(1))
-    pack_qkv(1)
     project_back(1)
     grad_part(1, 2, gw)
     grad_part(1, 1, gw)
+    reduce_cores(1, 2, gw)
     parts_pass(2)
-    reduce_cores(1, 2, gw)
+    reduce_cores(1, 1, gw)
+    grad_part(1, 0, gw)
     finish_y(1)
-    grad_part(1, 0, gw)
-    reduce_cores(1, 1, gw)
+    z_pass(1, 2, gw)
     finish_e(1)
 
     late = w.at[1]
@@ -959,7 +1018,6 @@
     first_w_sent()
     second_w_sent()
     zero_sums()
-    z_pass(1, 2, gw)
     reduce_cores(1, 0, gw)
 
     @pl.loop(0, 8)
@@ -969,21 +1027,21 @@
         @pl.when((step_no == 0) | ((step_no >= 2) & (step_no < 5)))
         def _():
             arrive(*ag_g, k)
+            add_down_grad(k, late)
             hidden_back(0, t ^ k)
 
-        @pl.when(step_no == 5)
-        def _():
-            grad_part(0, 2, late)
+        @pl.when(step_no == 2)
+        def _():
+            z_pass(1, 1, gw)
 
         @pl.when(step_no == 4)
         def _():
-            z_pass(1, 1, gw)
+            z_pass(1, 0, gw)
 
         @pl.when(step_no == 6)
         def _():
             reduce_cores(0, 2, late)
             grad_part(0, 1, late)
-            z_pass(1, 0, gw)
 
         @pl.when(step_no == 7)
         def _():
@@ -999,7 +1057,6 @@
             renorm_all(0)
 
     z_pass(0, 2, late)
-    pack_qkv(0)
     project_back(0)
 
     to_sib = remote(sm.at[1 - s], smr, sms.at[0], smrs.at[0], sib)
@@ -1041,8 +1098,10 @@
         remote(
             tall.at[t ^ k], tall.at[t ^ k], sms.at[n + k - 1], smrs.at[n + k - 1], plane(k)
         ).wait_recv()
-    out_s[...] = tall[...]
+    small_out = pltpu.make_async_copy(tall, out_s, lsem.at[5])
+    small_out.start()
     matrix_end(0)
+    small_out.wait()
 
     for p in range(3):
         pltpu.make_async_copy(wacc.at[p], out_w.at[p], lsem.at[p]).wait()
@@ -1063,19 +1122,29 @@
 
 
 def write_outputs(
-    head_cols, y, g, wg, small, y_out, g_out, up, down, qkv, out, gain, shift, qv, upb, resid, sem
+    head_cols, y, g, wg, small, y_out, g_out, up, down, qkv, out, gain, shift, qv, upb, resid,
+    buf_a, buf_b, buf_c, sem
 ):
-    pairs = ((y, y_out), (g, g_out), (wg.at[1], up), (wg.at[2], down))
-    copies = [pltpu.make_async_copy(src, dst, sem.at[i]) for i, (src, dst) in enumerate(pairs)]
-    for copy in copies:
-        copy.start()
-    first = wg[0]
+    halves = [(y.at[i], y_out.at[i]) for i in range(2)] + [(g.at[i], g_out.at[i]) for i in range(2)]
+    pairs = halves + [(wg.at[1], up), (wg.at[2], down)]
+    held = [buf_a.at[i] for i in range(4)] + [buf_b.at[i] for i in range(2)]
+    loads = [pltpu.make_async_copy(p[0], v, sem.at[0, i]) for i, (p, v) in enumerate(zip(pairs, held))]
+    copies = [pltpu.make_async_copy(v, p[1], sem.at[1, i]) for i, (p, v) in enumerate(zip(pairs, held))]
+    head = pltpu.make_async_copy(wg.at[0], buf_c, sem.at[0, 6])
+    head.start()
+    for load in loads:
+        load.start()
+    head.wait()
+    first = buf_c[...]
     width = first.shape[1]
     for i in range(3):
         turned = pltpu.roll(first, width - i * head_cols, 1) if i else first
         qkv[i] = turned[:, :head_cols]
     last = pltpu.roll(first, width - 3 * head_cols, 1)[:, :256]
     out[...] = last.T[:head_cols, :]
+    for load, copy in zip(loads, copies):
+        load.wait()
+        copy.start()
     total = small[0] + small[1] + small[2] + small[3]
     gain[...] = total[0:2]
     shift[...] = total[2:4]
@@ -1141,6 +1210,16 @@
         return pltpu.VMEM(shape, dtype)
 
     scratch = dict(
+        seg_in=vmem(*segment_ids.shape, dtype=jnp.int32),
+        qkv_in=vmem(*qkv_weight.shape),
+        wo_in=vmem(*out_weight.shape),
+        gain_in=vmem(*norm_gain.shape, dtype=F32),
+        shift_in=vmem(*norm_bias.shape, dtype=F32),
+        qv_in=vmem(*qv_bias.shape, dtype=F32),
+        upb_in=vmem(*up_bias.shape, dtype=F32),
+        resid_in=vmem(*resid_bias.shape, dtype=F32),
+        taba=vmem(*first.shape, dtype=F32),
+        tabb=vmem(*second.shape, dtype=F32),
         w=vmem(2, 3, width, width),
         x=vmem(2, length, width),
         an=vmem(length, width),
@@ -1167,6 +1246,7 @@
         pscr=vmem(BK, blk, dtype=F32),
         dpscr=vmem(BK, blk, dtype=F32),
         dscr=vmem(BK, blk),
+        pbf=vmem(BK, blk),
         sendb=vmem(3, chunk, width),
         recvb=vmem(2, 2, chunk, width),
         relayed=vmem(2, 2, chunk // 2, width),
@@ -1186,6 +1266,7 @@
         smz=vmem(n - 1, 8, width, dtype=F32),
         tall=vmem(4, 8, width, dtype=F32),
         lsem=dma((8,)),
+        isem=dma((10,)),
         psem=dma((2,)),
         xs=dma((6,)),
         xr=dma((6,)),
@@ -1203,8 +1284,8 @@
         rsr=dma((4, 6)),
         osend=dma((4,)),
         orecv=dma((2,)),
-        ghs=dma((3,)),
-        ghr=dma((3,)),
+        ghs=dma((3, 3)),
+        ghr=dma((3, 3)),
         zs=dma((2, 3, n)),
         zr=dma((3, 4)),
         za=dma((2, 3, n)),
@@ -1219,8 +1300,8 @@
             jax.ShapeDtypeStruct((3, rows_z, width), F32),
             jax.ShapeDtypeStruct((4, 8, width), F32),
         ),
-        in_specs=[anywhere, anywhere, vm, vm, vm, anywhere, anywhere] + [vm] * 7,
-        out_specs=(anywhere, anywhere, anywhere, vm),
+        in_specs=[anywhere] * 14,
+        out_specs=(anywhere,) * 4,
         scratch_shapes=list(scratch.values()),
         compiler_params=pltpu.CompilerParams(
             collective_id=0, has_side_effects=True, vmem_limit_bytes=67043328
@@ -1258,9 +1339,14 @@
     y, g, up_g, down_g, qkv_g, out_gr, gain_g, shift_g, qv_g, upb_g, resid_g = pl.pallas_call(
         functools.partial(write_outputs, head_cols),
         out_shape=tuple(jax.ShapeDtypeStruct(shape, F32) for shape in shapes),
-        in_specs=[vm] * 4,
+        in_specs=[anywhere] * 3 + [vm],
         out_specs=(anywhere,) * 4 + (vm,) * 7,
-        scratch_shapes=[dma((4,))],
+        scratch_shapes=[
+            vmem(4, chunk, width, dtype=F32),
+            vmem(2, rows_z, width, dtype=F32),
+            vmem(rows_z, width, dtype=F32),
+            dma((2, 7)),
+        ],
         name="outputs",
     )(out_y, out_g, out_w, out_s)
     return (

time: 181 us -> 178 us (0.983)
  Pallas kernels: 180 us -> 177 us
    pallas_call x1, Pallas kernels: 175 us -> 171 us  [body(): pl.pallas_call(functools.partial(kernel, n, heads), out_shape=(jax.ShapeD...]
where the time goes in v5:
time: 178 us; the launch traced here: 177 us
  Pallas kernels  177 us (99%)
    pallas_call x1, Pallas kernels, body(): pl.pallas_call(functools.partial(kernel, n, heads), out_shape=(jax.ShapeD...  171 us
    pallas_call x1, Pallas kernels, body(): pl.pallas_call(functools.partial(write_outputs, head_cols), out_shape=tup...  5.35 us

profile of v5, /device:TPU:0, one launch (start us, length us, event | category | flops | bytes accessed | tf_op | source)
XLA Modules:
  0.0 177.4 jit_solution(184976375939784175)
XLA Ops:
  0.6 171.2 %two_layers.1 = (f32[2,256,768]{2,1,0:T(8,128)}, f32[2,256,768]{2,1,0:T(8,128)}, f32[3,192,768]{2,1,0:T(8,128)}, f32[4,8,768]{2,1,0:T(8,128)}) custom-call(bf16[2,256,768]{2,1,0:T(8,128)(2,1)} %bitcast.21, f32[2,256,768]{2,1,0:T(8,128)} %bitcast.20, s32[2,1,1024]{2,1,0:T(1,128)} %seg_far.1, bf16[1,3,192,192]{3,2,1,0:T(8,128)(2,1)} %qkv_far.1, ...), custom_call_target="tpu_custom_call" | custom-call | tf_op jit(solution)/shard_map/two_layers/pallas_call | solution.py:1295
  171.9 5.3 %outputs.1 = (f32[2,256,768]{2,1,0:T(8,128)}, f32[2,256,768]{2,1,0:T(8,128)}, f32[192,768]{1,0:T(8,128)}, f32[192,768]{1,0:T(8,128)}, f32[3,192,192]{2,1,0:T(8,1...) custom-call(f32[2,256,768]{2,1,0:T(8,128)} %get-tuple-element.26.y, ...), custom_call_target="tpu_custom_call" | custom-call | tf_op jit(solution)/shard_map/outputs/pallas_call | solution.py:1339

commit v6 on v5

--- a/solution.py
+++ b/solution.py
@@ -960,13 +960,13 @@
     project_out(0)
     parts_pass(0)
     second_w_pass(1)
+    second_w_pass(0)
     finish_y(0)
 
     @pl.loop(0, 4)
     def _(k):
         @pl.when(k == 2)
         def _():
-            second_w_pass(2)
             second_w_give(0)
 
         @pl.when(k == 3)
@@ -984,7 +984,7 @@
         def _():
             second_w_give(1)
             gather_pass(*ag_x)
-            second_w_pass(0)
+            second_w_pass(2)
             second_w(1)
 
         hidden(1, t ^ k)

time: 178 us -> 176 us (0.989)
  Pallas kernels: 177 us -> 175 us
where the time goes in v6:
time: 176 us
  Pallas kernels  175 us (99%)
    pallas_call x1, Pallas kernels, body(): pl.pallas_call(functools.partial(kernel, n, heads), out_shape=(jax.ShapeD...  170 us
    pallas_call x1, Pallas kernels, body(): pl.pallas_call(functools.partial(write_outputs, head_cols), out_shape=tup...  5.35 us

profile of v6, /device:TPU:0, one launch (start us, length us, event | category | flops | bytes accessed | tf_op | source)
XLA Modules:
  0.0 175.8 jit_solution(11006197500959398839)
XLA Ops:
  0.6 169.6 %two_layers.1 = (f32[2,256,768]{2,1,0:T(8,128)}, f32[2,256,768]{2,1,0:T(8,128)}, f32[3,192,768]{2,1,0:T(8,128)}, f32[4,8,768]{2,1,0:T(8,128)}) custom-call(bf16[2,256,768]{2,1,0:T(8,128)(2,1)} %bitcast.21, f32[2,256,768]{2,1,0:T(8,128)} %bitcast.20, s32[2,1,1024]{2,1,0:T(1,128)} %seg_far.1, bf16[1,3,192,192]{3,2,1,0:T(8,128)(2,1)} %qkv_far.1, ...), custom_call_target="tpu_custom_call" | custom-call | tf_op jit(solution)/shard_map/two_layers/pallas_call | solution.py:1295
  170.2 5.3 %outputs.1 = (f32[2,256,768]{2,1,0:T(8,128)}, f32[2,256,768]{2,1,0:T(8,128)}, f32[192,768]{1,0:T(8,128)}, f32[192,768]{1,0:T(8,128)}, f32[3,192,192]{2,1,0:T(8,1...) custom-call(f32[2,256,768]{2,1,0:T(8,128)} %get-tuple-element.26.y, ...), custom_call_target="tpu_custom_call" | custom-call | tf_op jit(solution)/shard_map/outputs/pallas_call | solution.py:1339

commit v7 on v6

--- a/solution.py
+++ b/solution.py
@@ -512,7 +512,7 @@
             [jnp.where(lane == h, block, jnp.zeros_like(block)) for h in range(heads)], axis=0
         )
 
-    sub = 64
+    sub = 128
 
     def norm_chunk(layer, c):
         @pl.loop(0, chunk // sub)

time: 176 us -> 175 us (level)
  no operation moved by 1% of the time
where the time goes in v7:
time: 175 us
  Pallas kernels  174 us (99%)
    pallas_call x1, Pallas kernels, body(): pl.pallas_call(functools.partial(kernel, n, heads), out_shape=(jax.ShapeD...  169 us
    pallas_call x1, Pallas kernels, body(): pl.pallas_call(functools.partial(write_outputs, head_cols), out_shape=tup...  5.35 us

profile of v7, /device:TPU:0, one launch (start us, length us, event | category | flops | bytes accessed | tf_op | source)
XLA Modules:
  0.0 174.8 jit_solution(7170091957791935261)
XLA Ops:
  0.6 168.6 %two_layers.1 = (f32[2,256,768]{2,1,0:T(8,128)}, f32[2,256,768]{2,1,0:T(8,128)}, f32[3,192,768]{2,1,0:T(8,128)}, f32[4,8,768]{2,1,0:T(8,128)}) custom-call(bf16[2,256,768]{2,1,0:T(8,128)(2,1)} %bitcast.21, f32[2,256,768]{2,1,0:T(8,128)} %bitcast.20, s32[2,1,1024]{2,1,0:T(1,128)} %seg_far.1, bf16[1,3,192,192]{3,2,1,0:T(8,128)(2,1)} %qkv_far.1, ...), custom_call_target="tpu_custom_call" | custom-call | tf_op jit(solution)/shard_map/two_layers/pallas_call | solution.py:1295
  169.2 5.3 %outputs.1 = (f32[2,256,768]{2,1,0:T(8,128)}, f32[2,256,768]{2,1,0:T(8,128)}, f32[192,768]{1,0:T(8,128)}, f32[192,768]{1,0:T(8,128)}, f32[3,192,192]{2,1,0:T(8,1...) custom-call(f32[2,256,768]{2,1,0:T(8,128)} %get-tuple-element.26.y, ...), custom_call_target="tpu_custom_call" | custom-call | tf_op jit(solution)/shard_map/outputs/pallas_call | solution.py:1339
